TPU v7x, 512 devices: a whole 4x8x8 slice. The times are simulated.
512 devices in a mesh: row: 32 (over y_lo, x, core), col: 8 (over z), dp: 2 (over y_hi).
Axes of the slice: x: 4, y: 8 (y_hi: 2, y_lo: 4; y = y_hi * 4 + y_lo), z: 8, core: 2. Of those that a mesh axis runs over, the one named last changes fastest.
Arguments:
- pixels: bfloat16 [2, 3, 1024, 1024], P('dp', None, 'row', 'col'), may hold values from -6 to 6
- cotangent: bfloat16 [2, 256, 256, 1024], P('dp', 'row', 'col'), may hold values from -6 to 6
- embed_weight: bfloat16 [48, 1024], replicated, may hold values from -0.875 to 0.875
- embed_bias: float32 [1024], replicated, may hold values from -4 to 4
- layer_norm_gain: float32 [1024], replicated, may hold values from 0.5 to 1.5
- qkv_weight: bfloat16 [1024, 2304], P('row', ('col', 'dp')), may hold values from -0.1875 to 0.1875
- out_weight: bfloat16 [768, 1024], P('row', ('col', 'dp')), may hold values from -0.21875 to 0.21875
- bias_table: float32 [12, 225], replicated, may hold values from -4 to 404
- rel_index: int32 [64, 64], replicated, may hold values from 0 to 224
- shifts: int32 [2, 2], P('dp'), may hold values from 1 to 7
Outputs:
- out_weight_grad: float32 [768, 1024], P('row', ('col', 'dp'))
- embed_weight_grad: float32 [48, 1024], replicated
- embed_bias_grad: float32 [1024], replicated
- norm_gain_grad: float32 [1024], replicated
- bias_table_grad: float32 [12, 225], replicated
Inputs may be any that keep to these rules, and one draw needn't show every extreme that they name: `rel_index`: each entry names one of the 225 columns of bias_table.
All inputs are finite; a program needn't handle non-finite values.
Results may differ from a plain program's by a relative error of at most 0.023.
Values may be sent and summed in bfloat16 or wider, within the bound.
No kernel may reach another device: no remote copies, remote signals or barrier semaphores. Data moves between devices by JAX's collectives and lax.ppermute only.
A program may use at most 64 MiB of HBM per device.

v0:
```python
import jax
import jax.numpy as jnp
from jax import lax
from jax.sharding import PartitionSpec as P

WIN = 8
PATCH = 4


norm_epsilon = 1e-05


def laid_out(blocks, dim):
    blocks = jnp.moveaxis(blocks, 0, dim)
    lengths = blocks.shape
    return blocks.reshape(*lengths[:dim], lengths[dim] * lengths[dim + 1], *lengths[dim + 2 :])


def gather_together(arrays, axis, dims):
    line = jnp.concatenate([a.reshape(-1) for a in arrays])
    lines, at, gathered = (lax.all_gather(line, axis), 0, [])
    for a, dim in zip(arrays, dims):
        blocks = lines[:, at : at + a.size].reshape(-1, *a.shape)
        gathered.append(laid_out(blocks, dim))
        at += a.size
    return tuple(gathered)


def from_behind(value, axis, steps):
    count = lax.axis_size(axis)
    pairs = [(source, (source + steps) % count) for source in range(count)]
    return lax.ppermute(value, axis, pairs)


def in_blocks(x, dim, length):
    before, after = (x.shape[:dim], x.shape[dim + 1 :])
    return jnp.moveaxis(x.reshape(*before, length, -1, *after), dim, 0)


def summed_on_arrival(x, axis, dim):
    blocks = in_blocks(x, dim, lax.axis_size(axis))
    arrived = lax.all_to_all(blocks, axis, split_axis=0, concat_axis=0, tiled=True)
    return arrived.astype(jnp.float32).sum(axis=0)


def summed_on_arrival_2(x, axis, dim):
    blocks = in_blocks(x, dim, lax.axis_size(axis))
    arrived = lax.all_to_all(blocks, axis, split_axis=0, concat_axis=0, tiled=True)
    return arrived.sum(axis=0)


def make_patches(pixel_block):
    images, channels, pixel_rows, pixel_cols = pixel_block.shape
    grid_rows = pixel_rows // PATCH
    grid_cols = pixel_cols // PATCH
    shaped = pixel_block.reshape(images, channels, grid_rows, PATCH, grid_cols, PATCH)
    return shaped.transpose(0, 2, 4, 1, 3, 5).reshape(
        images, grid_rows, grid_cols, channels * PATCH * PATCH
    )


def embed_cells(patches, embed_weight, embed_bias):
    return (jnp.dot(patches, embed_weight, preferred_element_type=jnp.float32) + embed_bias).astype(
        jnp.bfloat16
    )


def window_split(block):
    rows_all, cols_all, features = block.shape
    shaped = block.reshape(rows_all // WIN, WIN, cols_all // WIN, WIN, features)
    return shaped.transpose(0, 2, 1, 3, 4).reshape(-1, WIN * WIN, features)


def window_join(windows, rows_all, cols_all):
    features = windows.shape[-1]
    shaped = windows.reshape(rows_all // WIN, cols_all // WIN, WIN, WIN, features)
    return shaped.transpose(0, 2, 1, 3, 4).reshape(rows_all, cols_all, features)


def splice_after(own_block, borrowed, offsets, along_dim):
    length = own_block.shape[along_dim]

    def single(own_item, borrowed_item, offset):
        joined = jnp.concatenate([own_item, borrowed_item], along_dim - 1)
        return lax.dynamic_slice_in_dim(joined, offset, length, along_dim - 1)

    return jax.vmap(single)(own_block, borrowed, offsets)


def attend_forward(cell_windows, labels, layer_norm_gain, qkv_full, bias_full):
    window_count, cell_count, features = cell_windows.shape
    head_count = bias_full.shape[0]
    inner_width = qkv_full.shape[1] // 3
    head_size = inner_width // head_count
    score_scale = head_size ** (-0.5)
    flat_rows = cell_windows.reshape(-1, features).astype(jnp.float32)
    average = jnp.mean(flat_rows, axis=-1, keepdims=True)
    centered_input = flat_rows - average
    inverse_deviation = lax.rsqrt(
        jnp.mean(centered_input * centered_input, axis=-1, keepdims=True) + norm_epsilon
    )
    standardized_rows = centered_input * inverse_deviation
    normalized_rows = (standardized_rows * layer_norm_gain).astype(jnp.bfloat16)
    projected = jnp.dot(normalized_rows, qkv_full, preferred_element_type=jnp.float32).astype(
        jnp.bfloat16
    )
    head_shape = (window_count, cell_count, head_count, head_size)
    query_rows = projected[:, :inner_width].reshape(head_shape)
    key_vectors = projected[:, inner_width : 2 * inner_width].reshape(head_shape)
    value_rows = projected[:, 2 * inner_width :].reshape(head_shape)
    scores = (
        jnp.einsum("wmhd,wnhd->whmn", query_rows, key_vectors, preferred_element_type=jnp.float32)
        * score_scale
        + bias_full[None]
    )
    same_region = labels[:, None, :, None] == labels[:, None, None, :]
    scores = jnp.where(same_region, scores, -1e30)
    row_peak = jnp.max(scores, axis=-1, keepdims=True)
    exp_scores = jnp.exp(scores - row_peak)
    attention_weights = exp_scores / jnp.sum(exp_scores, axis=-1, keepdims=True)
    reduced_probability = attention_weights.astype(jnp.bfloat16)
    attended = jnp.einsum(
        "whmn,wnhd->wmhd", reduced_probability, value_rows, preferred_element_type=jnp.float32
    ).astype(jnp.bfloat16)
    stored_residuals = (
        standardized_rows,
        inverse_deviation,
        query_rows,
        key_vectors,
        value_rows,
        attention_weights,
        reduced_probability,
    )
    return (stored_residuals, attended.reshape(-1, inner_width))


def attend_backward(stored_residuals, d_attended, layer_norm_gain, qkv_full):
    (
        standardized_rows,
        inverse_deviation,
        query_rows,
        key_vectors,
        value_rows,
        attention_weights,
        reduced_probability,
    ) = stored_residuals
    head_shape = query_rows.shape
    score_scale = head_shape[3] ** (-0.5)
    total_row_count = standardized_rows.shape[0]
    inner_width = head_shape[2] * head_shape[3]
    d_heads = d_attended.reshape(head_shape)
    d_prob = jnp.einsum("wmhd,wnhd->whmn", d_heads, value_rows, preferred_element_type=jnp.float32)
    d_values = jnp.einsum(
        "whmn,wmhd->wnhd", reduced_probability, d_heads, preferred_element_type=jnp.float32
    ).astype(jnp.bfloat16)
    d_scores = attention_weights * (
        d_prob - jnp.sum(attention_weights * d_prob, axis=-1, keepdims=True)
    )
    table_part = jnp.sum(d_scores, axis=0)
    d_low = d_scores.astype(jnp.bfloat16)
    d_queries = (
        jnp.einsum("whmn,wnhd->wmhd", d_low, key_vectors, preferred_element_type=jnp.float32)
        * score_scale
    ).astype(jnp.bfloat16)
    d_keys = (
        jnp.einsum("whmn,wmhd->wnhd", d_low, query_rows, preferred_element_type=jnp.float32)
        * score_scale
    ).astype(jnp.bfloat16)
    d_projected = jnp.concatenate(
        [
            d_queries.reshape(total_row_count, inner_width),
            d_keys.reshape(total_row_count, inner_width),
            d_values.reshape(total_row_count, inner_width),
        ],
        axis=1,
    )
    normalized_gradient = lax.dot_general(
        d_projected, qkv_full, (((1,), (1,)), ((), ())), preferred_element_type=jnp.float32
    )
    gain_contribution = jnp.sum(normalized_gradient * standardized_rows, axis=0)
    scaled_rows = normalized_gradient * layer_norm_gain
    branch_gradient = inverse_deviation * (
        scaled_rows
        - jnp.mean(scaled_rows, axis=-1, keepdims=True)
        - standardized_rows * jnp.mean(scaled_rows * standardized_rows, axis=-1, keepdims=True)
    )
    return (branch_gradient.astype(jnp.bfloat16), gain_contribution, table_part)


def on_device(
    pixels,
    cotangent,
    embed_weight,
    embed_bias,
    layer_norm_gain,
    qkv_weight,
    out_weight,
    bias_table,
    rel_index,
    shifts,
):
    images, rows_dev, cols_dev, features = cotangent.shape
    head_count = bias_table.shape[0]
    grid_rows = rows_dev * lax.axis_size("row")
    grid_cols = cols_dev * lax.axis_size("col")
    row_shift = shifts[:, 0]
    col_shift = shifts[:, 1]
    qkv_columns, out_columns = gather_together((qkv_weight, out_weight), ("col", "dp"), (1, 1))
    qkv_full = lax.all_gather(qkv_columns, "row", axis=0, tiled=True)
    patches = make_patches(pixels)
    below = from_behind((pixels, cotangent), "row", -1)
    moved_pixels = splice_after(pixels, below[0], row_shift * PATCH, 2)
    shifted_cot = splice_after(cotangent, below[1], row_shift, 1)
    beside = from_behind((moved_pixels[:, :, :, : WIN * PATCH], shifted_cot[:, :, :WIN]), "col", -1)
    moved_pixels = splice_after(moved_pixels, beside[0], col_shift * PATCH, 3)
    shifted_cot = splice_after(shifted_cot, beside[1], col_shift, 2)
    moved_patches = make_patches(moved_pixels)
    shifted = embed_cells(moved_patches, embed_weight, embed_bias)
    row_ids = lax.axis_index("row") * rows_dev + jnp.arange(rows_dev, dtype=jnp.int32)
    col_ids = lax.axis_index("col") * cols_dev + jnp.arange(cols_dev, dtype=jnp.int32)
    row_part = (row_ids[None, :] >= grid_rows - row_shift[:, None]).astype(jnp.int32)
    col_part = (col_ids[None, :] >= grid_cols - col_shift[:, None]).astype(jnp.int32)
    region = 2 * row_part[:, :, None] + col_part[:, None, :]
    labels = window_split(region.reshape(images * rows_dev, cols_dev, 1))[:, :, 0]
    cell_windows = window_split(shifted.reshape(images * rows_dev, cols_dev, features))
    cot_flat = window_split(shifted_cot.reshape(images * rows_dev, cols_dev, features)).reshape(
        -1, features
    )
    selector = (
        rel_index.reshape(-1)[:, None] == jnp.arange(bias_table.shape[1], dtype=jnp.int32)[None, :]
    ).astype(jnp.float32)
    bias_full = jnp.dot(selector, bias_table.T, precision=lax.Precision.HIGHEST).T.reshape(
        head_count, WIN * WIN, WIN * WIN
    )
    stored_residuals, attended = attend_forward(
        cell_windows, labels, layer_norm_gain, qkv_full, bias_full
    )
    d_attended = lax.dot_general(
        cot_flat,
        lax.all_gather(out_columns, "row", axis=0, tiled=True),
        (((1,), (1,)), ((), ())),
        preferred_element_type=jnp.float32,
    ).astype(jnp.bfloat16)
    partial_rows = summed_on_arrival(
        lax.dot_general(
            attended, cot_flat, (((0,), (0,)), ((), ())), preferred_element_type=jnp.float32
        ).astype(jnp.bfloat16),
        "row",
        0,
    )
    out_weight_grad = summed_on_arrival_2(partial_rows, ("col", "dp"), 1)
    d_rows, gain_contribution, table_part = attend_backward(
        stored_residuals, d_attended, layer_norm_gain, qkv_full
    )
    branch_gradient = window_join(
        d_rows.reshape(-1, WIN * WIN, features), images * rows_dev, cols_dev
    ).reshape(images, rows_dev, cols_dev, features)
    patch_rows = patches.reshape(-1, patches.shape[-1])
    cot_rows = cotangent.reshape(-1, features)
    contract = (((0,), (0,)), ((), ()))
    branch_patches = moved_patches.reshape(-1, patches.shape[-1])
    back_rows = branch_gradient.reshape(-1, features)
    embed_grad = lax.dot_general(
        patch_rows, cot_rows, contract, preferred_element_type=jnp.float32
    ) + lax.dot_general(branch_patches, back_rows, contract, preferred_element_type=jnp.float32)
    bias_grad = jnp.sum(cot_rows, axis=0, dtype=jnp.float32) + jnp.sum(
        back_rows, axis=0, dtype=jnp.float32
    )
    table_grad = jnp.dot(
        table_part.reshape(head_count, -1), selector, precision=lax.Precision.HIGHEST
    )
    totals = lax.psum((embed_grad, bias_grad, gain_contribution, table_grad), ("row", "col", "dp"))
    return (out_weight_grad, totals[0], totals[1], totals[2], totals[3])


def solution(mesh):
    return jax.shard_map(
        on_device,
        mesh=mesh,
        in_specs=(
            P("dp", None, "row", "col"),
            P("dp", "row", "col", None),
            P(),
            P(),
            P(),
            P("row", ("col", "dp")),
            P("row", ("col", "dp")),
            P(),
            P(),
            P("dp", None),
        ),
        out_specs=(P("row", ("col", "dp")), P(), P(), P(), P()),
        check_vma=False,
    )
```

profile of v0, /device:TPU:1, one launch (start us, length us, event | category | flops | bytes accessed | tf_op | source)
XLA Modules:
  0.0 531.3 jit_solution(17640539228730412857)
XLA Ops:
  8.9 54.6 %all-gather = bf16[98304]{0:T(1024)(128)(2,1)S(1)} all-gather(bf16[6144]{0:T(1024)(128)(2,1)S(1)} %pad_maximum_fusion), channel_id=2, replica_groups=mesh['row'=32,'col'=8,'dp'=2] {'col','dp'}, dimensions={0}, use_global_device_ids=true | all-gather | bytes 208896 | tf_op jit(solution)/shard_map/all_gather | solution.py:21
  64.2 1.0 reshape.201
  65.3 10.1 %collective-permute-start = (bf16[1,3,32,128]{3,2,1,0:T(8,128)(2,1)S(1)}, bf16[1,3,32,128]{3,2,1,0:T(8,128)(2,1)S(1)}, u32[]{:S(2)}, u32[]{:S(2)}) collective-permute-start(bf16[1,3,32,128]{3,2,1,0:T(8,128)(2,1)S(1)} %copy-done.12), channel_id=1, source_target_pairs={{0,496},{16,0},{32,16},{48,32},{64,48},{80,64},{96,80},{112,96},{1... | collective-permute-start | bytes 73736 | tf_op jit(solution)/shard_map/ppermute | solution.py:32
  75.4 1.9 collective-permute-start.2
  78.3 1.7 reshape.208
  82.9 2.6 convolution_bitcast_fusion
  85.5 0.9 fusion.43
  87.2 1.9 collective-permute-start.1
  94.3 1.7 reshape.196
  97.7 1.2 fusion.28
  98.9 2.1 collective-permute-start.3
  101.0 1.0 multiply_convert_fusion.3
  102.7 2.2 collective-permute-done.3
  106.1 26.1 %all-gather.4.cloned.1.call-done = bf16[1024,2304]{1,0:T(8,128)(2,1)} async-done(((bf16[32,2304]{1,0:T(8,128)(2,1)}), bf16[1024,2304]{1,0:T(8,128)(2,1)}) %all-gather.4.cloned.1.call-update) | async-done | bytes 4718608 | tf_op jit(solution)/shard_map/all_gather | solution.py:209
  132.1 3.9 convolution_convert_fusion
  136.0 1.0 fusion.39
  138.5 2.6 reshape.338
  141.1 1.6 reshape.339
  142.7 1.8 copy.192
  144.9 1.6 fusion.42
  146.5 3.8 fusion.7
  150.3 1.8 copy.179
  152.1 1.2 reshape.205
  153.3 2.9 convolution_convert_fusion.1
  156.2 5.3 all-to-all-start
  161.4 40.1 %all-gather.6.cloned.1.call-done = bf16[768,1024]{1,0:T(8,128)(2,1)} async-done(((bf16[24,1024]{1,0:T(8,128)(2,1)}), bf16[768,1024]{1,0:T(8,128)(2,1)}) %all-gather.6.cloned.1.call-update) | async-done | bytes 1572880 | tf_op jit(solution)/shard_map/all_gather | solution.py:240
  201.5 2.8 convolution_convert_fusion.4
  204.3 2.4 reshape.341
  206.7 1.8 copy.196
  208.5 2.5 multiply_reduce_fusion
  211.1 1.3 fusion.21
  212.4 1.9 copy.200
  214.3 1.8 reshape.216
  216.1 1.5 fusion.9
  217.6 1.5 copy.191
  219.1 1.2 reshape.213
  220.4 1.5 fusion.10
  221.8 1.6 copy.195
  223.4 1.2 reshape.214
  224.7 2.5 fusion.8
  228.3 4.0 multiply_reduce_fusion.1
  233.3 0.9 convolution_add_fusion.1
  234.2 1.7 convert_reduce_fusion
  236.9 10.7 %all-to-all-start.1 = ((f32[16,1,1536]{2,1,0:T(1,128)}), f32[16,1,1536]{2,1,0:T(1,128)S(1)}, u32[]{:S(2)}, u32[]{:S(2)}) async-start(f32[16,1,1536]{2,1,0:T(1,128)} %reshape.342), calls=%async_computation.1 | async-start | bytes 196608 | tf_op jit(solution)/shard_map/all_to_all | solution.py:48
  247.7 1.4 fusion.1
  249.3 100.0 %all-reduce.2 = (f32[1024]{0:T(1024)}, f32[1024]{0:T(1024)}, f32[12,225]{1,0:T(8,128)}) all-reduce(f32[1024]{0:T(1024)S(1)} %add.126, f32[1024]{0:T(1024)S(1)} %get-tuple-element.49, f32[12,225]{1,0:T(8,128)S(1)} %fusion.1), channel_id=1, replica_groups=mesh['row'=32,'col'=8,'dp'=2] {'row','col','dp'}, use_global_device_ids=true, to_apply=%region_12.13 | all-reduce | flops 4748 | bytes 37984 | tf_op jit(solution)/shard_map/psum | solution.py:272
  351.4 171.8 %all-reduce.5.cloned.1.call-done = f32[48,1024]{1,0:T(8,128)} async-done(((f32[48,1024]{1,0:T(8,128)}), f32[48,1024]{1,0:T(8,128)}) %all-reduce.5.cloned.1.call-update) | async-done | bytes 196624 | tf_op jit(solution)/shard_map/psum | solution.py:272
  523.2 1.6 copy.233
  (108 shorter events, 16.4 us)
Async XLA Ops:
  7.2 89.5 %copy-start = (bf16[48,1024]{1,0:T(8,128)(2,1)S(1)}, bf16[48,1024]{1,0:T(8,128)(2,1)}, u32[]{:S(2)}) copy-start(bf16[48,1024]{1,0:T(8,128)(2,1)} %param.12) | copy-start | bytes 294916
  7.2 58.1 %copy-start.12 = (bf16[1,3,32,128]{3,2,1,0:T(8,128)(2,1)S(1)}, bf16[1,3,32,128]{3,2,1,0:T(8,128)(2,1)}, u32[]{:S(2)}) copy-start(bf16[1,3,32,128]{3,2,1,0:T(8,128)(2,1)} %param.10) | copy-start | bytes 73732
  7.2 68.2 %copy-start.3 = (bf16[1,8,32,1024]{3,2,1,0:T(8,128)(2,1)S(1)}, bf16[1,8,32,1024]{3,2,1,0:T(8,128)(2,1)}, u32[]{:S(2)}) copy-start(bf16[1,8,32,1024]{3,2,1,0:T(8,128)(2,1)} %param.11) | copy-start | bytes 1572868
  7.2 124.9 %all-gather.4.cloned.1.call-start = ((), (), s32[]{:S(2)}) async-start(), calls=%async_computation.2 | async-start | bytes 4866048 | tf_op jit(solution)/shard_map/all_gather | solution.py:209
  63.6 16.3 %copy-start.19 = (s32[1,2]{1,0:T(1,128)S(1)}, s32[1,2]{1,0:T(1,128)}, u32[]{:S(2)}) copy-start(s32[1,2]{1,0:T(1,128)} %param.19) | copy-start | bytes 28
  63.6 18.4 %copy-start.14 = (s32[64,64]{1,0:T(8,128)S(1)}, s32[64,64]{1,0:T(8,128)}, u32[]{:S(2)}) copy-start(s32[64,64]{1,0:T(8,128)} %param.18) | copy-start | bytes 49156
  64.2 18.7 %copy-start.20 = (f32[12,225]{1,0:T(8,128)S(1)}, f32[12,225]{1,0:T(8,128)}, u32[]{:S(2)}) copy-start(f32[12,225]{1,0:T(8,128)} %param.17) | copy-start | bytes 32404
  65.2 136.3 %all-gather.6.cloned.1.call-start = ((), (), s32[]{:S(2)}) async-start(), calls=%async_computation.3 | async-start | bytes 1622016 | tf_op jit(solution)/shard_map/all_gather | solution.py:240
  65.3 21.8 %collective-permute-start = (bf16[1,3,32,128]{3,2,1,0:T(8,128)(2,1)S(1)}, bf16[1,3,32,128]{3,2,1,0:T(8,128)(2,1)S(1)}, u32[]{:S(2)}, u32[]{:S(2)}) collective-permute-start(bf16[1,3,32,128]{3,2,1,0:T(8,128)(2,1)S(1)} %copy-done.12), channel_id=1, source_target_pairs={{0,496},{16,0},{32,16},{48,32},{64,48},{80,64},{96,80},{112,96},{1... | collective-permute-start | bytes 73736 | tf_op jit(solution)/shard_map/ppermute | solution.py:32
  75.4 22.3 %collective-permute-start.2 = (bf16[1,8,32,1024]{3,2,1,0:T(8,128)(2,1)S(1)}, bf16[1,8,32,1024]{3,2,1,0:T(8,128)(2,1)}, u32[]{:S(2)}, u32[]{:S(2)}) collective-permute-start(bf16[1,8,32,1024]{3,2,1,0:T(8,128)(2,1)S(1)} %copy-done.3), channel_id=1, source_target_pairs={{0,496},{16,0},{32,16},{48,32},{64,48},{80,64},{96,80},{112,96},{1... | collective-permute-start | bytes 1572872 | tf_op jit(solution)/shard_map/ppermute | solution.py:32
  82.1 5.1 copy-start.16
  87.2 6.9 %collective-permute-start.1 = (bf16[1,3,32,32]{3,2,1,0:T(8,128)(2,1)S(1)}, bf16[1,3,32,32]{3,2,1,0:T(8,128)(2,1)S(1)}, u32[]{:S(2)}, u32[]{:S(2)}) collective-permute-start(bf16[1,3,32,32]{3,2,1,0:T(8,128)(2,1)S(1)} %bitcast.126), channel_id=1, source_target_pairs={{0,14},{2,0},{4,2},{6,4},{8,6},{10,8},{12,10},{14,12},{1,15},{3,1}... | collective-permute-start | bytes 18440 | tf_op jit(solution)/shard_map/ppermute | solution.py:32
  92.5 4.1 copy-start.18
  97.3 3.7 copy-start.15
  98.9 6.1 %collective-permute-start.3 = (bf16[1,8,8,1024]{3,2,1,0:T(8,128)(2,1)S(1)}, bf16[1,8,8,1024]{3,2,1,0:T(8,128)(2,1)S(1)}, u32[]{:S(2)}, u32[]{:S(2)}) collective-permute-start(bf16[1,8,8,1024]{3,2,1,0:T(8,128)(2,1)S(1)} %slice.121), channel_id=1, source_target_pairs={{0,14},{2,0},{4,2},{6,4},{8,6},{10,8},{12,10},{14,12},{1,15},{3,1}... | collective-permute-start | bytes 393224 | tf_op jit(solution)/shard_map/ppermute | solution.py:32
  138.5 2.6 copy-start.5
  144.9 1.6 copy-start.1
  156.2 45.3 %copy-start.4 = (bf16[1,4,8,8,1024]{4,3,2,1,0:T(8,128)(2,1)S(1)}, bf16[1,4,8,8,1024]{4,3,2,1,0:T(8,128)(2,1)}, u32[]{:S(2)}) copy-start(bf16[1,4,8,8,1024]{4,3,2,1,0:T(8,128)(2,1)} %copy.180) | copy-start | bytes 1572868
  156.2 78.1 %all-to-all-start = ((bf16[32,24,1024]{2,1,0:T(8,128)(2,1)}), bf16[32,24,1024]{2,1,0:T(8,128)(2,1)}, u32[]{:S(2)}, u32[]{:S(2)}) async-start(bf16[32,24,1024]{2,1,0:T(8,128)(2,1)} %bitcast.113), calls=%async_computation | async-start | bytes 3145728 | tf_op jit(solution)/shard_map/all_to_all | solution.py:42
  208.5 2.6 copy-start.6
  208.5 2.6 copy-start.2
  221.8 2.8 copy-start.7
  227.2 1.1 copy-start.9
  227.2 1.1 copy-start.10
  232.4 0.9 copy-start.8
  232.4 0.9 copy-start.13
  234.2 13.5 %copy-start.11 = (f32[12,4096]{1,0:T(8,128)S(1)}, f32[12,4096]{1,0:T(8,128)}, u32[]{:S(2)}) copy-start(f32[12,4096]{1,0:T(8,128)} %reshape.216) | copy-start | bytes 589828
  234.2 13.5 %copy-start.17 = (s32[4096]{0:T(1024)S(1)}, s32[4096]{0:T(1024)}, u32[]{:S(2)}) copy-start(s32[4096]{0:T(1024)} %copy-done.16) | copy-start | bytes 49156
  236.9 112.4 %all-to-all-start.1 = ((f32[16,1,1536]{2,1,0:T(1,128)}), f32[16,1,1536]{2,1,0:T(1,128)S(1)}, u32[]{:S(2)}, u32[]{:S(2)}) async-start(f32[16,1,1536]{2,1,0:T(1,128)} %reshape.342), calls=%async_computation.1 | async-start | bytes 196608 | tf_op jit(solution)/shard_map/all_to_all | solution.py:48
  247.6 275.5 %all-reduce.5.cloned.1.call-start = ((), (), s32[]{:S(2)}) async-start(), calls=%async_computation.4 | async-start | bytes 393216 | tf_op jit(solution)/shard_map/psum | solution.py:272
Sparse Core Ops, SparseCore 0:
  65.4 66.7 all-gather.3
  134.3 67.1 all-gather.5
  254.0 269.1 all-reduce.4
where the time goes:
time: 532 us; the launch traced here: 531 us
  waiting for transfers between devices  240 us (45%)
  blocking collectives  155 us (29%)
  local copies, waits for them, and re-layouts  41.8 us (8%)
  starting transfers between devices  32.1 us (6%)
  matrix products  32 us (6%)
  between operations  20.9 us (4%)
  other arithmetic  9.81 us (2%)
    psum x1, waiting for transfers between devices, on_device(): lax.psum((embed_grad, bias_grad, gain_contribution, table_grad), ('row',...  172 us
    psum x1, blocking collectives, on_device(): lax.psum((embed_grad, bias_grad, gain_contribution, table_grad), ('row',...  100 us
    all_gather x1, blocking collectives, gather_together(): lines, at, gathered = (lax.all_gather(line, axis), 0, [])  54.6 us
    all_gather x1, waiting for transfers between devices, on_device(): lax.all_gather(out_columns, 'row', axis=0, tiled=True)  40.1 us
    all_gather x1, waiting for transfers between devices, on_device(): qkv_full = lax.all_gather(qkv_columns, 'row', axis=0, tiled=True)  26.1 us
    ppermute x4, starting transfers between devices, from_behind(): return lax.ppermute(value, axis, pairs)  16 us
    all_to_all x1, starting transfers between devices, summed_on_arrival_2(): lax.all_to_all(blocks, axis, split_axis=0, concat_axis=0, tiled=True)  10.7 us
  transfers between devices with their start and end apart: 9, of which 4 were waited for; matrix products, arithmetic and copies ran while one was open for 14% of the time, Pallas kernels for 0%

commit v1 on v0

--- a/solution.py
+++ b/solution.py
@@ -16,9 +16,18 @@
     return blocks.reshape(*lengths[:dim], lengths[dim] * lengths[dim + 1], *lengths[dim + 2 :])
 
 
+def exchange(blocks, axis):
+    return lax.all_to_all(blocks, axis, split_axis=0, concat_axis=0, tiled=True)
+
+
+def spread(line, axis):
+    copies = jnp.broadcast_to(line[None], (lax.axis_size(axis), *line.shape))
+    return exchange(copies, axis)
+
+
 def gather_together(arrays, axis, dims):
     line = jnp.concatenate([a.reshape(-1) for a in arrays])
-    lines, at, gathered = (lax.all_gather(line, axis), 0, [])
+    lines, at, gathered = (spread(line, axis), 0, [])
     for a, dim in zip(arrays, dims):
         blocks = lines[:, at : at + a.size].reshape(-1, *a.shape)
         gathered.append(laid_out(blocks, dim))
@@ -41,12 +50,6 @@
     blocks = in_blocks(x, dim, lax.axis_size(axis))
     arrived = lax.all_to_all(blocks, axis, split_axis=0, concat_axis=0, tiled=True)
     return arrived.astype(jnp.float32).sum(axis=0)
-
-
-def summed_on_arrival_2(x, axis, dim):
-    blocks = in_blocks(x, dim, lax.axis_size(axis))
-    arrived = lax.all_to_all(blocks, axis, split_axis=0, concat_axis=0, tiled=True)
-    return arrived.sum(axis=0)
 
 
 def make_patches(pixel_block):
@@ -206,7 +209,13 @@
     row_shift = shifts[:, 0]
     col_shift = shifts[:, 1]
     qkv_columns, out_columns = gather_together((qkv_weight, out_weight), ("col", "dp"), (1, 1))
-    qkv_full = lax.all_gather(qkv_columns, "row", axis=0, tiled=True)
+    rows_qkv, width_qkv = qkv_columns.shape
+    out_tall = out_columns.reshape(rows_qkv, -1)
+    weights = lax.all_gather(
+        jnp.concatenate([qkv_columns, out_tall], axis=1), "row", axis=0, tiled=True
+    )
+    qkv_full = weights[:, :width_qkv]
+    out_full = weights[:, width_qkv:].reshape(-1, features)
     patches = make_patches(pixels)
     below = from_behind((pixels, cotangent), "row", -1)
     moved_pixels = splice_after(pixels, below[0], row_shift * PATCH, 2)
@@ -237,7 +246,7 @@
     )
     d_attended = lax.dot_general(
         cot_flat,
-        lax.all_gather(out_columns, "row", axis=0, tiled=True),
+        out_full,
         (((1,), (1,)), ((), ())),
         preferred_element_type=jnp.float32,
     ).astype(jnp.bfloat16)
@@ -248,7 +257,6 @@
         "row",
         0,
     )
-    out_weight_grad = summed_on_arrival_2(partial_rows, ("col", "dp"), 1)
     d_rows, gain_contribution, table_part = attend_backward(
         stored_residuals, d_attended, layer_norm_gain, qkv_full
     )
@@ -269,8 +277,25 @@
     table_grad = jnp.dot(
         table_part.reshape(head_count, -1), selector, precision=lax.Precision.HIGHEST
     )
-    totals = lax.psum((embed_grad, bias_grad, gain_contribution, table_grad), ("row", "col", "dp"))
-    return (out_weight_grad, totals[0], totals[1], totals[2], totals[3])
+    head_table = table_grad.reshape(-1)
+    pieces = [embed_grad.reshape(-1), bias_grad, gain_contribution, head_table]
+    line = jnp.concatenate(pieces)
+    row_count = lax.axis_size("row")
+    piece = -(-line.size // (row_count * 1024)) * 1024
+    line = jnp.pad(line, (0, row_count * piece - line.size)).reshape(row_count, piece // 128, 128)
+    mine = exchange(line, "row").sum(axis=0).reshape(-1)
+    col_blocks = in_blocks(partial_rows, 1, lax.axis_size(("col", "dp")))
+    block_shape = col_blocks.shape
+    col_blocks = col_blocks.reshape(block_shape[0], -1)
+    own = jnp.broadcast_to(mine[None], (block_shape[0], piece))
+    both = exchange(jnp.concatenate([own, col_blocks], axis=1), ("col", "dp")).sum(axis=0)
+    out_weight_grad = both[piece:].reshape(block_shape[1:])
+    total = spread(both[:piece].reshape(piece // 128, 128), "row").reshape(-1)
+    results, at = ([], 0)
+    for a, shape in zip(pieces, (embed_grad.shape, (features,), (features,), table_grad.shape)):
+        results.append(total[at : at + a.size].reshape(shape))
+        at += a.size
+    return (out_weight_grad, *results)
 
 
 def solution(mesh):

time: 532 us -> 270 us (0.51)
  waiting for transfers between devices: 240 us -> 86.7 us
  blocking collectives: 155 us -> 50.4 us
    psum x1 -> x0, waiting for transfers between devices: 172 us -> none  [on_device(): lax.psum((embed_grad, bias_grad, gain_contribution, table_grad), ('row',...]
    psum x1 -> x0, blocking collectives: 100 us -> none  [on_device(): lax.psum((embed_grad, bias_grad, gain_contribution, table_grad), ('row',...]
    all_gather x1 -> x0, blocking collectives: 54.6 us -> none  [gather_together(): lines, at, gathered = (lax.all_gather(line, axis), 0, [])]
    all_to_all x0 -> x2, blocking collectives: none -> 50.4 us  [exchange(): return lax.all_to_all(blocks, axis, split_axis=0, concat_axis=0, tiled=True)]
    all_to_all x1, waiting for transfers between devices: 0.01 us -> 36.9 us  [summed_on_arrival(): lax.all_to_all(blocks, axis, split_axis=0, concat_axis=0, tiled=True)]
    all_gather x2 -> x1, waiting for transfers between devices: 66.1 us -> 31 us  [on_device(): lax.all_gather(jnp.concatenate([qkv_columns, out_tall], axis=1), 'row', a...]
    all_to_all x1 -> x2, waiting for transfers between devices: 0.01 us -> 16.1 us  [exchange(): return lax.all_to_all(blocks, axis, split_axis=0, concat_axis=0, tiled=True)]
    reshape x0 -> x6, local copies, waits for them, and re-layouts: none -> 6.17 us  [the longest x1 3.89 us: on_device(): out_full = weights[:, width_qkv:].reshape(-1, features)]
  transfers between devices with their start and end apart: 9 -> 8, of which waited for: 4 -> 5; matrix products, arithmetic and copies ran while one was open for 14% -> 7% of each run, Pallas kernels for 0% -> 0%
where the time goes in v1:
time: 270 us; the launch traced here: 269 us
  waiting for transfers between devices  86.7 us (32%)
  blocking collectives  50.4 us (19%)
  local copies, waits for them, and re-layouts  44.5 us (16%)
  matrix products  30 us (11%)
  starting transfers between devices  27.9 us (10%)
  between operations  21.3 us (8%)
  other arithmetic  8.47 us (3%)
    all_to_all x2, blocking collectives, exchange(): return lax.all_to_all(blocks, axis, split_axis=0, concat_axis=0, tiled=True)  50.4 us
    all_to_all x1, waiting for transfers between devices, summed_on_arrival(): lax.all_to_all(blocks, axis, split_axis=0, concat_axis=0, tiled=True)  36.9 us
    all_gather x1, waiting for transfers between devices, on_device(): lax.all_gather(jnp.concatenate([qkv_columns, out_tall], axis=1), 'row', a...  31 us
    all_to_all x2, waiting for transfers between devices, exchange(): return lax.all_to_all(blocks, axis, split_axis=0, concat_axis=0, tiled=True)  16.1 us
    all_to_all x2, starting transfers between devices, exchange(): return lax.all_to_all(blocks, axis, split_axis=0, concat_axis=0, tiled=True)  12.5 us
    ppermute x4, starting transfers between devices, from_behind(): return lax.ppermute(value, axis, pairs)  11.6 us
  transfers between devices with their start and end apart: 8, of which 5 were waited for; matrix products, arithmetic and copies ran while one was open for 7% of the time, Pallas kernels for 0%

profile of v1, /device:TPU:1, one launch (start us, length us, event | category | flops | bytes accessed | tf_op | source)
XLA Modules:
  0.0 269.2 jit_solution(6066088477923813417)
XLA Ops:
  7.2 0.8 reshape.251
  8.0 0.8 reshape.250
  9.6 1.8 reduce.5
  11.5 28.5 %all_to_all.33 = bf16[16,2,3072]{2,1,0:T(2,128)(2,1)S(1)} all-to-all(bf16[16,2,3072]{2,1,0:T(2,128)(2,1)S(1)} %reshape.400), channel_id=1, replica_groups=mesh['row'=32,'col'=8,'dp'=2] {'col','dp'}, dimensions={0} | all-to-all | bytes 393216 | tf_op jit(solution)/shard_map/all_to_all | solution.py:20
  42.2 3.7 %collective-permute-start = (bf16[1,3,32,128]{3,2,1,0:T(8,128)(2,1)S(1)}, bf16[1,3,32,128]{3,2,1,0:T(8,128)(2,1)S(1)}, u32[]{:S(2)}, u32[]{:S(2)}) collective-permute-start(bf16[1,3,32,128]{3,2,1,0:T(8,128)(2,1)S(1)} %copy-done.12), channel_id=1, source_target_pairs={{0,496},{16,0},{32,16},{48,32},{64,48},{80,64},{96,80},{112,96},{1... | collective-permute-start | bytes 73736 | tf_op jit(solution)/shard_map/ppermute | solution.py:41
  45.9 3.3 %collective-permute-start.2 = (bf16[1,8,32,1024]{3,2,1,0:T(8,128)(2,1)S(1)}, bf16[1,8,32,1024]{3,2,1,0:T(8,128)(2,1)S(1)}, u32[]{:S(2)}, u32[]{:S(2)}) collective-permute-start(bf16[1,8,32,1024]{3,2,1,0:T(8,128)(2,1)S(1)} %copy-done.3), channel_id=1, source_target_pairs={{0,496},{16,0},{32,16},{48,32},{64,48},{80,64},{96,80},{112,96},{1... | collective-permute-start | bytes 1572872 | tf_op jit(solution)/shard_map/ppermute | solution.py:41
  49.3 1.7 reshape.246
  54.0 2.6 convolution_bitcast_fusion
  56.5 0.9 fusion.48
  58.3 1.9 collective-permute-start.1
  63.7 0.9 copy.218
  66.1 1.7 reshape.248
  69.7 2.6 collective-permute-start.3
  73.3 2.6 collective-permute-done.3
  76.2 31.0 %all-gather.2.cloned.1.call-done = bf16[1024,3072]{1,0:T(8,128)(2,1)} async-done(((bf16[32,3072]{1,0:T(8,128)(2,1)}), bf16[1024,3072]{1,0:T(8,128)(2,1)}) %all-gather.2.cloned.1.call-update) | async-done | bytes 6291472 | tf_op jit(solution)/shard_map/all_gather | solution.py:214
  107.2 3.7 %fusion.6 = bf16[256,2304]{1,0:T(8,128)(2,1)S(1)} fusion(bf16[256,1024]{1,0:T(8,128)(2,1)S(1)} %multiply_convert_fusion.3, bf16[1024,3072]{1,0:T(8,128)(2,1)} %all-gather.2.cloned.1.call-done), kind=kOutput, calls=%fused_computation.8 | convolution fusion | flops 1208549376 | bytes 6422528 | tf_op jit(solution)/shard_map/dot_general | solution.py:107
  110.9 1.0 fusion.43
  112.5 1.0 copy.224
  113.5 1.7 reshape.398
  115.2 1.6 copy.237
  116.8 2.5 reshape.396
  119.2 1.8 copy.228
  121.0 2.7 %slice.173 = bf16[1024,768]{1,0:T(8,128)(2,1)} slice(bf16[1024,3072]{1,0:T(8,128)(2,1)} %all-gather.2.cloned.1.call-done), slice={[0:1024], [2304:3072]} | slice | bytes 3145728 | tf_op jit(solution)/shard_map/slice | solution.py:218
  123.8 3.9 %reshape.257 = bf16[768,1024]{1,0:T(8,128)(2,1)} reshape(bf16[1024,768]{1,0:T(8,128)(2,1)} %slice.173) | data formatting | bytes 3145728 | tf_op jit(solution)/shard_map/reshape | solution.py:218
  127.7 2.8 %convolution_convert_fusion.3 = bf16[256,768]{1,0:T(8,128)(2,1)} fusion(bf16[256,1024]{1,0:T(8,128)(2,1)S(1)} %bitcast.133, bf16[768,1024]{1,0:T(8,128)(2,1)} %reshape.257), kind=kOutput, calls=%fused_computation.28 | convolution fusion | flops 402849792 | bytes 2490368 | tf_op jit(solution)/shard_map/dot_general | solution.py:247
  130.4 2.5 reshape.397
  132.9 2.5 copy.232
  135.9 1.7 fusion.47
  137.6 3.6 %fusion.14 = bf16[4,64,12,64]{1,3,2,0:T(8,128)(2,1)} fusion(bf16[4,64,12,64]{1,3,2,0:T(8,128)(2,1)} %copy.232, f32[4,12,64]{2,1,0:T(8,128)S(1)} %get-tuple-element.63, f32[4,12,64,64]{2,3,1,0:T(8,128)} %copy-done.1), kind=kOutput, calls=%fused_computation.24 | convolution fusion | flops 25955392 | bytes 1585152 | tf_op jit(solution)/shard_map/whmn,wmhd->wnhd/dot_general | solution.py:156
  141.2 2.5 multiply_reduce_fusion
  143.7 1.3 fusion.29
  145.0 1.5 fusion.17
  146.4 1.5 fusion.16
  149.1 1.6 copy.227
  150.7 1.3 reshape.260
  152.0 0.8 copy.231
  153.3 4.2 %multiply_reduce_fusion.2 = (f32[256]{0:T(256)S(1)}, f32[1024]{0:T(1024)S(1)}, f32[256]{0:T(256)S(1)}, f32[256,1024]{1,0:T(8,128)S(1)}) fusion(f32[1,4,8,8,1024]{4,3,2,1,0:T(8,128)S(1)} %copy.211, f32[1024]{0:T(1024)S(1)} %copy-done.15, f32[256]{0:T(256)S(1)} %div.24, f32[256]{0:T(256)S(1)} %rsqrt.12, bf16[1024,3072]{1,0:T(8,128)(2,1)} %all-gather.2.cloned.1.call-done, ...), kind=kOutput, calls=%fused_computation.47 | convolution fusion | flops 1213594112 | bytes 8007680 | tf_op jit(solution)/shard_map/dot_general | solution.py:180
  158.8 1.4 fusion.1
  160.7 0.7 select_maximum_fusion
  161.4 5.1 %all-to-all-start.1 = ((f32[32,16,128]{2,1,0:T(8,128)}), f32[32,16,128]{2,1,0:T(8,128)S(1)}, u32[]{:S(2)}, u32[]{:S(2)}) async-start(f32[32,16,128]{2,1,0:T(8,128)} %bitcast.30), calls=%async_computation.1 | async-start | bytes 524288 | tf_op jit(solution)/shard_map/all_to_all | solution.py:20
  166.5 2.5 fusion.15
  170.1 1.7 convolution_convert_fusion
  171.8 5.7 %all-to-all-done.1 = f32[32,16,128]{2,1,0:T(8,128)S(1)} async-done(((f32[32,16,128]{2,1,0:T(8,128)}), f32[32,16,128]{2,1,0:T(8,128)S(1)}, u32[]{:S(2)}, u32[]{:S(2)}) %all-to-all-start.1) | async-done | bytes 262176 | tf_op jit(solution)/shard_map/all_to_all | solution.py:20
  177.6 3.9 %all-to-all-start.2 = ((bf16[32,24,1024]{2,1,0:T(8,128)(2,1)}), bf16[32,24,1024]{2,1,0:T(8,128)(2,1)S(1)}, u32[]{:S(2)}, u32[]{:S(2)}) async-start(bf16[32,24,1024]{2,1,0:T(8,128)(2,1)} %bitcast.33), calls=%async_computation.2 | async-start | bytes 3145728 | tf_op jit(solution)/shard_map/all_to_all | solution.py:51
  181.5 36.9 %all-to-all-done.2 = bf16[32,24,1024]{2,1,0:T(8,128)(2,1)S(1)} async-done(((bf16[32,24,1024]{2,1,0:T(8,128)(2,1)}), bf16[32,24,1024]{2,1,0:T(8,128)(2,1)S(1)}, u32[]{:S(2)}, u32[]{:S(2)}) %all-to-all-start.2) | async-done | bytes 1572896 | tf_op jit(solution)/shard_map/all_to_all | solution.py:51
  219.1 21.9 %all_to_all.34 = f32[16,1,3584]{2,1,0:T(1,128)S(1)} all-to-all(f32[16,1,3584]{2,1,0:T(1,128)S(1)} %all_to_all.25), channel_id=1, replica_groups=mesh['row'=32,'col'=8,'dp'=2] {'col','dp'}, dimensions={0} | all-to-all | bytes 458752 | tf_op jit(solution)/shard_map/all_to_all | solution.py:20
  241.9 7.4 %all-to-all-start.4 = ((f32[32,16,128]{2,1,0:T(8,128)}), f32[32,16,128]{2,1,0:T(8,128)S(1)}, u32[]{:S(2)}, u32[]{:S(2)}) async-start(f32[32,16,128]{2,1,0:T(8,128)} %broadcast_in_dim.66), calls=%async_computation.4 | async-start | bytes 524288 | tf_op jit(solution)/shard_map/all_to_all | solution.py:20
  250.0 10.4 %all-to-all-done.4 = f32[32,16,128]{2,1,0:T(8,128)S(1)} async-done(((f32[32,16,128]{2,1,0:T(8,128)}), f32[32,16,128]{2,1,0:T(8,128)S(1)}, u32[]{:S(2)}, u32[]{:S(2)}) %all-to-all-start.4) | async-done | bytes 262176 | tf_op jit(solution)/shard_map/all_to_all | solution.py:20
  (125 shorter events, 18.0 us)
Async XLA Ops:
  7.2 61.2 %copy-start = (bf16[48,1024]{1,0:T(8,128)(2,1)S(1)}, bf16[48,1024]{1,0:T(8,128)(2,1)}, u32[]{:S(2)}) copy-start(bf16[48,1024]{1,0:T(8,128)(2,1)} %param.12) | copy-start | bytes 294916
  7.2 100.0 %all-gather.2.cloned.1.call-start = ((), (), s32[]{:S(2)}) async-start(), calls=%async_computation.5 | async-start | bytes 6488064 | tf_op jit(solution)/shard_map/all_gather | solution.py:214
  40.1 2.1 copy-start.12
  40.1 5.8 %copy-start.3 = (bf16[1,8,32,1024]{3,2,1,0:T(8,128)(2,1)S(1)}, bf16[1,8,32,1024]{3,2,1,0:T(8,128)(2,1)}, u32[]{:S(2)}) copy-start(bf16[1,8,32,1024]{3,2,1,0:T(8,128)(2,1)} %param.11) | copy-start | bytes 1572868
  40.4 10.6 %copy-start.19 = (s32[1,2]{1,0:T(1,128)S(1)}, s32[1,2]{1,0:T(1,128)}, u32[]{:S(2)}) copy-start(s32[1,2]{1,0:T(1,128)} %param.19) | copy-start | bytes 28
  40.4 12.7 %copy-start.14 = (s32[64,64]{1,0:T(8,128)S(1)}, s32[64,64]{1,0:T(8,128)}, u32[]{:S(2)}) copy-start(s32[64,64]{1,0:T(8,128)} %param.18) | copy-start | bytes 49156
  41.2 12.8 %copy-start.20 = (f32[12,225]{1,0:T(8,128)S(1)}, f32[12,225]{1,0:T(8,128)}, u32[]{:S(2)}) copy-start(f32[12,225]{1,0:T(8,128)} %param.17) | copy-start | bytes 32404
  42.2 16.0 %collective-permute-start = (bf16[1,3,32,128]{3,2,1,0:T(8,128)(2,1)S(1)}, bf16[1,3,32,128]{3,2,1,0:T(8,128)(2,1)S(1)}, u32[]{:S(2)}, u32[]{:S(2)}) collective-permute-start(bf16[1,3,32,128]{3,2,1,0:T(8,128)(2,1)S(1)} %copy-done.12), channel_id=1, source_target_pairs={{0,496},{16,0},{32,16},{48,32},{64,48},{80,64},{96,80},{112,96},{1... | collective-permute-start | bytes 73736 | tf_op jit(solution)/shard_map/ppermute | solution.py:41
  45.9 23.5 %collective-permute-start.2 = (bf16[1,8,32,1024]{3,2,1,0:T(8,128)(2,1)S(1)}, bf16[1,8,32,1024]{3,2,1,0:T(8,128)(2,1)S(1)}, u32[]{:S(2)}, u32[]{:S(2)}) collective-permute-start(bf16[1,8,32,1024]{3,2,1,0:T(8,128)(2,1)S(1)} %copy-done.3), channel_id=1, source_target_pairs={{0,496},{16,0},{32,16},{48,32},{64,48},{80,64},{96,80},{112,96},{1... | collective-permute-start | bytes 1572872 | tf_op jit(solution)/shard_map/ppermute | solution.py:41
  53.1 5.1 %copy-start.16 = (s32[4096]{0:T(1024)}, s32[4096]{0:T(1024)S(1)}, u32[]{:S(2)}) copy-start(s32[4096]{0:T(1024)S(1)} %eq.39) | copy-start | bytes 49156
  58.3 7.7 %collective-permute-start.1 = (bf16[1,3,32,32]{3,2,1,0:T(8,128)(2,1)S(1)}, bf16[1,3,32,32]{3,2,1,0:T(8,128)(2,1)S(1)}, u32[]{:S(2)}, u32[]{:S(2)}) collective-permute-start(bf16[1,3,32,32]{3,2,1,0:T(8,128)(2,1)S(1)} %bitcast.145), channel_id=1, source_target_pairs={{0,14},{2,0},{4,2},{6,4},{8,6},{10,8},{12,10},{14,12},{1,15},{3,1}... | collective-permute-start | bytes 18440 | tf_op jit(solution)/shard_map/ppermute | solution.py:41
  63.5 4.9 %copy-start.18 = (f32[1024]{0:T(1024)S(1)}, f32[1024]{0:T(1024)}, u32[]{:S(2)}) copy-start(f32[1024]{0:T(1024)} %param.13) | copy-start | bytes 12292
  69.1 3.2 %copy-start.15 = (f32[1024]{0:T(1024)S(1)}, f32[1024]{0:T(1024)}, u32[]{:S(2)}) copy-start(f32[1024]{0:T(1024)} %param.14) | copy-start | bytes 12292
  69.7 6.1 %collective-permute-start.3 = (bf16[1,8,8,1024]{3,2,1,0:T(8,128)(2,1)S(1)}, bf16[1,8,8,1024]{3,2,1,0:T(8,128)(2,1)S(1)}, u32[]{:S(2)}, u32[]{:S(2)}) collective-permute-start(bf16[1,8,8,1024]{3,2,1,0:T(8,128)(2,1)S(1)} %slice.172), channel_id=1, source_target_pairs={{0,14},{2,0},{4,2},{6,4},{8,6},{10,8},{12,10},{14,12},{1,15},{3,1}... | collective-permute-start | bytes 393224 | tf_op jit(solution)/shard_map/ppermute | solution.py:41
  76.2 51.5 %copy-start.5 = (bf16[1,4,8,8,1024]{4,3,2,1,0:T(8,128)(2,1)}, bf16[1,4,8,8,1024]{4,3,2,1,0:T(8,128)(2,1)S(1)}, u32[]{:S(2)}) copy-start(bf16[1,4,8,8,1024]{4,3,2,1,0:T(8,128)(2,1)S(1)} %copy.219) | copy-start | bytes 1572868
  130.4 5.0 %copy-start.7 = (f32[12,64,64]{1,2,0:T(8,128)S(1)}, f32[12,64,64]{1,2,0:T(8,128)}, u32[]{:S(2)}) copy-start(f32[12,64,64]{1,2,0:T(8,128)} %copy.218) | copy-start | bytes 589828
  135.9 1.7 copy-start.1
  141.2 2.5 copy-start.2
  146.4 1.5 copy-start.10
  149.1 2.9 %copy-start.4 = (bf16[4,64,12,64]{3,1,2,0:T(8,128)(2,1)S(1)}, bf16[4,64,12,64]{3,1,2,0:T(8,128)(2,1)}, u32[]{:S(2)}) copy-start(bf16[4,64,12,64]{3,1,2,0:T(8,128)(2,1)} %fusion.17) | copy-start | bytes 1179652
  157.5 1.0 copy-start.8
  157.9 0.9 copy-start.17
  158.0 2.3 copy-start.11
  158.0 2.3 copy-start.13
  158.8 7.7 %copy-start.9 = (bf16[4,64,12,64]{1,3,2,0:T(8,128)(2,1)S(1)}, bf16[4,64,12,64]{1,3,2,0:T(8,128)(2,1)}, u32[]{:S(2)}) copy-start(bf16[4,64,12,64]{1,3,2,0:T(8,128)(2,1)} %copy.237) | copy-start | bytes 1179652
  161.4 16.2 %all-to-all-start.1 = ((f32[32,16,128]{2,1,0:T(8,128)}), f32[32,16,128]{2,1,0:T(8,128)S(1)}, u32[]{:S(2)}, u32[]{:S(2)}) async-start(f32[32,16,128]{2,1,0:T(8,128)} %bitcast.30), calls=%async_computation.1 | async-start | bytes 524288 | tf_op jit(solution)/shard_map/all_to_all | solution.py:20
  169.0 1.1 copy-start.6
  177.6 40.9 %all-to-all-start.2 = ((bf16[32,24,1024]{2,1,0:T(8,128)(2,1)}), bf16[32,24,1024]{2,1,0:T(8,128)(2,1)S(1)}, u32[]{:S(2)}, u32[]{:S(2)}) async-start(bf16[32,24,1024]{2,1,0:T(8,128)(2,1)} %bitcast.33), calls=%async_computation.2 | async-start | bytes 3145728 | tf_op jit(solution)/shard_map/all_to_all | solution.py:51
  241.9 18.4 %all-to-all-start.4 = ((f32[32,16,128]{2,1,0:T(8,128)}), f32[32,16,128]{2,1,0:T(8,128)S(1)}, u32[]{:S(2)}, u32[]{:S(2)}) async-start(f32[32,16,128]{2,1,0:T(8,128)} %broadcast_in_dim.66), calls=%async_computation.4 | async-start | bytes 524288 | tf_op jit(solution)/shard_map/all_to_all | solution.py:20
Sparse Core Ops, SparseCore 0:
  42.3 64.7 all-gather.1

commit v2 on v1

v2 whole, which is shorter than its diff:
```python
import jax
import jax.numpy as jnp
from jax import lax
from jax.experimental import pallas as pl
from jax.experimental.pallas import tpu as pltpu
from jax.sharding import PartitionSpec as P

WIN = 8
PATCH = 4
CELLS = WIN * WIN
norm_epsilon = 1e-05

STEP = 256
PAIR = 128
HEAD = 64
SCALE = HEAD ** (-0.5)


def dot_nn(a, b):
    return lax.dot_general(a, b, (((1,), (0,)), ((), ())), preferred_element_type=jnp.float32)


def dot_nt(a, b):
    return lax.dot_general(a, b, (((1,), (1,)), ((), ())), preferred_element_type=jnp.float32)


def dot_tn(a, b):
    return lax.dot_general(a, b, (((0,), (0,)), ((), ())), preferred_element_type=jnp.float32)


def head_lanes(width):
    lane = lax.broadcasted_iota(jnp.int32, (PAIR, width), 1)
    return [(lane // HEAD) == i for i in range(width // HEAD)]


def slabs(features):
    return [(at, min(PAIR, features - at)) for at in range(0, features, PAIR)]


def choose(masks, parts):
    return parts[0] if len(parts) == 1 else jnp.where(masks[0], parts[0], parts[1])


def forward_kernel(
    normed, cot, wq, wk, wv, bias, lab_col, lab_row, q_out, k_out, v_out, p_out, og_out, att, og_acc
):
    step = pl.program_id(0)
    x = normed[...]
    for weight, out in ((wq, q_out), (wk, k_out), (wv, v_out)):
        out[...] = dot_nn(x, weight[...]).astype(jnp.bfloat16)
    features = q_out.shape[1]
    for pair in range(STEP // PAIR):
        rows = slice(pair * PAIR, (pair + 1) * PAIR)
        same = lab_col[rows, :] == lab_row[pair, 0:1, :]
        for at, width in slabs(features):
            cols = slice(at, at + width)
            masks = head_lanes(width)
            q, k, v = q_out[rows, cols], k_out[rows, cols], v_out[rows, cols]
            parts = []
            for i, mask in enumerate(masks):
                head = at // HEAD + i
                mine = q if len(masks) == 1 else jnp.where(mask, q, jnp.zeros_like(q))
                scores = jnp.where(same, dot_nt(mine, k) * SCALE + bias[head], -1e30)
                peak = jnp.max(scores, axis=-1, keepdims=True)
                e = jnp.exp(scores - peak)
                p = e / jnp.sum(e, axis=-1, keepdims=True)
                p_out[pair, head] = p
                parts.append(dot_nn(p.astype(jnp.bfloat16), v))
            att[rows, cols] = choose(masks, parts).astype(jnp.bfloat16)
    grad = dot_tn(att[...], cot[...])

    @pl.when(step == 0)
    def _():
        og_acc[...] = grad

    @pl.when(step > 0)
    def _():
        og_acc[...] += grad

    @pl.when(step == pl.num_programs(0) - 1)
    def _():
        og_out[...] = og_acc[...].astype(og_out.dtype)


def backward_kernel(
    cot, patches, q_in, k_in, v_in, p_in, xhat, inv, gain, wq, wk, wv, wo,
    embed_out, bias_out, gain_out, table_out, datt, dq, dk, dv, dn, branch
):
    step = pl.program_id(0)
    features = q_in.shape[1]

    @pl.when(step == 0)
    def _():
        embed_out[...] = jnp.zeros_like(embed_out)
        bias_out[...] = jnp.zeros_like(bias_out)
        gain_out[...] = jnp.zeros_like(gain_out)
        table_out[...] = jnp.zeros_like(table_out)

    datt[...] = dot_nt(cot[...], wo[...]).astype(jnp.bfloat16)
    for pair in range(STEP // PAIR):
        rows = slice(pair * PAIR, (pair + 1) * PAIR)
        for at, width in slabs(features):
            cols = slice(at, at + width)
            masks = head_lanes(width)
            q, k, v = q_in[rows, cols], k_in[rows, cols], v_in[rows, cols]
            d_out = datt[rows, cols]
            qs, ks, vs = [], [], []
            for i, mask in enumerate(masks):
                head = at // HEAD + i
                mine = d_out if len(masks) == 1 else jnp.where(mask, d_out, jnp.zeros_like(d_out))
                p = p_in[pair, head]
                d_prob = dot_nt(mine, v)
                vs.append(dot_tn(p.astype(jnp.bfloat16), d_out))
                d_scores = p * (d_prob - jnp.sum(p * d_prob, axis=-1, keepdims=True))
                table_out[head] += d_scores
                low = d_scores.astype(jnp.bfloat16)
                qs.append(dot_nn(low, k))
                ks.append(dot_tn(low, q))
            dq[rows, cols] = (choose(masks, qs) * SCALE).astype(jnp.bfloat16)
            dk[rows, cols] = (choose(masks, ks) * SCALE).astype(jnp.bfloat16)
            dv[rows, cols] = choose(masks, vs).astype(jnp.bfloat16)
    dn[...] = dot_nt(dq[...], wq[...]) + dot_nt(dk[...], wk[...]) + dot_nt(dv[...], wv[...])
    chunk = 16
    width = dn.shape[1]
    gain_row = gain[0:1, :]

    def rows_at(i, carry):
        bias_sum, gain_sum = carry
        rows = pl.ds(pl.multiple_of(i * chunk, chunk), chunk)
        d, x = dn[rows, :], xhat[rows, :]
        gain_sum = gain_sum + (d * x).reshape(chunk // 8, 8, width).sum(axis=0)
        g = d * gain_row
        mean = jnp.mean(g, axis=-1, keepdims=True)
        along = jnp.mean(g * x, axis=-1, keepdims=True)
        out = (inv[rows, 0:1] * (g - mean - x * along)).astype(jnp.bfloat16)
        branch[rows, :] = out
        bias_sum = bias_sum + out.astype(jnp.float32).reshape(chunk // 8, 8, width).sum(axis=0)
        return bias_sum, gain_sum

    zero = jnp.zeros((8, width), jnp.float32)
    bias_sum, gain_sum = lax.fori_loop(0, STEP // chunk, rows_at, (zero, zero))
    bias_out[...] += bias_sum
    gain_out[...] += gain_sum
    embed_out[...] += dot_tn(patches[...], branch[...])


def stepped(shape, lead=False):
    rest = len(shape) - 1
    return pl.BlockSpec(shape, lambda i: (i,) + (0,) * rest)


def whole(shape, index=None):
    index = index or (0,) * len(shape)
    return pl.BlockSpec(shape, lambda i: index)


def params():
    return pltpu.CompilerParams(
        dimension_semantics=("arbitrary",), vmem_limit_bytes=56 * 1024 * 1024
    )


def run_forward(normed, cot, weights, weight_index, features, bias, lab_col, lab_row):
    cells, width = normed.shape
    heads = features // HEAD
    f32, bf16 = jnp.float32, jnp.bfloat16
    w_specs = [whole((width, features), index) for index in weight_index[:3]]
    return pl.pallas_call(
        forward_kernel,
        grid=(cells // STEP,),
        in_specs=[
            stepped((STEP, width)), stepped((STEP, width)), *w_specs,
            whole((heads, PAIR, PAIR)), stepped((STEP, PAIR)), stepped((STEP // PAIR, 8, PAIR)),
        ],
        out_specs=[
            *[stepped((STEP, features))] * 3,
            stepped((STEP // PAIR, heads, PAIR, PAIR)),
            whole((features, width)),
        ],
        out_shape=[
            *[jax.ShapeDtypeStruct((cells, features), bf16)] * 3,
            jax.ShapeDtypeStruct((cells // PAIR, heads, PAIR, PAIR), f32),
            jax.ShapeDtypeStruct((features, width), bf16),
        ],
        scratch_shapes=[pltpu.VMEM((STEP, features), bf16), pltpu.VMEM((features, width), f32)],
        compiler_params=params(), name="forward",
    )(normed, cot, *weights, bias, lab_col, lab_row)


def run_backward(cot, patches, q, k, v, p, xhat, inv, gain, weights, weight_index, wo):
    cells, width = cot.shape
    features = q.shape[1]
    heads = features // HEAD
    f32, bf16 = jnp.float32, jnp.bfloat16
    kd = patches.shape[1]
    w_specs = [whole((width, features), index) for index in weight_index[:3]]
    return pl.pallas_call(
        backward_kernel,
        grid=(cells // STEP,),
        in_specs=[
            stepped((STEP, width)), stepped((STEP, kd)), *[stepped((STEP, features))] * 3,
            stepped((STEP // PAIR, heads, PAIR, PAIR)),
            stepped((STEP, width)), stepped((STEP, PAIR)), whole((8, width)), *w_specs,
            whole((features, width)),
        ],
        out_specs=[whole((kd, width)), whole((8, width)), whole((8, width)), whole((heads, PAIR, PAIR))],
        out_shape=[
            jax.ShapeDtypeStruct((kd, width), f32), jax.ShapeDtypeStruct((8, width), f32),
            jax.ShapeDtypeStruct((8, width), f32), jax.ShapeDtypeStruct((heads, PAIR, PAIR), f32),
        ],
        scratch_shapes=[
            *[pltpu.VMEM((STEP, features), bf16)] * 4,
            pltpu.VMEM((STEP, width), f32), pltpu.VMEM((STEP, width), bf16),
        ],
        compiler_params=params(), name="backward",
    )(cot, patches, q, k, v, p, xhat, inv, gain, *weights, wo)


def exchange(blocks, axis):
    return lax.all_to_all(blocks, axis, split_axis=0, concat_axis=0, tiled=True)


def spread(line, axis):
    copies = jnp.broadcast_to(line[None], (lax.axis_size(axis), *line.shape))
    return exchange(copies, axis)


def from_behind(value, axis, steps):
    count = lax.axis_size(axis)
    pairs = [(source, (source + steps) % count) for source in range(count)]
    return lax.ppermute(value, axis, pairs)


def in_blocks(x, dim, length):
    before, after = (x.shape[:dim], x.shape[dim + 1 :])
    return jnp.moveaxis(x.reshape(*before, length, -1, *after), dim, 0)


def make_patches(pixel_block):
    channels, pixel_rows, pixel_cols = pixel_block.shape
    grid_rows = pixel_rows // PATCH
    grid_cols = pixel_cols // PATCH
    shaped = pixel_block.reshape(channels, grid_rows, PATCH, grid_cols, PATCH)
    return shaped.transpose(1, 3, 0, 2, 4).reshape(grid_rows, grid_cols, channels * PATCH * PATCH)


def window_split(block):
    rows_all, cols_all, features = block.shape
    shaped = block.reshape(rows_all // WIN, WIN, cols_all // WIN, WIN, features)
    return shaped.transpose(0, 2, 1, 3, 4).reshape(-1, features)


def splice_after(own, borrowed, offset, dim):
    joined = jnp.concatenate([own, borrowed], dim)
    return lax.dynamic_slice_in_dim(joined, offset, own.shape[dim], dim)


def on_device(
    pixels,
    cotangent,
    embed_weight,
    embed_bias,
    layer_norm_gain,
    qkv_weight,
    out_weight,
    bias_table,
    rel_index,
    shifts,
):
    cotangent, pixels = cotangent[0], pixels[0]
    rows_dev, cols_dev, width = cotangent.shape
    heads, table_size = bias_table.shape
    features = heads * HEAD
    grid_rows = rows_dev * lax.axis_size("row")
    grid_cols = cols_dev * lax.axis_size("col")
    row_shift, col_shift = shifts[0, 0], shifts[0, 1]
    rows_w = qkv_weight.shape[0]

    line = jnp.concatenate([qkv_weight.reshape(-1), out_weight.reshape(-1)])
    lines = spread(line, ("col", "dp"))
    count = lines.shape[0]
    split = qkv_weight.size
    qkv_rows = jnp.moveaxis(lines[:, :split].reshape(count, *qkv_weight.shape), 0, 1)
    out_rows = jnp.moveaxis(lines[:, split:].reshape(count, *out_weight.shape), 0, 1)
    weights = lax.all_gather(
        jnp.concatenate([qkv_rows.reshape(rows_w, -1), out_rows.reshape(rows_w, -1)], axis=1),
        "row", axis=0, tiled=True,
    )
    wo = weights[:, 3 * features :].reshape(features, width)

    below = from_behind((pixels, cotangent), "row", -1)
    pix = splice_after(pixels, below[0], row_shift * PATCH, 1)
    cot = splice_after(cotangent, below[1], row_shift, 0)
    beside = from_behind((pix[:, :, : WIN * PATCH], cot[:, :WIN]), "col", -1)
    pix = splice_after(pix, beside[0], col_shift * PATCH, 2)
    cot = splice_after(cot, beside[1], col_shift, 1)
    patches = window_split(make_patches(pix))
    cot = window_split(cot)
    cells = cot.shape[0]
    tokens = jnp.dot(patches, embed_weight, preferred_element_type=jnp.float32) + embed_bias
    tokens = tokens.astype(jnp.bfloat16).astype(jnp.float32)
    centered = tokens - jnp.mean(tokens, axis=-1, keepdims=True)
    inv = lax.rsqrt(jnp.mean(centered * centered, axis=-1, keepdims=True) + norm_epsilon)
    xhat = centered * inv
    normed = (xhat * layer_norm_gain).astype(jnp.bfloat16)
    inv = jnp.broadcast_to(inv, (cells, PAIR))

    row_ids = lax.axis_index("row") * rows_dev + jnp.arange(rows_dev, dtype=jnp.int32)
    col_ids = lax.axis_index("col") * cols_dev + jnp.arange(cols_dev, dtype=jnp.int32)
    row_part = (row_ids >= grid_rows - row_shift).astype(jnp.int32)
    col_part = (col_ids >= grid_cols - col_shift).astype(jnp.int32)
    region = window_split((2 * row_part[:, None] + col_part[None, :])[:, :, None])[:, 0]
    label = region + 4 * (jnp.arange(cells, dtype=jnp.int32) // CELLS)
    lab_col = jnp.broadcast_to(label[:, None], (cells, PAIR))
    lab_row = jnp.broadcast_to(label.reshape(-1, 1, PAIR), (cells // PAIR, 8, PAIR))
    selector = (
        rel_index.reshape(-1)[:, None] == jnp.arange(table_size, dtype=jnp.int32)[None, :]
    ).astype(jnp.float32)
    bias = jnp.dot(selector, bias_table.T, precision=lax.Precision.HIGHEST).T
    bias = jnp.tile(bias.reshape(heads, CELLS, CELLS), (1, 2, 2))

    trio = (weights, weights, weights)
    places = ((0, 0), (0, 1), (0, 2))
    q, k, v, prob, out_grad = run_forward(
        normed, cot, trio, places, features, bias, lab_col, lab_row
    )
    arrived = exchange(in_blocks(out_grad, 0, lax.axis_size("row")), "row")
    gain = jnp.broadcast_to(layer_norm_gain[None], (8, width))
    embed_part, bias_part, gain_part, table_part = run_backward(
        cot, patches, q, k, v, prob, xhat, inv, gain, trio, places, wo
    )
    contract = (((0,), (0,)), ((), ()))
    embed_grad = embed_part + lax.dot_general(
        patches, cot, contract, preferred_element_type=jnp.float32
    )
    bias_grad = bias_part.sum(axis=0) + jnp.sum(cot, axis=0, dtype=jnp.float32)
    gain_grad = gain_part.sum(axis=0)
    table_part = table_part[:, :CELLS, :CELLS] + table_part[:, CELLS:, CELLS:]
    table_grad = jnp.dot(
        table_part.reshape(heads, -1), selector, precision=lax.Precision.HIGHEST
    )

    partial_rows = arrived.astype(jnp.float32).sum(axis=0)
    pieces = [embed_grad.reshape(-1), bias_grad, gain_grad, table_grad.reshape(-1)]
    line = jnp.concatenate(pieces)
    row_count = lax.axis_size("row")
    piece = -(-line.size // (row_count * 1024)) * 1024
    line = jnp.pad(line, (0, row_count * piece - line.size)).reshape(row_count, piece // 128, 128)
    mine = exchange(line, "row").sum(axis=0).reshape(-1)
    col_blocks = in_blocks(partial_rows, 1, lax.axis_size(("col", "dp")))
    block_shape = col_blocks.shape
    col_blocks = col_blocks.reshape(block_shape[0], -1)
    own = jnp.broadcast_to(mine[None], (block_shape[0], piece))
    both = exchange(jnp.concatenate([own, col_blocks], axis=1), ("col", "dp")).sum(axis=0)
    out_weight_grad = both[piece:].reshape(block_shape[1:])
    total = spread(both[:piece].reshape(piece // 128, 128), "row").reshape(-1)
    results, at = ([], 0)
    for a, shape in zip(pieces, (embed_grad.shape, (width,), (width,), table_grad.shape)):
        results.append(total[at : at + a.size].reshape(shape))
        at += a.size
    return (out_weight_grad, *results)


def solution(mesh):
    return jax.shard_map(
        on_device,
        mesh=mesh,
        in_specs=(
            P("dp", None, "row", "col"),
            P("dp", "row", "col", None),
            P(),
            P(),
            P(),
            P("row", ("col", "dp")),
            P("row", ("col", "dp")),
            P(),
            P(),
            P("dp", None),
        ),
        out_specs=(P("row", ("col", "dp")), P(), P(), P(), P()),
        check_vma=False,
    )
```

time: 270 us -> 254 us (0.941)
  Pallas kernels: 0 us -> 28.4 us
  matrix products: 30 us -> 4.6 us
  local copies, waits for them, and re-layouts: 44.5 us -> 21.7 us
  blocking collectives: 50.4 us -> 66 us
  waiting for transfers between devices: 86.7 us -> 81 us
  starting transfers between devices: 27.9 us -> 22.8 us
    all_to_all x1 -> x0, waiting for transfers between devices: 36.9 us -> none  [summed_on_arrival(): lax.all_to_all(blocks, axis, split_axis=0, concat_axis=0, tiled=True)]
    all_to_all x2, waiting for transfers between devices: 16.1 us -> 47.3 us  [exchange(): return lax.all_to_all(blocks, axis, split_axis=0, concat_axis=0, tiled=True)]
    pallas_call x0 -> x2, Pallas kernels: none -> 28.4 us  [the longest x1 15.1 us: run_backward(): pl.pallas_call(backward_kernel, grid=(cells // STEP,), in_specs=[stepped(...]
    dot_general x15 -> x4, matrix products: 30 us -> 4.6 us  [the longest x1 2.58 us: on_device(): bias = jnp.dot(selector, bias_table.T, precision=lax.Precision.HIGHEST).T]
    reshape x24 -> x11, local copies, waits for them, and re-layouts: 26.9 us -> 7.51 us  [the longest x1 2.14 us: on_device(): wo = weights[:, 3 * features:].reshape(features, width)]
    all_to_all x2 -> x3, blocking collectives: 50.4 us -> 66 us  [exchange(): return lax.all_to_all(blocks, axis, split_axis=0, concat_axis=0, tiled=True)]
    all_to_all x1 -> x0, starting transfers between devices: 3.86 us -> none  [summed_on_arrival(): lax.all_to_all(blocks, axis, split_axis=0, concat_axis=0, tiled=True)]
    convert_element_type x5 -> x0, local copies, waits for them, and re-layouts: 3.75 us -> none  [the longest x1 1.6 us: attend_backward(): d_queries = (jnp.einsum('whmn,wnhd->wmhd', d_low, key_vectors, preferred_...]
  transfers between devices with their start and end apart: 8 -> 7, of which waited for: 5 -> 4; matrix products, arithmetic and copies ran while one was open for 7% -> 5% of each run, Pallas kernels for 0% -> 0%
where the time goes in v2:
time: 254 us; the launch traced here: 253 us
  waiting for transfers between devices  81 us (32%)
  blocking collectives  66 us (26%)
  Pallas kernels  28.4 us (11%)
  starting transfers between devices  22.8 us (9%)
  local copies, waits for them, and re-layouts  21.7 us (9%)
  between operations  21.1 us (8%)
  other arithmetic  7.19 us (3%)
  matrix products  4.6 us (2%)
    all_to_all x3, blocking collectives, exchange(): return lax.all_to_all(blocks, axis, split_axis=0, concat_axis=0, tiled=True)  66 us
    all_to_all x2, waiting for transfers between devices, exchange(): return lax.all_to_all(blocks, axis, split_axis=0, concat_axis=0, tiled=True)  47.3 us
    all_gather x1, waiting for transfers between devices, on_device(): lax.all_gather(jnp.concatenate([qkv_rows.reshape(rows_w, -1), out_rows.re...  31.6 us
    pallas_call x1, Pallas kernels, run_backward(): pl.pallas_call(backward_kernel, grid=(cells // STEP,), in_specs=[stepped(...  15.1 us
    pallas_call x1, Pallas kernels, run_forward(): pl.pallas_call(forward_kernel, grid=(cells // STEP,), in_specs=[stepped((...  13.3 us
    ppermute x4, starting transfers between devices, from_behind(): return lax.ppermute(value, axis, pairs)  11.6 us
    all_to_all x2, starting transfers between devices, exchange(): return lax.all_to_all(blocks, axis, split_axis=0, concat_axis=0, tiled=True)  11.2 us
  transfers between devices with their start and end apart: 7, of which 4 were waited for; matrix products, arithmetic and copies ran while one was open for 5% of the time, Pallas kernels for 0%

profile of v2, /device:TPU:1, one launch (start us, length us, event | category | flops | bytes accessed | tf_op | source)
XLA Modules:
  0.0 252.8 jit_solution(12265614541505746069)
XLA Ops:
  7.2 0.8 reshape.217
  8.0 0.8 reshape.216
  9.0 0.5 broadcast.220
  9.6 1.8 reduce.2
  11.5 28.5 %all_to_all.33 = bf16[16,2,3072]{2,1,0:T(2,128)(2,1)S(1)} all-to-all(bf16[16,2,3072]{2,1,0:T(2,128)(2,1)S(1)} %reshape.238), channel_id=1, replica_groups=mesh['row'=32,'col'=8,'dp'=2] {'col','dp'}, dimensions={0} | all-to-all | bytes 393216 | tf_op jit(solution)/shard_map/all_to_all | solution.py:220
  40.6 0.4 reshape.218
  41.2 0.3 reshape.219
  41.5 0.7 pad_maximum_fusion.1
  42.2 3.7 %collective-permute-start.2 = (bf16[3,32,128]{2,1,0:T(8,128)(2,1)S(1)}, bf16[3,32,128]{2,1,0:T(8,128)(2,1)S(1)}, u32[]{:S(2)}, u32[]{:S(2)}) collective-permute-start(bf16[3,32,128]{2,1,0:T(8,128)(2,1)S(1)} %bitcast.86), channel_id=1, source_target_pairs={{0,496},{16,0},{32,16},{48,32},{64,48},{80,64},{96,80},{112,96},{1... | collective-permute-start | bytes 73736 | tf_op jit(solution)/shard_map/ppermute | solution.py:231
  45.9 3.3 %collective-permute-start = (bf16[8,32,1024]{2,1,0:T(8,128)(2,1)S(1)}, bf16[8,32,1024]{2,1,0:T(8,128)(2,1)S(1)}, u32[]{:S(2)}, u32[]{:S(2)}) collective-permute-start(bf16[8,32,1024]{2,1,0:T(8,128)(2,1)S(1)} %bitcast.81), channel_id=1, source_target_pairs={{0,496},{16,0},{32,16},{48,32},{64,48},{80,64},{96,80},{112,96},{1... | collective-permute-start | bytes 1572872 | tf_op jit(solution)/shard_map/ppermute | solution.py:231
  49.4 0.6 fusion.21
  51.5 2.6 %convolution_bitcast_fusion = f32[12,4096]{1,0:T(8,128)S(1)} fusion(f32[12,225]{1,0:T(8,128)S(1)} %copy-done.11, s32[4096]{0:T(1024)S(1)} %eq.15), kind=kOutput, calls=%fused_computation | convolution fusion | flops 133632000 | bytes 223792 | tf_op jit(solution)/shard_map/dot_general | solution.py:319
  54.9 1.9 collective-permute-start.3
  60.2 0.7 tile.11
  60.9 1.8 tile.12.bias
  64.1 1.7 reshape.214
  65.8 0.7 copy.33
  66.7 0.4 copy.34
  67.2 0.4 convert_reduce_fusion.1
  67.5 0.3 fusion.8
  68.1 2.6 %collective-permute-start.1 = (bf16[8,8,1024]{2,1,0:T(8,128)(2,1)S(1)}, bf16[8,8,1024]{2,1,0:T(8,128)(2,1)S(1)}, u32[]{:S(2)}, u32[]{:S(2)}) collective-permute-start(bf16[8,8,1024]{2,1,0:T(8,128)(2,1)S(1)} %slice.78), channel_id=1, source_target_pairs={{0,14},{2,0},{4,2},{6,4},{8,6},{10,8},{12,10},{14,12},{1,15},{3,1}... | collective-permute-start | bytes 393224 | tf_op jit(solution)/shard_map/ppermute | solution.py:231
  70.7 1.5 fusion.4
  72.2 2.0 collective-permute-done.1
  74.2 0.3 fusion.10
  74.5 0.9 copy.32
  75.4 0.3 convert_reduce_fusion.2
  75.7 31.6 %all-gather.2.cloned.1.call-done.wq.wk.wv = bf16[1024,3072]{1,0:T(8,128)(2,1)} async-done(((bf16[32,3072]{1,0:T(8,128)(2,1)}), bf16[1024,3072]{1,0:T(8,128)(2,1)}) %all-gather.2.cloned.1.call-update) | async-done | bytes 6291472 | tf_op jit(solution)/shard_map/all_gather | solution.py:285
  107.3 1.4 slice-done
  108.7 2.1 reshape.222.wo
  110.9 0.8 broadcast_in_dim.17.lab_col
  111.6 0.6 broadcast_in_dim.18.lab_row
  112.2 13.3 %forward.1 = (bf16[256,768]{1,0:T(8,128)(2,1)}, bf16[256,768]{1,0:T(8,128)(2,1)}, bf16[256,768]{1,0:T(8,128)(2,1)}, f32[2,12,128,128]{3,2,1,0:T(8,128)}, bf16[768,1024]{1,0:T(8,128)(2,1)}) custom-call(bf16[256,1024]{1,0:T(8,128)(2,1)} %get-tuple-element.24.normed, bf16[256,1024]{1,0:T(8,128)(2,1)} %bitcast.67, ...), custom_call_target="tpu_custom_call" | custom-call | tf_op jit(solution)/shard_map/forward/pallas_call | solution.py:168
  125.5 0.7 broadcast_in_dim.19.inv
  126.3 0.6 broadcast_in_dim.20.gain
  126.9 15.1 %backward.1 = (f32[48,1024]{1,0:T(8,128)}, f32[8,1024]{1,0:T(8,128)}, f32[8,1024]{1,0:T(8,128)}, f32[12,128,128]{2,1,0:T(8,128)}) custom-call(bf16[256,1024]{1,0:T(8,128)(2,1)} %bitcast.68, bf16[256,48]{1,0:T(8,128)(2,1)} %bitcast.80, bf16[256,768]{1,0:T(8,128)(2,1)} %get-tuple-element.14.q_in, bf16[256,768]{1,0:T(8,128)(2,1)} %get-tuple-element.15.k_in, ...), custom_call_target="tpu_custom_call" | custom-call | tf_op jit(solution)/shard_map/backward/pallas_call | solution.py:197
  142.0 1.3 slice_add_fusion
  143.5 1.4 fusion
  145.5 15.8 %all_to_all.34 = f32[32,16,128]{2,1,0:T(8,128)S(1)} all-to-all(f32[32,16,128]{2,1,0:T(8,128)S(1)} %bitcast.71), channel_id=1, replica_groups=mesh['row'=32,'col'=8,'dp'=2] {'row'}, dimensions={0} | all-to-all | bytes 524288 | tf_op jit(solution)/shard_map/all_to_all | solution.py:220
  161.3 3.9 %all-to-all-start.2 = ((bf16[32,24,1024]{2,1,0:T(8,128)(2,1)}), bf16[32,24,1024]{2,1,0:T(8,128)(2,1)S(1)}, u32[]{:S(2)}, u32[]{:S(2)}) async-start(bf16[32,24,1024]{2,1,0:T(8,128)(2,1)} %bitcast.70), calls=%async_computation.2 | async-start | bytes 3145728 | tf_op jit(solution)/shard_map/all_to_all | solution.py:220
  165.2 36.9 %all-to-all-done.2 = bf16[32,24,1024]{2,1,0:T(8,128)(2,1)S(1)} async-done(((bf16[32,24,1024]{2,1,0:T(8,128)(2,1)}), bf16[32,24,1024]{2,1,0:T(8,128)(2,1)S(1)}, u32[]{:S(2)}, u32[]{:S(2)}) %all-to-all-start.2) | async-done | bytes 1572896 | tf_op jit(solution)/shard_map/all_to_all | solution.py:220
  202.8 21.7 %all_to_all.35 = f32[16,1,3584]{2,1,0:T(1,128)S(1)} all-to-all(f32[16,1,3584]{2,1,0:T(1,128)S(1)} %all_to_all.25), channel_id=1, replica_groups=mesh['row'=32,'col'=8,'dp'=2] {'col','dp'}, dimensions={0} | all-to-all | bytes 458752 | tf_op jit(solution)/shard_map/all_to_all | solution.py:220
  224.7 0.7 broadcast_in_dim.23
  225.5 7.4 %all-to-all-start.4 = ((f32[32,16,128]{2,1,0:T(8,128)}), f32[32,16,128]{2,1,0:T(8,128)S(1)}, u32[]{:S(2)}, u32[]{:S(2)}) async-start(f32[32,16,128]{2,1,0:T(8,128)} %broadcast_in_dim.23), calls=%async_computation.4 | async-start | bytes 524288 | tf_op jit(solution)/shard_map/all_to_all | solution.py:220
  232.8 0.7 reshape.232
  233.5 10.4 %all-to-all-done.4 = f32[32,16,128]{2,1,0:T(8,128)S(1)} async-done(((f32[32,16,128]{2,1,0:T(8,128)}), f32[32,16,128]{2,1,0:T(8,128)S(1)}, u32[]{:S(2)}, u32[]{:S(2)}) %all-to-all-start.4) | async-done | bytes 262176 | tf_op jit(solution)/shard_map/all_to_all | solution.py:220
  243.9 0.6 fusion.20
  244.5 0.7 reshape.233
  245.2 0.7 reshape.235
  (80 shorter events, 3.8 us)
Async XLA Ops:
  7.2 60.0 %copy-start = (bf16[48,1024]{1,0:T(8,128)(2,1)S(1)}, bf16[48,1024]{1,0:T(8,128)(2,1)}, u32[]{:S(2)}) copy-start(bf16[48,1024]{1,0:T(8,128)(2,1)} %param.12) | copy-start | bytes 294916
  7.2 100.1 %all-gather.2.cloned.1.call-start = ((), (), s32[]{:S(2)}) async-start(), calls=%async_computation.5 | async-start | bytes 6488064 | tf_op jit(solution)/shard_map/all_gather | solution.py:285
  40.1 2.1 copy-start.8
  40.1 5.8 %copy-start.3 = (bf16[1,8,32,1024]{3,2,1,0:T(8,128)(2,1)S(1)}, bf16[1,8,32,1024]{3,2,1,0:T(8,128)(2,1)}, u32[]{:S(2)}) copy-start(bf16[1,8,32,1024]{3,2,1,0:T(8,128)(2,1)} %param.11) | copy-start | bytes 1572868
  40.1 9.2 %copy-start.5 = (s32[64,64]{1,0:T(8,128)S(1)}, s32[64,64]{1,0:T(8,128)}, u32[]{:S(2)}) copy-start(s32[64,64]{1,0:T(8,128)} %param.18) | copy-start | bytes 49156
  40.3 9.1 %copy-start.10 = (s32[1,2]{1,0:T(1,128)S(1)}, s32[1,2]{1,0:T(1,128)}, u32[]{:S(2)}) copy-start(s32[1,2]{1,0:T(1,128)} %param.19) | copy-start | bytes 28
  40.3 11.2 %copy-start.11 = (f32[12,225]{1,0:T(8,128)S(1)}, f32[12,225]{1,0:T(8,128)}, u32[]{:S(2)}) copy-start(f32[12,225]{1,0:T(8,128)} %param.17) | copy-start | bytes 32404
  42.2 12.6 %collective-permute-start.2 = (bf16[3,32,128]{2,1,0:T(8,128)(2,1)S(1)}, bf16[3,32,128]{2,1,0:T(8,128)(2,1)S(1)}, u32[]{:S(2)}, u32[]{:S(2)}) collective-permute-start(bf16[3,32,128]{2,1,0:T(8,128)(2,1)S(1)} %bitcast.86), channel_id=1, source_target_pairs={{0,496},{16,0},{32,16},{48,32},{64,48},{80,64},{96,80},{112,96},{1... | collective-permute-start | bytes 73736 | tf_op jit(solution)/shard_map/ppermute | solution.py:231
  45.9 21.9 %collective-permute-start = (bf16[8,32,1024]{2,1,0:T(8,128)(2,1)S(1)}, bf16[8,32,1024]{2,1,0:T(8,128)(2,1)S(1)}, u32[]{:S(2)}, u32[]{:S(2)}) collective-permute-start(bf16[8,32,1024]{2,1,0:T(8,128)(2,1)S(1)} %bitcast.81), channel_id=1, source_target_pairs={{0,496},{16,0},{32,16},{48,32},{64,48},{80,64},{96,80},{112,96},{1... | collective-permute-start | bytes 1572872 | tf_op jit(solution)/shard_map/ppermute | solution.py:231
  54.9 9.1 %collective-permute-start.3 = (bf16[3,32,32]{2,1,0:T(8,128)(2,1)S(1)}, bf16[3,32,32]{2,1,0:T(8,128)(2,1)S(1)}, u32[]{:S(2)}, u32[]{:S(2)}) collective-permute-start(bf16[3,32,32]{2,1,0:T(8,128)(2,1)S(1)} %bitcast.84), channel_id=1, source_target_pairs={{0,14},{2,0},{4,2},{6,4},{8,6},{10,8},{12,10},{14,12},{1,15},{3,1}... | collective-permute-start | bytes 18440 | tf_op jit(solution)/shard_map/ppermute | solution.py:231
  62.7 4.5 %copy-start.12 = (f32[1024]{0:T(1024)S(1)}, f32[1024]{0:T(1024)}, u32[]{:S(2)}) copy-start(f32[1024]{0:T(1024)} %param.13) | copy-start | bytes 12292
  67.2 5.0 %copy-start.1 = (bf16[1,8,4,8,48]{4,3,1,2,0:T(8,128)(2,1)}, bf16[1,8,4,8,48]{4,3,1,2,0:T(8,128)(2,1)S(1)}, u32[]{:S(2)}) copy-start(bf16[1,8,4,8,48]{4,3,1,2,0:T(8,128)(2,1)S(1)} %copy.34) | copy-start | bytes 73732
  67.2 3.6 %copy-start.9 = (f32[1024]{0:T(1024)S(1)}, f32[1024]{0:T(1024)}, u32[]{:S(2)}) copy-start(f32[1024]{0:T(1024)} %param.14) | copy-start | bytes 12292
  68.1 6.1 %collective-permute-start.1 = (bf16[8,8,1024]{2,1,0:T(8,128)(2,1)S(1)}, bf16[8,8,1024]{2,1,0:T(8,128)(2,1)S(1)}, u32[]{:S(2)}, u32[]{:S(2)}) collective-permute-start(bf16[8,8,1024]{2,1,0:T(8,128)(2,1)S(1)} %slice.78), channel_id=1, source_target_pairs={{0,14},{2,0},{4,2},{6,4},{8,6},{10,8},{12,10},{14,12},{1,15},{3,1}... | collective-permute-start | bytes 393224 | tf_op jit(solution)/shard_map/ppermute | solution.py:231
  107.3 1.4 slice-start
  142.0 3.1 %copy-start.7 = (f32[8,1024]{1,0:T(8,128)S(1)}, f32[8,1024]{1,0:T(8,128)}, u32[]{:S(2)}) copy-start(f32[8,1024]{1,0:T(8,128)} %get-tuple-element.20) | copy-start | bytes 98308
  142.0 3.1 %copy-start.6 = (f32[8,1024]{1,0:T(8,128)S(1)}, f32[8,1024]{1,0:T(8,128)}, u32[]{:S(2)}) copy-start(f32[8,1024]{1,0:T(8,128)} %get-tuple-element.19) | copy-start | bytes 98308
  142.0 3.1 %copy-start.2 = (bf16[1,8,4,8,48]{4,3,1,2,0:T(8,128)(2,1)S(1)}, bf16[1,8,4,8,48]{4,3,1,2,0:T(8,128)(2,1)}, u32[]{:S(2)}) copy-start(bf16[1,8,4,8,48]{4,3,1,2,0:T(8,128)(2,1)} %copy-done.1) | copy-start | bytes 73732
  142.0 3.1 %copy-start.4 = (f32[48,1024]{1,0:T(8,128)S(1)}, f32[48,1024]{1,0:T(8,128)}, u32[]{:S(2)}) copy-start(f32[48,1024]{1,0:T(8,128)} %get-tuple-element.18) | copy-start | bytes 589828
  161.3 40.9 %all-to-all-start.2 = ((bf16[32,24,1024]{2,1,0:T(8,128)(2,1)}), bf16[32,24,1024]{2,1,0:T(8,128)(2,1)S(1)}, u32[]{:S(2)}, u32[]{:S(2)}) async-start(bf16[32,24,1024]{2,1,0:T(8,128)(2,1)} %bitcast.70), calls=%async_computation.2 | async-start | bytes 3145728 | tf_op jit(solution)/shard_map/all_to_all | solution.py:220
  225.5 18.4 %all-to-all-start.4 = ((f32[32,16,128]{2,1,0:T(8,128)}), f32[32,16,128]{2,1,0:T(8,128)S(1)}, u32[]{:S(2)}, u32[]{:S(2)}) async-start(f32[32,16,128]{2,1,0:T(8,128)} %broadcast_in_dim.23), calls=%async_computation.4 | async-start | bytes 524288 | tf_op jit(solution)/shard_map/all_to_all | solution.py:220
Sparse Core Ops, SparseCore 0:
  42.3 64.9 all-gather.1

commit v3 on v2

v3 whole, which is shorter than its diff:
```python
import jax
import jax.numpy as jnp
from jax import lax
from jax.experimental import pallas as pl
from jax.experimental.pallas import tpu as pltpu
from jax.sharding import Mesh, PartitionSpec as P

WIN = 8
PATCH = 4
CELLS = WIN * WIN
norm_epsilon = 1e-05

STEP = 256
PAIR = 128
HEAD = 64
LANES = 128
SCALE = HEAD ** (-0.5)
UNITS = ((0, 128, 256, 0, 2), (384, 448, 512, 128, 1))
QKV = 640


def dot_nn(a, b):
    return lax.dot_general(a, b, (((1,), (0,)), ((), ())), preferred_element_type=jnp.float32)


def dot_nt(a, b):
    return lax.dot_general(a, b, (((1,), (1,)), ((), ())), preferred_element_type=jnp.float32)


def dot_tn(a, b):
    return lax.dot_general(a, b, (((0,), (0,)), ((), ())), preferred_element_type=jnp.float32)


def half_masks(count):
    lane = lax.broadcasted_iota(jnp.int32, (PAIR, count * HEAD), 1)
    return [(lane // HEAD) == i for i in range(count)]


def choose(masks, parts):
    return parts[0] if len(parts) == 1 else jnp.where(masks[0], parts[0], parts[1])


def only(masks, i, x):
    return x if len(masks) == 1 else jnp.where(masks[i], x, jnp.zeros_like(x))


def forward_kernel(
    cot, patches, embed_w, embed_b, gain, weights, bias, lab_col, lab_row,
    proj_out, prob_out, xhat_out, inv_out, grad_out, att, grad_acc
):
    step = pl.program_id(0)
    tokens = dot_nn(patches[...], embed_w[...]) + embed_b[0:1, :]
    tokens = tokens.astype(jnp.bfloat16).astype(jnp.float32)
    centered = tokens - jnp.mean(tokens, axis=-1, keepdims=True)
    inv = lax.rsqrt(jnp.mean(centered * centered, axis=-1, keepdims=True) + norm_epsilon)
    xhat = centered * inv
    xhat_out[...] = xhat
    inv_out[...] = jnp.broadcast_to(inv, inv_out.shape)
    normed = (xhat * gain[0:1, :]).astype(jnp.bfloat16)
    proj_out[...] = dot_nn(normed, weights[:, :QKV]).astype(jnp.bfloat16)
    for pair in range(STEP // PAIR):
        rows = slice(pair * PAIR, (pair + 1) * PAIR)
        same = lab_col[rows, :] == lab_row[pair, 0:1, :]
        for q_at, k_at, v_at, at, count in UNITS:
            width = count * HEAD
            masks = half_masks(count)
            q = proj_out[rows, q_at : q_at + width]
            k = proj_out[rows, k_at : k_at + width]
            v = proj_out[rows, v_at : v_at + width]
            parts = []
            for i in range(count):
                head = at // HEAD + i
                scores = dot_nt(only(masks, i, q), k) * SCALE + bias[head]
                scores = jnp.where(same, scores, -1e30)
                peak = jnp.max(scores, axis=-1, keepdims=True)
                e = jnp.exp(scores - peak)
                prob = e / jnp.sum(e, axis=-1, keepdims=True)
                prob_out[pair, head] = prob
                parts.append(dot_nn(prob.astype(jnp.bfloat16), v))
            att[rows, at : at + width] = choose(masks, parts).astype(jnp.bfloat16)
    grad = dot_tn(att[...], cot[...])

    @pl.when(step == 0)
    def _():
        grad_acc[...] = grad

    @pl.when(step > 0)
    def _():
        grad_acc[...] += grad

    @pl.when(step == pl.num_programs(0) - 1)
    def _():
        grad_out[...] = grad_acc[...].astype(grad_out.dtype)


def backward_kernel(
    cot, patches, proj, prob_in, xhat, inv, gain, weights, wo,
    embed_out, bias_out, gain_out, table_out, datt, dproj, dn, branch
):
    step = pl.program_id(0)

    @pl.when(step == 0)
    def _():
        embed_out[...] = jnp.zeros_like(embed_out)
        bias_out[...] = jnp.zeros_like(bias_out)
        gain_out[...] = jnp.zeros_like(gain_out)
        table_out[...] = jnp.zeros_like(table_out)
        dproj[...] = jnp.zeros_like(dproj)

    datt[...] = dot_nt(cot[...], wo[...]).astype(jnp.bfloat16)
    for pair in range(STEP // PAIR):
        rows = slice(pair * PAIR, (pair + 1) * PAIR)
        for q_at, k_at, v_at, at, count in UNITS:
            width = count * HEAD
            masks = half_masks(count)
            q = proj[rows, q_at : q_at + width]
            k = proj[rows, k_at : k_at + width]
            v = proj[rows, v_at : v_at + width]
            d_out = datt[rows, at : at + width]
            qs, ks, vs = [], [], []
            for i in range(count):
                head = at // HEAD + i
                prob = prob_in[pair, head]
                d_prob = dot_nt(only(masks, i, d_out), v)
                vs.append(dot_tn(prob.astype(jnp.bfloat16), d_out))
                d_scores = prob * (d_prob - jnp.sum(prob * d_prob, axis=-1, keepdims=True))
                table_out[head] += d_scores
                low = d_scores.astype(jnp.bfloat16)
                qs.append(dot_nn(low, k))
                ks.append(dot_tn(low, q))
            dproj[rows, q_at : q_at + width] = (choose(masks, qs) * SCALE).astype(jnp.bfloat16)
            dproj[rows, k_at : k_at + width] = (choose(masks, ks) * SCALE).astype(jnp.bfloat16)
            dproj[rows, v_at : v_at + width] = choose(masks, vs).astype(jnp.bfloat16)
    dn[...] = dot_nt(dproj[...], weights[:, :QKV])
    chunk = 16
    width = dn.shape[1]
    gain_row = gain[0:1, :]

    def rows_at(i, carry):
        bias_sum, gain_sum = carry
        rows = pl.ds(pl.multiple_of(i * chunk, chunk), chunk)
        d, x = dn[rows, :], xhat[rows, :]
        gain_sum = gain_sum + (d * x).reshape(chunk // 8, 8, width).sum(axis=0)
        g = d * gain_row
        mean = jnp.mean(g, axis=-1, keepdims=True)
        along = jnp.mean(g * x, axis=-1, keepdims=True)
        out = (inv[rows, 0:1] * (g - mean - x * along)).astype(jnp.bfloat16)
        branch[rows, :] = out
        bias_sum = bias_sum + out.astype(jnp.float32).reshape(chunk // 8, 8, width).sum(axis=0)
        return bias_sum, gain_sum

    zero = jnp.zeros((8, width), jnp.float32)
    bias_sum, gain_sum = lax.fori_loop(0, STEP // chunk, rows_at, (zero, zero))
    bias_out[...] += bias_sum
    gain_out[...] += gain_sum
    embed_out[...] += dot_tn(patches[...], branch[...])


def stepped(shape, lead=False):
    rest = len(shape) - 1
    return pl.BlockSpec(shape, lambda i: (i,) + (0,) * rest)


def whole(shape, index=None):
    index = index or (0,) * len(shape)
    return pl.BlockSpec(shape, lambda i: index)


def params():
    return pltpu.CompilerParams(
        dimension_semantics=("arbitrary",), vmem_limit_bytes=56 * 1024 * 1024
    )


def run_forward(joined, embed_w, embed_b, gain, weights, bias, lab_col, lab_row):
    cells, width = joined.shape[0], gain.shape[1]
    heads = bias.shape[0]
    features = heads * HEAD
    f32, bf16 = jnp.float32, jnp.bfloat16
    return pl.pallas_call(
        forward_kernel,
        grid=(cells // STEP,),
        in_specs=[
            stepped((STEP, width)),
            pl.BlockSpec((STEP, LANES), lambda i: (i, width // LANES)),
            whole((LANES, width)), whole((8, width)), whole((8, width)), whole(weights.shape),
            whole((heads, PAIR, PAIR)), stepped((STEP, PAIR)), stepped((STEP // PAIR, 8, PAIR)),
        ],
        out_specs=[
            stepped((STEP, QKV)), stepped((STEP // PAIR, heads, PAIR, PAIR)),
            stepped((STEP, width)), stepped((STEP, LANES)), whole((features, width)),
        ],
        out_shape=[
            jax.ShapeDtypeStruct((cells, QKV), bf16),
            jax.ShapeDtypeStruct((cells // PAIR, heads, PAIR, PAIR), f32),
            jax.ShapeDtypeStruct((cells, width), f32),
            jax.ShapeDtypeStruct((cells, LANES), f32),
            jax.ShapeDtypeStruct((features, width), bf16),
        ],
        scratch_shapes=[pltpu.VMEM((STEP, features), bf16), pltpu.VMEM((features, width), f32)],
        compiler_params=params(), name="forward",
        cost_estimate=pl.CostEstimate(
            flops=2 * cells * width * (QKV + features + LANES), transcendentals=cells * heads * PAIR,
            bytes_accessed=cells * width * 8,
        ),
    )(joined, joined, embed_w, embed_b, gain, weights, bias, lab_col, lab_row)


def run_backward(joined, proj, prob, xhat, inv, gain, weights, wo):
    cells, width = xhat.shape
    features = wo.shape[0]
    heads = features // HEAD
    f32, bf16 = jnp.float32, jnp.bfloat16
    return pl.pallas_call(
        backward_kernel,
        grid=(cells // STEP,),
        in_specs=[
            stepped((STEP, width)),
            pl.BlockSpec((STEP, LANES), lambda i: (i, width // LANES)),
            stepped((STEP, QKV)), stepped((STEP // PAIR, heads, PAIR, PAIR)),
            stepped((STEP, width)), stepped((STEP, LANES)), whole((8, width)),
            whole(weights.shape), whole((features, width)),
        ],
        out_specs=[
            whole((LANES, width)), whole((8, width)), whole((8, width)),
            whole((heads, PAIR, PAIR)),
        ],
        out_shape=[
            jax.ShapeDtypeStruct((LANES, width), f32), jax.ShapeDtypeStruct((8, width), f32),
            jax.ShapeDtypeStruct((8, width), f32), jax.ShapeDtypeStruct((heads, PAIR, PAIR), f32),
        ],
        scratch_shapes=[
            pltpu.VMEM((STEP, features), bf16), pltpu.VMEM((STEP, QKV), bf16),
            pltpu.VMEM((STEP, width), f32), pltpu.VMEM((STEP, width), bf16),
        ],
        compiler_params=params(), name="backward",
        cost_estimate=pl.CostEstimate(
            flops=2 * cells * width * (QKV + features + LANES), transcendentals=0,
            bytes_accessed=cells * width * 8,
        ),
    )(joined, joined, proj, prob, xhat, inv, gain, weights, wo)


ROW = ("yl", "x", "core")
COL = ("col", "dp")
CHIP_ROW = ("x", "core")
FAR = ("yl", "col", "dp")


def exchange(blocks, axis):
    return lax.all_to_all(blocks, axis, split_axis=0, concat_axis=0, tiled=True)


def spread(line, axis):
    copies = jnp.broadcast_to(line[None], (lax.axis_size(axis), *line.shape))
    return exchange(copies, axis)


def from_behind(value, axis):
    count = lax.axis_size(axis)
    return lax.ppermute(value, axis, [(source, (source - 1) % count) for source in range(count)])


def swap(value, axis):
    count = lax.axis_size(axis)
    return lax.ppermute(value, axis, [(source, source ^ 1) for source in range(count)])


def make_patches(pixel_block):
    channels, pixel_rows, pixel_cols = pixel_block.shape
    grid_rows = pixel_rows // PATCH
    grid_cols = pixel_cols // PATCH
    shaped = pixel_block.reshape(channels, grid_rows, PATCH, grid_cols, PATCH)
    return shaped.transpose(1, 3, 0, 2, 4).reshape(grid_rows, grid_cols, channels * PATCH * PATCH)


def window_split(block):
    rows_all, cols_all, features = block.shape
    shaped = block.reshape(rows_all // WIN, WIN, cols_all // WIN, WIN, features)
    return shaped.transpose(0, 2, 1, 3, 4).reshape(-1, features)


def splice_after(own, borrowed, offset, dim):
    joined = jnp.concatenate([own, borrowed], dim)
    return lax.dynamic_slice_in_dim(joined, offset, own.shape[dim], dim)


def pack_out(rows):
    tall = rows[:16].reshape(16, 8, LANES).transpose(1, 0, 2).reshape(LANES, LANES)
    low = rows[16:].reshape(8, 8, LANES).transpose(1, 0, 2).reshape(64, 2, 64)
    return jnp.concatenate([low.transpose(1, 0, 2).reshape(LANES, 64), tall], axis=1)


def unpack_out(blocks):
    count = blocks.shape[0]
    tall = blocks[:, :, 64:].reshape(count, 8, 16, LANES).transpose(0, 2, 1, 3)
    low = blocks[:, :, :64].reshape(count, 2, 64, 64).transpose(0, 2, 1, 3)
    low = low.reshape(count, 8, 8, LANES).transpose(0, 2, 1, 3)
    return jnp.concatenate([tall, low], axis=1).reshape(count * 24, 8 * LANES)


def gather_weights(qkv_weight, out_weight, half, heads):
    line = jnp.concatenate([qkv_weight.reshape(-1), out_weight.reshape(-1)])
    lines = spread(line, FAR)
    split = qkv_weight.size
    bands = lax.axis_size("yl")
    cols = lines.shape[0] // bands
    rows_w, rows_o = qkv_weight.shape[0], out_weight.shape[0]
    qkv = lines[:, :split].reshape(bands, cols, *qkv_weight.shape).transpose(0, 2, 1, 3)
    qkv = qkv.reshape(bands * rows_w, 3, -1)
    out = lines[:, split:].reshape(bands, cols, *out_weight.shape).transpose(0, 2, 1, 3)
    out = out.reshape(bands, rows_o, -1)
    features = qkv.shape[2]
    mine = lax.dynamic_slice_in_dim(qkv, half * (features // 2), features // 2, 2)
    out = lax.dynamic_slice_in_dim(out, half * 2, 2, 0)
    group = features // 4
    blocks = []
    for core in range(2):
        part = mine[:, :, core * group : (core + 1) * group]
        pieces = [part[:, i, :LANES] for i in range(3)] + [part[:, i, LANES:] for i in range(3)]
        blocks.append(jnp.concatenate([*pieces, pack_out(out[core])], axis=1))
    both = jnp.stack(blocks)
    chips = lax.axis_size("x")
    sent = jnp.broadcast_to(both[None], (chips, *both.shape)).reshape(2 * chips, *both.shape[1:])
    arrived = exchange(sent, CHIP_ROW)
    wo = unpack_out(arrived[:, :, QKV - 64 :])
    weights = arrived.reshape(2 * chips, bands, rows_w, -1).transpose(1, 0, 2, 3)
    return weights.reshape(bands * 2 * chips * rows_w, -1), wo


def on_device(
    pixels,
    cotangent,
    embed_weight,
    embed_bias,
    layer_norm_gain,
    qkv_weight,
    out_weight,
    bias_table,
    rel_index,
    shifts,
):
    cotangent, pixels = cotangent[0], pixels[0]
    rows_dev, cols_dev, width = cotangent.shape
    all_heads, table_size = bias_table.shape
    heads = all_heads // 4
    grid_rows = rows_dev * lax.axis_size(ROW)
    grid_cols = cols_dev * lax.axis_size("col")
    row_shift, col_shift = shifts[0, 0], shifts[0, 1]
    row_at, col_at, core = lax.axis_index(ROW), lax.axis_index("col"), lax.axis_index("core")
    half = col_at % 2
    group = 2 * half + core

    with jax.named_scope("weights"):
        weights, wo = gather_weights(qkv_weight, out_weight, half, heads)

    depth = embed_weight.shape[0]
    patches = make_patches(pixels)
    patches = jnp.pad(patches, ((0, 0), (0, 0), (0, LANES - depth)))
    block = jnp.concatenate([cotangent, patches], axis=-1)
    block = splice_after(block, from_behind(block[: WIN - 1], ROW), row_shift, 0)
    block = splice_after(block, from_behind(block[:, :WIN], "col"), col_shift, 1)
    own = window_split(block)
    two = jnp.concatenate([own, swap(own, "col")])
    joined = jnp.concatenate([two, swap(two, "core")])
    cells = joined.shape[0]

    labels = []
    for row_flip, col_flip in ((0, 0), (0, 1), (1, 0), (1, 1)):
        row_ids = (row_at ^ row_flip) * rows_dev + jnp.arange(rows_dev, dtype=jnp.int32)
        col_ids = (col_at ^ col_flip) * cols_dev + jnp.arange(cols_dev, dtype=jnp.int32)
        row_part = (row_ids >= grid_rows - row_shift).astype(jnp.int32)
        col_part = (col_ids >= grid_cols - col_shift).astype(jnp.int32)
        region = 2 * row_part[:, None] + col_part[None, :]
        labels.append(window_split(region[:, :, None])[:, 0])
    label = jnp.concatenate(labels) + 4 * (jnp.arange(cells, dtype=jnp.int32) // CELLS)
    lab_col = jnp.broadcast_to(label[:, None], (cells, PAIR))
    lab_row = jnp.broadcast_to(label.reshape(-1, 1, PAIR), (cells // PAIR, 8, PAIR))
    selector = (
        rel_index.reshape(-1)[:, None] == jnp.arange(table_size, dtype=jnp.int32)[None, :]
    ).astype(jnp.float32)
    my_table = lax.dynamic_slice_in_dim(bias_table, group * heads, heads, 0)
    bias = jnp.dot(selector, my_table.T, precision=lax.Precision.HIGHEST).T
    bias = jnp.tile(bias.reshape(heads, CELLS, CELLS), (1, 2, 2))
    embed_w = jnp.pad(embed_weight, ((0, LANES - depth), (0, 0)))
    embed_b = jnp.broadcast_to(embed_bias[None], (8, width))
    gain = jnp.broadcast_to(layer_norm_gain[None], (8, width))
    contract = (((0,), (0,)), ((), ()))
    cot_own, patches_own = own[:, :width], own[:, width:]
    embed_cot = lax.dot_general(patches_own, cot_own, contract, preferred_element_type=jnp.float32)
    bias_cot = jnp.sum(cot_own, axis=0, dtype=jnp.float32)

    proj, prob, xhat, inv, out_grad = run_forward(
        joined, embed_w, embed_b, gain, weights, bias, lab_col, lab_row
    )
    with jax.named_scope("outgrad"):
        count = lax.axis_size(CHIP_ROW)
        arrived = exchange(out_grad.reshape(count, -1, width), CHIP_ROW)
        by_core = arrived.reshape(count // 2, 2, -1, width).astype(jnp.float32).sum(axis=0)
        held = by_core.astype(jnp.bfloat16)
        none = jnp.zeros_like(held)
        bands = [jnp.where(half == i, held, none) for i in range(2)]
        partial_rows = exchange(jnp.concatenate(bands), "yl").astype(jnp.float32).sum(axis=0)
    embed_part, bias_part, gain_part, table_part = run_backward(
        joined, proj, prob, xhat, inv, gain, weights, wo
    )
    embed_grad = (embed_part + embed_cot)[:depth]
    bias_grad = bias_part.sum(axis=0) + bias_cot
    gain_grad = gain_part.sum(axis=0)
    table_part = table_part[:, :CELLS, :CELLS] + table_part[:, CELLS:, CELLS:]
    my_grad = jnp.dot(table_part.reshape(heads, -1), selector, precision=lax.Precision.HIGHEST)
    table_grad = lax.dynamic_update_slice_in_dim(
        jnp.zeros((all_heads, table_size), jnp.float32), my_grad, group * heads, 0
    )

    pieces = [embed_grad.reshape(-1), bias_grad, gain_grad, table_grad.reshape(-1)]
    line = jnp.concatenate(pieces)
    row_count = lax.axis_size(ROW)
    piece = -(-line.size // (row_count * 2048)) * 2048
    line = jnp.pad(line, (0, row_count * piece - line.size)).astype(jnp.bfloat16)
    line = line.reshape(row_count, piece // LANES, LANES)
    mine = exchange(line, ROW).astype(jnp.float32).sum(axis=0).reshape(-1)
    count = lax.axis_size(COL)
    col_blocks = partial_rows.reshape(partial_rows.shape[0], count, -1).transpose(1, 0, 2)
    block_shape = col_blocks.shape
    col_blocks = col_blocks.reshape(count, -1).astype(jnp.bfloat16)
    own = jnp.broadcast_to(mine[None].astype(jnp.bfloat16), (count, piece))
    both = exchange(jnp.concatenate([own, col_blocks], axis=1), COL)
    both = both.astype(jnp.float32).sum(axis=0)
    out_weight_grad = both[piece:].reshape(block_shape[1:])
    total = both[:piece].astype(jnp.bfloat16).reshape(piece // LANES, LANES)
    total = spread(total, ROW).reshape(-1).astype(jnp.float32)
    results, at = ([], 0)
    for a, shape in zip(pieces, (embed_grad.shape, (width,), (width,), table_grad.shape)):
        results.append(total[at : at + a.size].reshape(shape))
        at += a.size
    return (out_weight_grad, *results)


def solution(mesh):
    sizes = mesh.devices.shape
    names = ("yl", "x", "core", "col", "dp")
    fine = Mesh(mesh.devices.reshape(-1, 4, 2, *sizes[1:]), names)
    return jax.shard_map(
        on_device,
        mesh=fine,
        in_specs=(
            P("dp", None, ROW, "col"),
            P("dp", ROW, "col", None),
            P(),
            P(),
            P(),
            P(ROW, COL),
            P(ROW, COL),
            P(),
            P(),
            P("dp", None),
        ),
        out_specs=(P(ROW, COL), P(), P(), P(), P()),
        check_vma=False,
    )
```

time: 254 us -> 238 us (0.937)
  blocking collectives: 66 us -> 18.6 us
  starting transfers between devices: 22.8 us -> 56.2 us
  waiting for transfers between devices: 81 us -> 63.8 us
  between operations: 21.1 us -> 6.61 us
  other arithmetic: 7.19 us -> 18.3 us
  Pallas kernels: 28.4 us -> 38.2 us
  local copies, waits for them, and re-layouts: 21.7 us -> 30.8 us
    all_to_all x3 -> x1, blocking collectives: 66 us -> 18.6 us  [exchange(): return lax.all_to_all(blocks, axis, split_axis=0, concat_axis=0, tiled=True)]
    all_gather x1 -> x0, waiting for transfers between devices: 31.6 us -> none  [on_device(): lax.all_gather(jnp.concatenate([qkv_rows.reshape(rows_w, -1), out_rows.re...]
    all_to_all x2 -> x6, starting transfers between devices: 11.2 us -> 37.3 us  [exchange(): return lax.all_to_all(blocks, axis, split_axis=0, concat_axis=0, tiled=True)]
    ppermute x4, waiting for transfers between devices: 2.02 us -> 24.9 us  [the longest x2 13.7 us: from_behind(): lax.ppermute(value, axis, [(source, (source - 1) % count) for source in r...]
    all_to_all x2 -> x6, waiting for transfers between devices: 47.3 us -> 38.9 us  [exchange(): return lax.all_to_all(blocks, axis, split_axis=0, concat_axis=0, tiled=True)]
    ppermute x4, starting transfers between devices: 11.6 us -> 19 us  [the longest x2 12.9 us: from_behind(): lax.ppermute(value, axis, [(source, (source - 1) % count) for source in r...]
    pallas_call x1, Pallas kernels: 15.1 us -> 22.5 us  [run_backward(): pl.pallas_call(backward_kernel, grid=(cells // STEP,), in_specs=[stepped(...]
    concatenate x3 -> x6, other arithmetic: 0.72 us -> 5.63 us  [the longest x1 2.91 us: on_device(): joined = jnp.concatenate([two, swap(two, 'core')])]
  transfers between devices with their start and end apart: 7 -> 10, of which waited for: 4 -> 7; matrix products, arithmetic and copies ran while one was open for 5% -> 15% of each run, Pallas kernels for 0% -> 0%
where the time goes in v3:
time: 238 us; the launch traced here: 236 us
  waiting for transfers between devices  63.8 us (27%)
  starting transfers between devices  56.2 us (24%)
  Pallas kernels  38.2 us (16%)
  local copies, waits for them, and re-layouts  30.8 us (13%)
  blocking collectives  18.6 us (8%)
  other arithmetic  18.3 us (8%)
  between operations  6.61 us (3%)
  matrix products  3.83 us (2%)
    all_to_all x6, waiting for transfers between devices, exchange(): return lax.all_to_all(blocks, axis, split_axis=0, concat_axis=0, tiled=True)  38.9 us
    all_to_all x6, starting transfers between devices, exchange(): return lax.all_to_all(blocks, axis, split_axis=0, concat_axis=0, tiled=True)  37.3 us
    pallas_call x1, Pallas kernels, run_backward(): pl.pallas_call(backward_kernel, grid=(cells // STEP,), in_specs=[stepped(...  22.5 us
    all_to_all x1, blocking collectives, exchange(): return lax.all_to_all(blocks, axis, split_axis=0, concat_axis=0, tiled=True)  18.6 us
    pallas_call x1, Pallas kernels, run_forward(): pl.pallas_call(forward_kernel, grid=(cells // STEP,), in_specs=[stepped((...  15.7 us
    ppermute x2, waiting for transfers between devices, from_behind(): lax.ppermute(value, axis, [(source, (source - 1) % count) for source in r...  13.7 us
    ppermute x2, starting transfers between devices, from_behind(): lax.ppermute(value, axis, [(source, (source - 1) % count) for source in r...  12.9 us
    ppermute x2, waiting for transfers between devices, swap(): lax.ppermute(value, axis, [(source, source ^ 1) for source in range(count)])  11.2 us
  transfers between devices with their start and end apart: 10, of which 7 were waited for; matrix products, arithmetic and copies ran while one was open for 15% of the time, Pallas kernels for 0%

profile of v3, /device:TPU:1, one launch (start us, length us, event | category | flops | bytes accessed | tf_op | source)
XLA Modules:
  0.0 236.5 jit_solution(11041227269545840431)
XLA Ops:
  0.7 2.5 %reshape_squeeze.3 = bf16[3,8,4,32,4]{4,3,2,1,0:T(8,128)(2,1)S(1)} reshape(bf16[1,3,32,128]{3,2,1,0:T(8,128)(2,1)} %param.10) | data formatting | bytes 49152 | tf_op jit(solution)/shard_map/reshape;squeeze | solution.py:273
  3.2 0.7 copy.222
  4.0 0.8 pad_maximum_fusion.2
  4.8 8.7 %collective-permute-start = (bf16[7,32,1152]{2,1,0:T(8,128)(2,1)}, bf16[7,32,1152]{2,1,0:T(8,128)(2,1)}, u32[]{:S(2)}, u32[]{:S(2)}) collective-permute-start(bf16[7,32,1152]{2,1,0:T(8,128)(2,1)} %pad_maximum_fusion.2), channel_id=1, source_target_pairs={{0,496},{16,0},{32,16},{48,32},{64,48},{80,64},{96,80},{112,96},{1... | collective-permute-start | bytes 1548296 | tf_op jit(solution)/shard_map/ppermute | solution.py:261
  13.8 0.8 broadcast_in_dim.22
  15.1 5.4 %reduce.4 = bf16[64,6144]{1,0:T(8,128)(2,1)S(1)} reduce(bf16[64,1,6144]{2,1,0:T(2,128)(2,1)S(1)} %broadcast_in_dim.22, bf16[]{:T(256)} %broadcast.307), dimensions={1}, to_apply=%broadcast_in_dim.22.reduce_sub_computation | reduce | bytes 1572866 | tf_op jit(solution)/shard_map/weights/broadcast_in_dim | solution.py:255
  20.5 1.4 reshape.424
  22.0 11.0 %all-to-all-start = ((bf16[64,2,3072]{2,1,0:T(2,128)(2,1)}), bf16[64,2,3072]{2,1,0:T(2,128)(2,1)S(1)}, u32[]{:S(2)}, u32[]{:S(2)}) async-start(bf16[64,2,3072]{2,1,0:T(2,128)(2,1)} %reshape.424), calls=%async_computation | async-start | bytes 1572864 | tf_op jit(solution)/shard_map/weights/all_to_all | solution.py:251
  35.5 1.3 fusion.7
  36.8 4.1 %collective-permute-start.1 = (bf16[8,8,1152]{2,1,0:T(8,128)(2,1)S(1)}, bf16[8,8,1152]{2,1,0:T(8,128)(2,1)S(1)}, u32[]{:S(2)}, u32[]{:S(2)}) collective-permute-start(bf16[8,8,1152]{2,1,0:T(8,128)(2,1)S(1)} %slice.193), channel_id=1, source_target_pairs={{0,14},{2,0},{4,2},{6,4},{8,6},{10,8},{12,10},{14,12},{1,15},{3,1}... | collective-permute-start | bytes 442376 | tf_op jit(solution)/shard_map/ppermute | solution.py:261
  42.9 13.7 %collective-permute-done.1 = bf16[8,8,1152]{2,1,0:T(8,128)(2,1)S(1)} collective-permute-done((bf16[8,8,1152]{2,1,0:T(8,128)(2,1)S(1)}, bf16[8,8,1152]{2,1,0:T(8,128)(2,1)S(1)}, u32[]{:S(2)}, u32[]{:S(2)}) %collective-permute-start.1) | collective-permute-done | bytes 147488 | tf_op jit(solution)/shard_map/ppermute | solution.py:261
  57.0 2.7 %collective-permute-start.2 = (bf16[256,1152]{1,0:T(8,128)(2,1)S(1)}, bf16[256,1152]{1,0:T(8,128)(2,1)S(1)}, u32[]{:S(2)}, u32[]{:S(2)}) collective-permute-start(bf16[256,1152]{1,0:T(8,128)(2,1)S(1)} %bitcast.156), channel_id=1, source_target_pairs={{0,2},{2,0},{4,6},{6,4},{8,10},{10,8},{12,14},{14,12},{1,3},{3,1},... | collective-permute-start | bytes 1769480 | tf_op jit(solution)/shard_map/ppermute | solution.py:266
  62.1 11.2 %collective-permute-done.2 = bf16[256,1152]{1,0:T(8,128)(2,1)S(1)} collective-permute-done((bf16[256,1152]{1,0:T(8,128)(2,1)S(1)}, bf16[256,1152]{1,0:T(8,128)(2,1)S(1)}, u32[]{:S(2)}, u32[]{:S(2)}) %collective-permute-start.2) | collective-permute-done | bytes 589856 | tf_op jit(solution)/shard_map/ppermute | solution.py:266
  73.3 1.1 pad_maximum_fusion.1
  74.4 3.4 %collective-permute-start.3 = (bf16[512,1152]{1,0:T(8,128)(2,1)}, bf16[512,1152]{1,0:T(8,128)(2,1)}, u32[]{:S(2)}, u32[]{:S(2)}) collective-permute-start(bf16[512,1152]{1,0:T(8,128)(2,1)} %pad_maximum_fusion.1), channel_id=1, source_target_pairs={{0,16},{16,0},{1,17},{17,1},{2,18},{18,2},{3,19},{19,3},{4,20},{20... | collective-permute-start | bytes 3538952 | tf_op jit(solution)/shard_map/ppermute | solution.py:266
  82.3 1.8 reshape.392
  84.7 1.8 reshape.393
  88.3 1.3 broadcast_in_dim.23
  89.7 4.4 %all-to-all-start.1 = ((bf16[8,128,768]{2,1,0:T(8,128)(2,1)}), bf16[8,128,768]{2,1,0:T(8,128)(2,1)S(1)}, u32[]{:S(2)}, u32[]{:S(2)}) async-start(bf16[8,128,768]{2,1,0:T(8,128)(2,1)} %bitcast.164), calls=%async_computation.1 | async-start | bytes 3145728 | tf_op jit(solution)/shard_map/weights/all_to_all | solution.py:251
  94.9 2.2 fusion.1
  97.3 0.7 pad.14.embed_w
  98.1 0.9 tile.12.bias
  99.4 2.9 %pad_maximum_fusion.cot.patches = bf16[1024,1152]{1,0:T(8,128)(2,1)} fusion(bf16[512,1152]{1,0:T(8,128)(2,1)} %collective-permute-done.3, bf16[256,1152]{1,0:T(8,128)(2,1)S(1)} %collective-permute-done.2, bf16[256,1152]{1,0:T(8,128)(2,1)S(1)} %bitcast.160), kind=kLoop, calls=%fused_computation.3 | loop fusion | flops 7077888 | bytes 4718592 | tf_op jit(solution)/shard_map/concatenate | solution.py:365
  102.3 12.3 %all-to-all-done.1 = bf16[8,128,768]{2,1,0:T(8,128)(2,1)S(1)} async-done(((bf16[8,128,768]{2,1,0:T(8,128)(2,1)}), bf16[8,128,768]{2,1,0:T(8,128)(2,1)S(1)}, u32[]{:S(2)}, u32[]{:S(2)}) %all-to-all-start.1) | async-done | bytes 1572896 | tf_op jit(solution)/shard_map/weights/all_to_all | solution.py:251
  115.4 0.8 copy.285
  116.2 1.3 copy.243
  119.3 1.0 broadcast_in_dim.24.lab_col
  120.3 15.7 %forward.1 = (bf16[1024,640]{1,0:T(8,128)(2,1)}, f32[8,3,128,128]{3,2,1,0:T(8,128)}, f32[1024,1024]{1,0:T(8,128)}, f32[1024,128]{1,0:T(8,128)}, bf16[192,1024]{1,0:T(8,128)(2,1)}) custom-call(bf16[1024,1152]{1,0:T(8,128)(2,1)} %pad_maximum_fusion.cot.patches, bf16[1024,1152]{1,0:T(8,128)(2,1)} %pad_maximum_fusion.cot.patches, ...), custom_call_target="tpu_custom_call" | custom-call | flops 2013265920 | bytes 8388608 | tf_op jit(solution)/shard_map/forward/pallas_call | solution.py:180
  136.1 22.5 %backward.1 = (f32[128,1024]{1,0:T(8,128)}, f32[8,1024]{1,0:T(8,128)}, f32[8,1024]{1,0:T(8,128)}, f32[3,128,128]{2,1,0:T(8,128)}) custom-call(bf16[1024,1152]{1,0:T(8,128)(2,1)} %pad_maximum_fusion.cot.patches, bf16[1024,1152]{1,0:T(8,128)(2,1)} %pad_maximum_fusion.cot.patches, bf16[1024,640]{1,0:T(8,128)(2,1)} %get-tuple-element.14.proj, ...), custom_call_target="tpu_custom_call" | custom-call | flops 2013265920 | bytes 8388608 | tf_op jit(solution)/shard_map/backward/pallas_call | solution.py:214
  158.6 1.0 fusion.18
  159.6 0.8 reduce_sum.74
  160.4 0.8 reduce_sum.72
  161.1 4.3 %all-to-all-start.3 = ((bf16[8,24,1024]{2,1,0:T(8,128)(2,1)}), bf16[8,24,1024]{2,1,0:T(8,128)(2,1)S(1)}, u32[]{:S(2)}, u32[]{:S(2)}) async-start(bf16[8,24,1024]{2,1,0:T(8,128)(2,1)} %bitcast.51), calls=%async_computation.3 | async-start | bytes 786432 | tf_op jit(solution)/shard_map/outgrad/all_to_all | solution.py:251
  165.7 1.4 fusion
  168.0 5.2 %all-to-all-done.3 = bf16[8,24,1024]{2,1,0:T(8,128)(2,1)S(1)} async-done(((bf16[8,24,1024]{2,1,0:T(8,128)(2,1)}), bf16[8,24,1024]{2,1,0:T(8,128)(2,1)S(1)}, u32[]{:S(2)}, u32[]{:S(2)}) %all-to-all-start.3) | async-done | bytes 393248 | tf_op jit(solution)/shard_map/outgrad/all_to_all | solution.py:251
  173.2 6.7 %all-to-all-start.2 = ((bf16[32,16,128]{2,1,0:T(8,128)(2,1)}), bf16[32,16,128]{2,1,0:T(8,128)(2,1)S(1)}, u32[]{:S(2)}, u32[]{:S(2)}) async-start(bf16[32,16,128]{2,1,0:T(8,128)(2,1)} %bitcast.49), calls=%async_computation.2 | async-start | bytes 262144 | tf_op jit(solution)/shard_map/all_to_all | solution.py:251
  180.0 0.7 pad_maximum_fusion.5
  180.7 7.7 %all-to-all-done.2 = bf16[32,16,128]{2,1,0:T(8,128)(2,1)S(1)} async-done(((bf16[32,16,128]{2,1,0:T(8,128)(2,1)}), bf16[32,16,128]{2,1,0:T(8,128)(2,1)S(1)}, u32[]{:S(2)}, u32[]{:S(2)}) %all-to-all-start.2) | async-done | bytes 131104 | tf_op jit(solution)/shard_map/all_to_all | solution.py:251
  188.4 3.4 %all-to-all-start.4 = ((bf16[4,24,1024]{2,1,0:T(8,128)(2,1)}), bf16[4,24,1024]{2,1,0:T(8,128)(2,1)S(1)}, u32[]{:S(2)}, u32[]{:S(2)}) async-start(bf16[4,24,1024]{2,1,0:T(8,128)(2,1)} %pad_maximum_fusion.5), calls=%async_computation.4 | async-start | bytes 393216 | tf_op jit(solution)/shard_map/outgrad/all_to_all | solution.py:251
  191.9 5.8 %all-to-all-done.4 = bf16[4,24,1024]{2,1,0:T(8,128)(2,1)S(1)} async-done(((bf16[4,24,1024]{2,1,0:T(8,128)(2,1)}), bf16[4,24,1024]{2,1,0:T(8,128)(2,1)S(1)}, u32[]{:S(2)}, u32[]{:S(2)}) %all-to-all-start.4) | async-done | bytes 196640 | tf_op jit(solution)/shard_map/outgrad/all_to_all | solution.py:251
  198.0 0.7 reduce.5
  198.8 18.6 %all_to_all.43 = bf16[16,2,1792]{2,1,0:T(2,128)(2,1)S(1)} all-to-all(bf16[16,2,1792]{2,1,0:T(2,128)(2,1)S(1)} %reshape.426), channel_id=1, replica_groups=mesh['yl'=4,'x'=4,'core'=2,'col'=8,'dp'=2] {'col','dp'}, dimensions={0} | all-to-all | bytes 229376 | tf_op jit(solution)/shard_map/all_to_all | solution.py:251
  217.7 0.7 broadcast_in_dim.29
  218.3 7.5 %all-to-all-start.6 = ((bf16[32,16,128]{2,1,0:T(8,128)(2,1)}), bf16[32,16,128]{2,1,0:T(8,128)(2,1)S(1)}, u32[]{:S(2)}, u32[]{:S(2)}) async-start(bf16[32,16,128]{2,1,0:T(8,128)(2,1)} %broadcast_in_dim.29), calls=%async_computation.6 | async-start | bytes 262144 | tf_op jit(solution)/shard_map/all_to_all | solution.py:251
  225.9 0.7 reshape.419
  226.6 7.9 %all-to-all-done.6 = bf16[32,16,128]{2,1,0:T(8,128)(2,1)S(1)} async-done(((bf16[32,16,128]{2,1,0:T(8,128)(2,1)}), bf16[32,16,128]{2,1,0:T(8,128)(2,1)S(1)}, u32[]{:S(2)}, u32[]{:S(2)}) %all-to-all-start.6) | async-done | bytes 131104 | tf_op jit(solution)/shard_map/all_to_all | solution.py:251
  235.1 0.7 reshape.420
  235.8 0.7 reshape.421
  (130 shorter events, 16.1 us)
Async XLA Ops:
  0.6 94.3 %copy-start = (f32[12,225]{1,0:T(8,128)S(1)}, f32[12,225]{1,0:T(8,128)}, u32[]{:S(2)}) copy-start(f32[12,225]{1,0:T(8,128)} %param.17) | copy-start | bytes 32404
  0.6 3.3 %copy-start.1 = (bf16[1,8,32,1024]{3,2,1,0:T(8,128)(2,1)S(1)}, bf16[1,8,32,1024]{3,2,1,0:T(8,128)(2,1)}, u32[]{:S(2)}) copy-start(bf16[1,8,32,1024]{3,2,1,0:T(8,128)(2,1)} %param.11) | copy-start | bytes 1572868
  0.7 12.9 %copy-start.12 = (bf16[24,64]{1,0:T(8,128)(2,1)S(1)}, bf16[24,64]{1,0:T(8,128)(2,1)}, u32[]{:S(2)}) copy-start(bf16[24,64]{1,0:T(8,128)(2,1)} %param.16) | copy-start | bytes 9220
  0.7 13.0 %copy-start.9 = (bf16[32,144]{1,0:T(8,128)(2,1)S(1)}, bf16[32,144]{1,0:T(8,128)(2,1)}, u32[]{:S(2)}) copy-start(bf16[32,144]{1,0:T(8,128)(2,1)} %param.15) | copy-start | bytes 27652
  4.8 30.6 %collective-permute-start = (bf16[7,32,1152]{2,1,0:T(8,128)(2,1)}, bf16[7,32,1152]{2,1,0:T(8,128)(2,1)}, u32[]{:S(2)}, u32[]{:S(2)}) collective-permute-start(bf16[7,32,1152]{2,1,0:T(8,128)(2,1)} %pad_maximum_fusion.2), channel_id=1, source_target_pairs={{0,496},{16,0},{32,16},{48,32},{64,48},{80,64},{96,80},{112,96},{1... | collective-permute-start | bytes 1548296 | tf_op jit(solution)/shard_map/ppermute | solution.py:261
  20.5 12.4 %copy-start.17 = (s32[1,2]{1,0:T(1,128)S(1)}, s32[1,2]{1,0:T(1,128)}, u32[]{:S(2)}) copy-start(s32[1,2]{1,0:T(1,128)} %param.19) | copy-start | bytes 28
  22.0 55.9 %all-to-all-start = ((bf16[64,2,3072]{2,1,0:T(2,128)(2,1)}), bf16[64,2,3072]{2,1,0:T(2,128)(2,1)S(1)}, u32[]{:S(2)}, u32[]{:S(2)}) async-start(bf16[64,2,3072]{2,1,0:T(2,128)(2,1)} %reshape.424), calls=%async_computation | async-start | bytes 1572864 | tf_op jit(solution)/shard_map/weights/all_to_all | solution.py:251
  36.8 19.8 %collective-permute-start.1 = (bf16[8,8,1152]{2,1,0:T(8,128)(2,1)S(1)}, bf16[8,8,1152]{2,1,0:T(8,128)(2,1)S(1)}, u32[]{:S(2)}, u32[]{:S(2)}) collective-permute-start(bf16[8,8,1152]{2,1,0:T(8,128)(2,1)S(1)} %slice.193), channel_id=1, source_target_pairs={{0,14},{2,0},{4,2},{6,4},{8,6},{10,8},{12,10},{14,12},{1,15},{3,1}... | collective-permute-start | bytes 442376 | tf_op jit(solution)/shard_map/ppermute | solution.py:261
  57.0 16.3 %collective-permute-start.2 = (bf16[256,1152]{1,0:T(8,128)(2,1)S(1)}, bf16[256,1152]{1,0:T(8,128)(2,1)S(1)}, u32[]{:S(2)}, u32[]{:S(2)}) collective-permute-start(bf16[256,1152]{1,0:T(8,128)(2,1)S(1)} %bitcast.156), channel_id=1, source_target_pairs={{0,2},{2,0},{4,6},{6,4},{8,10},{10,8},{12,14},{14,12},{1,3},{3,1},... | collective-permute-start | bytes 1769480 | tf_op jit(solution)/shard_map/ppermute | solution.py:266
  74.4 25.0 %collective-permute-start.3 = (bf16[512,1152]{1,0:T(8,128)(2,1)}, bf16[512,1152]{1,0:T(8,128)(2,1)}, u32[]{:S(2)}, u32[]{:S(2)}) collective-permute-start(bf16[512,1152]{1,0:T(8,128)(2,1)} %pad_maximum_fusion.1), channel_id=1, source_target_pairs={{0,16},{16,0},{1,17},{17,1},{2,18},{18,2},{3,19},{19,3},{4,20},{20... | collective-permute-start | bytes 3538952 | tf_op jit(solution)/shard_map/ppermute | solution.py:266
  86.6 1.4 copy-start.5
  86.6 1.4 copy-start.6
  86.6 1.5 copy-start.3
  86.6 1.5 copy-start.4
  89.6 4.4 %copy-start.10 = (s32[4,8]{1,0:T(4,128)S(1)}, s32[4,8]{1,0:T(4,128)}, u32[]{:S(2)}) copy-start(s32[4,8]{1,0:T(4,128)} %get-tuple-element.65) | copy-start | bytes 388
  89.6 4.4 %copy-start.11 = (s32[4,8]{1,0:T(4,128)S(1)}, s32[4,8]{1,0:T(4,128)}, u32[]{:S(2)}) copy-start(s32[4,8]{1,0:T(4,128)} %get-tuple-element.66) | copy-start | bytes 388
  89.6 4.4 %copy-start.15 = (s32[8]{0:T(128)S(1)}, s32[8]{0:T(128)}, u32[]{:S(2)}) copy-start(s32[8]{0:T(128)} %get-tuple-element.51) | copy-start | bytes 100
  89.6 4.4 %copy-start.16 = (s32[8]{0:T(128)S(1)}, s32[8]{0:T(128)}, u32[]{:S(2)}) copy-start(s32[8]{0:T(128)} %get-tuple-element.52) | copy-start | bytes 100
  89.6 5.2 %copy-start.8 = (s32[64,64]{1,0:T(8,128)S(1)}, s32[64,64]{1,0:T(8,128)}, u32[]{:S(2)}) copy-start(s32[64,64]{1,0:T(8,128)} %param.18) | copy-start | bytes 49156
  89.6 7.6 %copy-start.7 = (bf16[48,1024]{1,0:T(8,128)(2,1)S(1)}, bf16[48,1024]{1,0:T(8,128)(2,1)}, u32[]{:S(2)}) copy-start(bf16[48,1024]{1,0:T(8,128)(2,1)} %param.12) | copy-start | bytes 294916
  89.7 25.0 %all-to-all-start.1 = ((bf16[8,128,768]{2,1,0:T(8,128)(2,1)}), bf16[8,128,768]{2,1,0:T(8,128)(2,1)S(1)}, u32[]{:S(2)}, u32[]{:S(2)}) async-start(bf16[8,128,768]{2,1,0:T(8,128)(2,1)} %bitcast.164), calls=%async_computation.1 | async-start | bytes 3145728 | tf_op jit(solution)/shard_map/weights/all_to_all | solution.py:251
  116.2 1.3 copy-start.13
  116.2 1.9 copy-start.14
  158.6 6.9 %copy-start.2 = (f32[3,128,128]{2,1,0:T(8,128)S(1)}, f32[3,128,128]{2,1,0:T(8,128)}, u32[]{:S(2)}) copy-start(f32[3,128,128]{2,1,0:T(8,128)} %get-tuple-element.21) | copy-start | bytes 589828
  161.1 12.1 %all-to-all-start.3 = ((bf16[8,24,1024]{2,1,0:T(8,128)(2,1)}), bf16[8,24,1024]{2,1,0:T(8,128)(2,1)S(1)}, u32[]{:S(2)}, u32[]{:S(2)}) async-start(bf16[8,24,1024]{2,1,0:T(8,128)(2,1)} %bitcast.51), calls=%async_computation.3 | async-start | bytes 786432 | tf_op jit(solution)/shard_map/outgrad/all_to_all | solution.py:251
  173.2 15.2 %all-to-all-start.2 = ((bf16[32,16,128]{2,1,0:T(8,128)(2,1)}), bf16[32,16,128]{2,1,0:T(8,128)(2,1)S(1)}, u32[]{:S(2)}, u32[]{:S(2)}) async-start(bf16[32,16,128]{2,1,0:T(8,128)(2,1)} %bitcast.49), calls=%async_computation.2 | async-start | bytes 262144 | tf_op jit(solution)/shard_map/all_to_all | solution.py:251
  188.4 9.2 %all-to-all-start.4 = ((bf16[4,24,1024]{2,1,0:T(8,128)(2,1)}), bf16[4,24,1024]{2,1,0:T(8,128)(2,1)S(1)}, u32[]{:S(2)}, u32[]{:S(2)}) async-start(bf16[4,24,1024]{2,1,0:T(8,128)(2,1)} %pad_maximum_fusion.5), calls=%async_computation.4 | async-start | bytes 393216 | tf_op jit(solution)/shard_map/outgrad/all_to_all | solution.py:251
  218.3 16.1 %all-to-all-start.6 = ((bf16[32,16,128]{2,1,0:T(8,128)(2,1)}), bf16[32,16,128]{2,1,0:T(8,128)(2,1)S(1)}, u32[]{:S(2)}, u32[]{:S(2)}) async-start(bf16[32,16,128]{2,1,0:T(8,128)(2,1)} %broadcast_in_dim.29), calls=%async_computation.6 | async-start | bytes 262144 | tf_op jit(solution)/shard_map/all_to_all | solution.py:251

commit v4 on v3

--- a/solution.py
+++ b/solution.py
@@ -156,7 +156,7 @@
     embed_out[...] += dot_tn(patches[...], branch[...])
 
 
-def stepped(shape, lead=False):
+def stepped(shape):
     rest = len(shape) - 1
     return pl.BlockSpec(shape, lambda i: (i,) + (0,) * rest)
 
@@ -243,6 +243,8 @@
 
 ROW = ("yl", "x", "core")
 COL = ("col", "dp")
+PLANE = ("x", "core", "col")
+RING = ("yl", "dp")
 CHIP_ROW = ("x", "core")
 FAR = ("yl", "col", "dp")
 
@@ -299,10 +301,10 @@
     return jnp.concatenate([tall, low], axis=1).reshape(count * 24, 8 * LANES)
 
 
-def gather_weights(qkv_weight, out_weight, half, heads):
-    line = jnp.concatenate([qkv_weight.reshape(-1), out_weight.reshape(-1)])
+def gather_weights(qkv_weight, out_weight, half, own):
+    split = qkv_weight.size // LANES
+    line = jnp.concatenate([qkv_weight.reshape(-1, LANES), out_weight.reshape(-1, LANES)])
     lines = spread(line, FAR)
-    split = qkv_weight.size
     bands = lax.axis_size("yl")
     cols = lines.shape[0] // bands
     rows_w, rows_o = qkv_weight.shape[0], out_weight.shape[0]
@@ -322,10 +324,11 @@
     both = jnp.stack(blocks)
     chips = lax.axis_size("x")
     sent = jnp.broadcast_to(both[None], (chips, *both.shape)).reshape(2 * chips, *both.shape[1:])
+    sent, own = lax.optimization_barrier((sent, own))
     arrived = exchange(sent, CHIP_ROW)
     wo = unpack_out(arrived[:, :, QKV - 64 :])
     weights = arrived.reshape(2 * chips, bands, rows_w, -1).transpose(1, 0, 2, 3)
-    return weights.reshape(bands * 2 * chips * rows_w, -1), wo
+    return weights.reshape(bands * 2 * chips * rows_w, -1), wo, own
 
 
 def on_device(
@@ -351,16 +354,14 @@
     half = col_at % 2
     group = 2 * half + core
 
-    with jax.named_scope("weights"):
-        weights, wo = gather_weights(qkv_weight, out_weight, half, heads)
-
     depth = embed_weight.shape[0]
     patches = make_patches(pixels)
     patches = jnp.pad(patches, ((0, 0), (0, 0), (0, LANES - depth)))
     block = jnp.concatenate([cotangent, patches], axis=-1)
-    block = splice_after(block, from_behind(block[: WIN - 1], ROW), row_shift, 0)
+    below = from_behind(block[: WIN - 1], ROW)
+    block = splice_after(block, below, row_shift, 0)
     block = splice_after(block, from_behind(block[:, :WIN], "col"), col_shift, 1)
-    own = window_split(block)
+    weights, wo, own = gather_weights(qkv_weight, out_weight, half, window_split(block))
     two = jnp.concatenate([own, swap(own, "col")])
     joined = jnp.concatenate([two, swap(two, "core")])
     cells = joined.shape[0]
@@ -393,14 +394,8 @@
     proj, prob, xhat, inv, out_grad = run_forward(
         joined, embed_w, embed_b, gain, weights, bias, lab_col, lab_row
     )
-    with jax.named_scope("outgrad"):
-        count = lax.axis_size(CHIP_ROW)
-        arrived = exchange(out_grad.reshape(count, -1, width), CHIP_ROW)
-        by_core = arrived.reshape(count // 2, 2, -1, width).astype(jnp.float32).sum(axis=0)
-        held = by_core.astype(jnp.bfloat16)
-        none = jnp.zeros_like(held)
-        bands = [jnp.where(half == i, held, none) for i in range(2)]
-        partial_rows = exchange(jnp.concatenate(bands), "yl").astype(jnp.float32).sum(axis=0)
+    count = lax.axis_size(CHIP_ROW)
+    arrived = exchange(out_grad.reshape(count, -1, width), CHIP_ROW)
     embed_part, bias_part, gain_part, table_part = run_backward(
         joined, proj, prob, xhat, inv, gain, weights, wo
     )
@@ -415,21 +410,32 @@
 
     pieces = [embed_grad.reshape(-1), bias_grad, gain_grad, table_grad.reshape(-1)]
     line = jnp.concatenate(pieces)
-    row_count = lax.axis_size(ROW)
-    piece = -(-line.size // (row_count * 2048)) * 2048
-    line = jnp.pad(line, (0, row_count * piece - line.size)).astype(jnp.bfloat16)
-    line = line.reshape(row_count, piece // LANES, LANES)
-    mine = exchange(line, ROW).astype(jnp.float32).sum(axis=0).reshape(-1)
-    count = lax.axis_size(COL)
-    col_blocks = partial_rows.reshape(partial_rows.shape[0], count, -1).transpose(1, 0, 2)
-    block_shape = col_blocks.shape
-    col_blocks = col_blocks.reshape(count, -1).astype(jnp.bfloat16)
-    own = jnp.broadcast_to(mine[None].astype(jnp.bfloat16), (count, piece))
-    both = exchange(jnp.concatenate([own, col_blocks], axis=1), COL)
-    both = both.astype(jnp.float32).sum(axis=0)
-    out_weight_grad = both[piece:].reshape(block_shape[1:])
-    total = both[:piece].astype(jnp.bfloat16).reshape(piece // LANES, LANES)
-    total = spread(total, ROW).reshape(-1).astype(jnp.float32)
+    plane, ring, deep = lax.axis_size(PLANE), lax.axis_size(RING), lax.axis_size("col")
+    piece = -(-line.size // (plane * 1024)) * 1024
+    tiles = piece // LANES
+    line = jnp.pad(line, (0, plane * piece - line.size)).astype(jnp.bfloat16)
+    line, arrived = lax.optimization_barrier((line, arrived))
+    mine = exchange(line.reshape(plane, tiles, LANES), PLANE)
+    mine = mine.astype(jnp.float32).sum(axis=0).astype(jnp.bfloat16)
+    held = arrived.reshape(count // 2, 2, -1, width).astype(jnp.float32).sum(axis=0)
+    held = held.astype(jnp.bfloat16)
+    owned = held.shape[1]
+    held = held.reshape(2, owned, deep, ring // 4, -1).transpose(0, 3, 2, 1, 4)
+    held = held.reshape(2, ring // 4, -1, LANES)
+    none = jnp.zeros_like(held)
+    bands = jnp.concatenate([jnp.where(half == i, held, none) for i in range(2)])
+    bands = bands.reshape(ring, -1, LANES)
+    mine = jnp.broadcast_to(mine[None], (ring, tiles, LANES))
+    both = exchange(jnp.concatenate([mine, bands], axis=1), RING)
+    both = both.astype(jnp.float32).sum(axis=0).astype(jnp.bfloat16)
+    mine = jnp.broadcast_to(both[None, :tiles], (plane, tiles, LANES))
+    bands = both[tiles:].reshape(1, deep, -1, LANES)
+    place = lax.axis_index(CHIP_ROW)
+    here = jnp.arange(plane // deep, dtype=jnp.int32)[:, None, None, None] == place
+    bands = jnp.where(here, bands, jnp.zeros_like(bands)).reshape(plane, -1, LANES)
+    total = exchange(jnp.concatenate([mine, bands], axis=1), PLANE).astype(jnp.float32)
+    out_weight_grad = total[:, tiles:].sum(axis=0).reshape(owned, -1)
+    total = total[:, :tiles].reshape(-1)
     results, at = ([], 0)
     for a, shape in zip(pieces, (embed_grad.shape, (width,), (width,), table_grad.shape)):
         results.append(total[at : at + a.size].reshape(shape))

time: 238 us -> 214 us (0.90)
  waiting for transfers between devices: 63.8 us -> 39.6 us
  other arithmetic: 18.3 us -> 8.53 us
  starting transfers between devices: 56.2 us -> 61.6 us
  blocking collectives: 18.6 us -> 21.7 us
    ppermute x2, waiting for transfers between devices: 11.2 us -> 0.01 us  [swap(): lax.ppermute(value, axis, [(source, source ^ 1) for source in range(count)])]
    all_to_all x6 -> x5, starting transfers between devices: 37.3 us -> 47.5 us  [exchange(): return lax.all_to_all(blocks, axis, split_axis=0, concat_axis=0, tiled=True)]
    all_to_all x6 -> x5, waiting for transfers between devices: 38.9 us -> 32.3 us  [exchange(): return lax.all_to_all(blocks, axis, split_axis=0, concat_axis=0, tiled=True)]
    ppermute x2, waiting for transfers between devices: 13.7 us -> 7.33 us  [from_behind(): lax.ppermute(value, axis, [(source, (source - 1) % count) for source in r...]
    ppermute x2, starting transfers between devices: 12.9 us -> 7.28 us  [from_behind(): lax.ppermute(value, axis, [(source, (source - 1) % count) for source in r...]
    broadcast_in_dim x1 -> x0, other arithmetic: 5.35 us -> none  [spread(): copies = jnp.broadcast_to(line[None], (lax.axis_size(axis), *line.shape))]
    all_to_all x1, blocking collectives: 18.6 us -> 21.7 us  [exchange(): return lax.all_to_all(blocks, axis, split_axis=0, concat_axis=0, tiled=True)]
    concatenate x3 -> x4, other arithmetic: 3.61 us -> 0.8 us  [the longest x1 0.7 us: on_device(): both = exchange(jnp.concatenate([mine, bands], axis=1), RING)]
  transfers between devices with their start and end apart: 10 -> 9, of which waited for: 7 -> 6; matrix products, arithmetic and copies ran while one was open for 15% -> 11% of each run, Pallas kernels for 0% -> 0%
where the time goes in v4:
time: 214 us; the launch traced here: 212 us
  starting transfers between devices  61.6 us (29%)
  waiting for transfers between devices  39.6 us (19%)
  Pallas kernels  38.3 us (18%)
  local copies, waits for them, and re-layouts  30.9 us (14%)
  blocking collectives  21.7 us (10%)
  other arithmetic  8.53 us (4%)
  between operations  6.61 us (3%)
  matrix products  4.66 us (2%)
    all_to_all x5, starting transfers between devices, exchange(): return lax.all_to_all(blocks, axis, split_axis=0, concat_axis=0, tiled=True)  47.5 us
    all_to_all x5, waiting for transfers between devices, exchange(): return lax.all_to_all(blocks, axis, split_axis=0, concat_axis=0, tiled=True)  32.3 us
    pallas_call x1, Pallas kernels, run_backward(): pl.pallas_call(backward_kernel, grid=(cells // STEP,), in_specs=[stepped(...  22.5 us
    all_to_all x1, blocking collectives, exchange(): return lax.all_to_all(blocks, axis, split_axis=0, concat_axis=0, tiled=True)  21.7 us
    pallas_call x1, Pallas kernels, run_forward(): pl.pallas_call(forward_kernel, grid=(cells // STEP,), in_specs=[stepped((...  15.7 us
    ppermute x2, waiting for transfers between devices, from_behind(): lax.ppermute(value, axis, [(source, (source - 1) % count) for source in r...  7.33 us
    ppermute x2, starting transfers between devices, from_behind(): lax.ppermute(value, axis, [(source, (source - 1) % count) for source in r...  7.28 us
    ppermute x2, starting transfers between devices, swap(): lax.ppermute(value, axis, [(source, source ^ 1) for source in range(count)])  6.86 us
  transfers between devices with their start and end apart: 9, of which 6 were waited for; matrix products, arithmetic and copies ran while one was open for 11% of the time, Pallas kernels for 0%

profile of v4, /device:TPU:1, one launch (start us, length us, event | category | flops | bytes accessed | tf_op | source)
XLA Modules:
  0.0 211.9 jit_solution(10237477536455433478)
XLA Ops:
  0.7 0.8 reshape.380
  1.4 0.8 reshape.379
  2.3 1.0 broadcast_in_dim.43
  3.3 17.3 %all-to-all-start = ((bf16[64,48,128]{2,1,0:T(8,128)(2,1)}), bf16[64,48,128]{2,1,0:T(8,128)(2,1)S(1)}, u32[]{:S(2)}, u32[]{:S(2)}) async-start(bf16[64,48,128]{2,1,0:T(8,128)(2,1)} %broadcast_in_dim.43), calls=%async_computation | async-start | bytes 1572864 | tf_op jit(solution)/shard_map/all_to_all | solution.py:253
  20.6 1.7 reshape_squeeze.3
  23.1 2.9 %collective-permute-start = (bf16[7,32,1152]{2,1,0:T(8,128)(2,1)S(1)}, bf16[7,32,1152]{2,1,0:T(8,128)(2,1)S(1)}, u32[]{:S(2)}, u32[]{:S(2)}) collective-permute-start(bf16[7,32,1152]{2,1,0:T(8,128)(2,1)S(1)} %pad_maximum_fusion.1), channel_id=1, source_target_pairs={{0,496},{16,0},{32,16},{48,32},{64,48},{80,64},{96,80},{112,96},{1... | collective-permute-start | bytes 1548296 | tf_op jit(solution)/shard_map/ppermute | solution.py:263
  28.5 5.6 %collective-permute-done = bf16[7,32,1152]{2,1,0:T(8,128)(2,1)S(1)} collective-permute-done((bf16[7,32,1152]{2,1,0:T(8,128)(2,1)S(1)}, bf16[7,32,1152]{2,1,0:T(8,128)(2,1)S(1)}, u32[]{:S(2)}, u32[]{:S(2)}) %collective-permute-start) | collective-permute-done | bytes 516128 | tf_op jit(solution)/shard_map/ppermute | solution.py:263
  34.5 4.4 %collective-permute-start.1 = (bf16[8,8,1152]{2,1,0:T(8,128)(2,1)S(1)}, bf16[8,8,1152]{2,1,0:T(8,128)(2,1)S(1)}, u32[]{:S(2)}, u32[]{:S(2)}) collective-permute-start(bf16[8,8,1152]{2,1,0:T(8,128)(2,1)S(1)} %slice.190), channel_id=1, source_target_pairs={{0,14},{2,0},{4,2},{6,4},{8,6},{10,8},{12,10},{14,12},{1,15},{3,1}... | collective-permute-start | bytes 442376 | tf_op jit(solution)/shard_map/ppermute | solution.py:263
  41.5 1.7 collective-permute-done.1
  44.6 1.6 reshape.381
  46.9 1.8 reshape.382
  50.4 1.2 broadcast_in_dim.44
  51.6 3.8 %collective-permute-start.2 = (bf16[256,1152]{1,0:T(8,128)(2,1)S(1)}, bf16[256,1152]{1,0:T(8,128)(2,1)S(1)}, u32[]{:S(2)}, u32[]{:S(2)}) collective-permute-start(bf16[256,1152]{1,0:T(8,128)(2,1)S(1)} %bitcast.160), channel_id=1, source_target_pairs={{0,2},{2,0},{4,6},{6,4},{8,10},{10,8},{12,14},{14,12},{1,3},{3,1},... | collective-permute-start | bytes 1769480 | tf_op jit(solution)/shard_map/ppermute | solution.py:268
  56.7 2.2 %fusion.1 = f32[3,4096]{1,0:T(4,128)S(1)} fusion(s32[4096]{0:T(1024)S(1)} %eq.34, f32[12,225]{1,0:T(8,128)S(1)} %copy-done, s32[]{:T(128)S(6)} %select_n.80), kind=kOutput, calls=%fused_computation.2 | convolution fusion | flops 34099200 | bytes 69636 | tf_op jit(solution)/shard_map/dot_general | solution.py:384
  58.9 11.4 %all-to-all-start.1 = ((bf16[8,128,768]{2,1,0:T(8,128)(2,1)}), bf16[8,128,768]{2,1,0:T(8,128)(2,1)}, u32[]{:S(2)}, u32[]{:S(2)}) async-start(bf16[8,128,768]{2,1,0:T(8,128)(2,1)} %bitcast.28), calls=%async_computation.1 | async-start | bytes 3145728 | tf_op jit(solution)/shard_map/all_to_all | solution.py:253
  70.2 1.1 pad_maximum_fusion
  71.4 3.1 %collective-permute-start.3 = (bf16[512,1152]{1,0:T(8,128)(2,1)}, bf16[512,1152]{1,0:T(8,128)(2,1)}, u32[]{:S(2)}, u32[]{:S(2)}) collective-permute-start(bf16[512,1152]{1,0:T(8,128)(2,1)} %pad_maximum_fusion), channel_id=1, source_target_pairs={{0,16},{16,0},{1,17},{17,1},{2,18},{18,2},{3,19},{19,3},{4,20},{20... | collective-permute-start | bytes 3538952 | tf_op jit(solution)/shard_map/ppermute | solution.py:268
  75.5 0.7 pad.14.embed_w
  76.4 0.9 tile.12.bias
  77.9 0.7 convert_reduce_fusion
  78.6 1.1 fusion.8
  79.7 11.2 %all-to-all-done.1 = bf16[8,128,768]{2,1,0:T(8,128)(2,1)} async-done(((bf16[8,128,768]{2,1,0:T(8,128)(2,1)}), bf16[8,128,768]{2,1,0:T(8,128)(2,1)}, u32[]{:S(2)}, u32[]{:S(2)}) %all-to-all-start.1) | async-done | bytes 1572896 | tf_op jit(solution)/shard_map/all_to_all | solution.py:253
  91.0 1.1 slice.192
  92.5 1.0 slice.191
  93.6 0.9 copy.235
  94.4 2.7 %copy.197 = bf16[4,8,32,768]{3,2,1,0:T(8,128)(2,1)} copy(bf16[4,8,32,768]{3,2,0,1:T(8,128)(2,1)} %bitcast.38) | data formatting | bytes 3145728 | tf_op jit(solution)/shard_map/transpose | solution.py:330
  97.2 1.5 constant_dynamic-update-slice_fusion.cot.patches
  98.7 0.7 broadcast_in_dim.46.gain
  99.3 0.7 broadcast_in_dim.45.embed_b
  100.7 1.0 broadcast_in_dim.47.lab_col
  101.7 15.7 %forward.1 = (bf16[1024,640]{1,0:T(8,128)(2,1)}, f32[8,3,128,128]{3,2,1,0:T(8,128)}, f32[1024,1024]{1,0:T(8,128)}, f32[1024,128]{1,0:T(8,128)}, bf16[192,1024]{1,0:T(8,128)(2,1)}) custom-call(bf16[1024,1152]{1,0:T(8,128)(2,1)} %copy-done.1, bf16[1024,1152]{1,0:T(8,128)(2,1)} %copy-done.1, bf16[128,1024]{1,0:T(8,128)(2,1)} %pad.14.embed_w, ...), custom_call_target="tpu_custom_call" | custom-call | flops 2013265920 | bytes 8388608 | tf_op jit(solution)/shard_map/forward/pallas_call | solution.py:180
  117.5 22.5 %backward.1 = (f32[128,1024]{1,0:T(8,128)}, f32[8,1024]{1,0:T(8,128)}, f32[8,1024]{1,0:T(8,128)}, f32[3,128,128]{2,1,0:T(8,128)}) custom-call(bf16[1024,1152]{1,0:T(8,128)(2,1)} %copy-done.1, bf16[1024,1152]{1,0:T(8,128)(2,1)} %copy-done.1, bf16[1024,640]{1,0:T(8,128)(2,1)} %get-tuple-element.20.proj, f32[8,3,128,128]{3,2,1,0:T(8,128)} %get-tuple-element.21.prob_in, ...), custom_call_target="tpu_custom_call" | custom-call | flops 2013265920 | bytes 8388608 | tf_op jit(solution)/shard_map/backward/pallas_call | solution.py:214
  140.0 1.1 fusion.18
  141.1 0.8 reduce_sum.74
  141.9 0.8 reduce_sum.72
  142.7 4.3 %all-to-all-start.2 = ((bf16[8,24,1024]{2,1,0:T(8,128)(2,1)}), bf16[8,24,1024]{2,1,0:T(8,128)(2,1)S(1)}, u32[]{:S(2)}, u32[]{:S(2)}) async-start(bf16[8,24,1024]{2,1,0:T(8,128)(2,1)} %bitcast.49), calls=%async_computation.2 | async-start | bytes 786432 | tf_op jit(solution)/shard_map/all_to_all | solution.py:253
  147.2 1.4 fusion
  148.9 0.7 fusion.17
  149.5 5.2 %all-to-all-done.2 = bf16[8,24,1024]{2,1,0:T(8,128)(2,1)S(1)} async-done(((bf16[8,24,1024]{2,1,0:T(8,128)(2,1)}), bf16[8,24,1024]{2,1,0:T(8,128)(2,1)S(1)}, u32[]{:S(2)}, u32[]{:S(2)}) %all-to-all-start.2) | async-done | bytes 393248 | tf_op jit(solution)/shard_map/all_to_all | solution.py:253
  154.8 8.1 %all-to-all-start.3 = ((bf16[64,8,128]{2,1,0:T(8,128)(2,1)}), bf16[64,8,128]{2,1,0:T(8,128)(2,1)S(1)}, u32[]{:S(2)}, u32[]{:S(2)}) async-start(bf16[64,8,128]{2,1,0:T(8,128)(2,1)} %bitcast.50), calls=%async_computation.3 | async-start | bytes 262144 | tf_op jit(solution)/shard_map/all_to_all | solution.py:253
  163.7 9.1 %all-to-all-done.3 = bf16[64,8,128]{2,1,0:T(8,128)(2,1)S(1)} async-done(((bf16[64,8,128]{2,1,0:T(8,128)(2,1)}), bf16[64,8,128]{2,1,0:T(8,128)(2,1)S(1)}, u32[]{:S(2)}, u32[]{:S(2)}) %all-to-all-start.3) | async-done | bytes 131104 | tf_op jit(solution)/shard_map/all_to_all | solution.py:253
  173.0 0.7 pad_maximum_fusion.5
  173.7 6.4 %all-to-all-start.4 = ((bf16[8,104,128]{2,1,0:T(8,128)(2,1)}), bf16[8,104,128]{2,1,0:T(8,128)(2,1)S(1)}, u32[]{:S(2)}, u32[]{:S(2)}) async-start(bf16[8,104,128]{2,1,0:T(8,128)(2,1)} %pad_maximum_fusion.5), calls=%async_computation.4 | async-start | bytes 425984 | tf_op jit(solution)/shard_map/all_to_all | solution.py:253
  180.2 6.8 %all-to-all-done.4 = bf16[8,104,128]{2,1,0:T(8,128)(2,1)S(1)} async-done(((bf16[8,104,128]{2,1,0:T(8,128)(2,1)}), bf16[8,104,128]{2,1,0:T(8,128)(2,1)S(1)}, u32[]{:S(2)}, u32[]{:S(2)}) %all-to-all-start.4) | async-done | bytes 213024 | tf_op jit(solution)/shard_map/all_to_all | solution.py:253
  187.3 21.7 %all_to_all.30 = bf16[64,20,128]{2,1,0:T(8,128)(2,1)S(1)} all-to-all(bf16[64,20,128]{2,1,0:T(8,128)(2,1)S(1)} %pad_maximum_fusion.4), channel_id=1, replica_groups=mesh['yl'=4,'x'=4,'core'=2,'col'=8,'dp'=2] {'x','core','col'}, dimensions={0} | all-to-all | bytes 655360 | tf_op jit(solution)/shard_map/all_to_all | solution.py:253
  209.8 0.7 copy.237
  210.5 0.7 reshape.412
  211.2 0.7 reshape.415
  (127 shorter events, 11.4 us)
Async XLA Ops:
  0.6 56.0 %copy-start = (f32[12,225]{1,0:T(8,128)S(1)}, f32[12,225]{1,0:T(8,128)}, u32[]{:S(2)}) copy-start(f32[12,225]{1,0:T(8,128)} %param.17) | copy-start | bytes 32404
  0.6 19.9 %copy-start.6 = (bf16[1,3,32,128]{3,2,1,0:T(8,128)(2,1)S(1)}, bf16[1,3,32,128]{3,2,1,0:T(8,128)(2,1)}, u32[]{:S(2)}) copy-start(bf16[1,3,32,128]{3,2,1,0:T(8,128)(2,1)} %param.10) | copy-start | bytes 73732
  3.3 19.8 %copy-start.2 = (bf16[1,8,32,1024]{3,2,1,0:T(8,128)(2,1)S(1)}, bf16[1,8,32,1024]{3,2,1,0:T(8,128)(2,1)}, u32[]{:S(2)}) copy-start(bf16[1,8,32,1024]{3,2,1,0:T(8,128)(2,1)} %param.11) | copy-start | bytes 1572868
  3.3 40.4 %all-to-all-start = ((bf16[64,48,128]{2,1,0:T(8,128)(2,1)}), bf16[64,48,128]{2,1,0:T(8,128)(2,1)S(1)}, u32[]{:S(2)}, u32[]{:S(2)}) async-start(bf16[64,48,128]{2,1,0:T(8,128)(2,1)} %broadcast_in_dim.43), calls=%async_computation | async-start | bytes 1572864 | tf_op jit(solution)/shard_map/all_to_all | solution.py:253
  20.5 5.5 %copy-start.14 = (s32[1,2]{1,0:T(1,128)S(1)}, s32[1,2]{1,0:T(1,128)}, u32[]{:S(2)}) copy-start(s32[1,2]{1,0:T(1,128)} %param.19) | copy-start | bytes 28
  23.1 11.0 %collective-permute-start = (bf16[7,32,1152]{2,1,0:T(8,128)(2,1)S(1)}, bf16[7,32,1152]{2,1,0:T(8,128)(2,1)S(1)}, u32[]{:S(2)}, u32[]{:S(2)}) collective-permute-start(bf16[7,32,1152]{2,1,0:T(8,128)(2,1)S(1)} %pad_maximum_fusion.1), channel_id=1, source_target_pairs={{0,496},{16,0},{32,16},{48,32},{64,48},{80,64},{96,80},{112,96},{1... | collective-permute-start | bytes 1548296 | tf_op jit(solution)/shard_map/ppermute | solution.py:263
  34.5 8.8 %collective-permute-start.1 = (bf16[8,8,1152]{2,1,0:T(8,128)(2,1)S(1)}, bf16[8,8,1152]{2,1,0:T(8,128)(2,1)S(1)}, u32[]{:S(2)}, u32[]{:S(2)}) collective-permute-start(bf16[8,8,1152]{2,1,0:T(8,128)(2,1)S(1)} %slice.190), channel_id=1, source_target_pairs={{0,14},{2,0},{4,2},{6,4},{8,6},{10,8},{12,10},{14,12},{1,15},{3,1}... | collective-permute-start | bytes 442376 | tf_op jit(solution)/shard_map/ppermute | solution.py:263
  50.2 5.9 %copy-start.5 = (s32[64,64]{1,0:T(8,128)S(1)}, s32[64,64]{1,0:T(8,128)}, u32[]{:S(2)}) copy-start(s32[64,64]{1,0:T(8,128)} %param.18) | copy-start | bytes 49156
  51.6 18.6 %collective-permute-start.2 = (bf16[256,1152]{1,0:T(8,128)(2,1)S(1)}, bf16[256,1152]{1,0:T(8,128)(2,1)S(1)}, u32[]{:S(2)}, u32[]{:S(2)}) collective-permute-start(bf16[256,1152]{1,0:T(8,128)(2,1)S(1)} %bitcast.160), channel_id=1, source_target_pairs={{0,2},{2,0},{4,6},{6,4},{8,10},{10,8},{12,14},{14,12},{1,3},{3,1},... | collective-permute-start | bytes 1769480 | tf_op jit(solution)/shard_map/ppermute | solution.py:268
  56.2 2.7 %copy-start.9 = (s32[4096]{0:T(1024)}, s32[4096]{0:T(1024)S(1)}, u32[]{:S(2)}) copy-start(s32[4096]{0:T(1024)S(1)} %eq.34) | copy-start | bytes 49156
  58.9 32.1 %all-to-all-start.1 = ((bf16[8,128,768]{2,1,0:T(8,128)(2,1)}), bf16[8,128,768]{2,1,0:T(8,128)(2,1)}, u32[]{:S(2)}, u32[]{:S(2)}) async-start(bf16[8,128,768]{2,1,0:T(8,128)(2,1)} %bitcast.28), calls=%async_computation.1 | async-start | bytes 3145728 | tf_op jit(solution)/shard_map/all_to_all | solution.py:253
  70.2 5.3 %copy-start.4 = (bf16[48,1024]{1,0:T(8,128)(2,1)S(1)}, bf16[48,1024]{1,0:T(8,128)(2,1)}, u32[]{:S(2)}) copy-start(bf16[48,1024]{1,0:T(8,128)(2,1)} %param.12) | copy-start | bytes 294916
  71.4 25.8 %collective-permute-start.3 = (bf16[512,1152]{1,0:T(8,128)(2,1)}, bf16[512,1152]{1,0:T(8,128)(2,1)}, u32[]{:S(2)}, u32[]{:S(2)}) collective-permute-start(bf16[512,1152]{1,0:T(8,128)(2,1)} %pad_maximum_fusion), channel_id=1, source_target_pairs={{0,16},{16,0},{1,17},{17,1},{2,18},{18,2},{3,19},{19,3},{4,20},{20... | collective-permute-start | bytes 3538952 | tf_op jit(solution)/shard_map/ppermute | solution.py:268
  97.1 1.5 copy-start.12
  97.1 2.2 %copy-start.13 = (f32[1024]{0:T(1024)S(1)}, f32[1024]{0:T(1024)}, u32[]{:S(2)}) copy-start(f32[1024]{0:T(1024)} %param.13) | copy-start | bytes 12292
  97.1 2.9 %copy-start.11 = (s32[8,128]{1,0:T(8,128)S(1)}, s32[8,128]{1,0:T(8,128)}, u32[]{:S(2)}) copy-start(s32[8,128]{1,0:T(8,128)} %fusion.24) | copy-start | bytes 12292
  97.1 3.5 %copy-start.8 = (s32[1024]{0:T(1024)S(1)}, s32[1024]{0:T(1024)}, u32[]{:S(2)}) copy-start(s32[1024]{0:T(1024)} %fusion.21) | copy-start | bytes 12292
  98.7 3.0 %copy-start.1 = (bf16[1024,1152]{1,0:T(8,128)(2,1)}, bf16[1024,1152]{1,0:T(8,128)(2,1)S(1)}, u32[]{:S(2)}) copy-start(bf16[1024,1152]{1,0:T(8,128)(2,1)S(1)} %constant_dynamic-update-slice_fusion.cot.patches) | copy-start | bytes 7077892
  140.0 7.0 %copy-start.3 = (f32[3,128,128]{2,1,0:T(8,128)S(1)}, f32[3,128,128]{2,1,0:T(8,128)}, u32[]{:S(2)}) copy-start(f32[3,128,128]{2,1,0:T(8,128)} %get-tuple-element.27) | copy-start | bytes 589828
  140.0 7.2 %copy-start.10 = (s32[4096]{0:T(1024)S(1)}, s32[4096]{0:T(1024)}, u32[]{:S(2)}) copy-start(s32[4096]{0:T(1024)} %copy-done.9) | copy-start | bytes 49156
  140.0 8.9 %copy-start.7 = (f32[1024]{0:T(1024)S(1)}, f32[1024]{0:T(1024)}, u32[]{:S(2)}) copy-start(f32[1024]{0:T(1024)} %convert_reduce_fusion) | copy-start | bytes 12292
  142.7 12.0 %all-to-all-start.2 = ((bf16[8,24,1024]{2,1,0:T(8,128)(2,1)}), bf16[8,24,1024]{2,1,0:T(8,128)(2,1)S(1)}, u32[]{:S(2)}, u32[]{:S(2)}) async-start(bf16[8,24,1024]{2,1,0:T(8,128)(2,1)} %bitcast.49), calls=%async_computation.2 | async-start | bytes 786432 | tf_op jit(solution)/shard_map/all_to_all | solution.py:253
  154.8 18.1 %all-to-all-start.3 = ((bf16[64,8,128]{2,1,0:T(8,128)(2,1)}), bf16[64,8,128]{2,1,0:T(8,128)(2,1)S(1)}, u32[]{:S(2)}, u32[]{:S(2)}) async-start(bf16[64,8,128]{2,1,0:T(8,128)(2,1)} %bitcast.50), calls=%async_computation.3 | async-start | bytes 262144 | tf_op jit(solution)/shard_map/all_to_all | solution.py:253
  173.7 13.3 %all-to-all-start.4 = ((bf16[8,104,128]{2,1,0:T(8,128)(2,1)}), bf16[8,104,128]{2,1,0:T(8,128)(2,1)S(1)}, u32[]{:S(2)}, u32[]{:S(2)}) async-start(bf16[8,104,128]{2,1,0:T(8,128)(2,1)} %pad_maximum_fusion.5), calls=%async_computation.4 | async-start | bytes 425984 | tf_op jit(solution)/shard_map/all_to_all | solution.py:253

commit v5 on v4

v5 whole, which is shorter than its diff:
```python
import jax
import jax.numpy as jnp
from jax import lax
from jax.experimental import pallas as pl
from jax.experimental.pallas import tpu as pltpu
from jax.sharding import Mesh, PartitionSpec as P

WIN = 8
PATCH = 4
CELLS = WIN * WIN
norm_epsilon = 1e-05

STEP = 256
PAIR = 128
HEAD = 64
LANES = 128
SCALE = HEAD ** (-0.5)
UNITS = ((0, 128, 256, 0, 2), (384, 448, 512, 128, 1))
QKV = 640


def dot_nn(a, b):
    return lax.dot_general(a, b, (((1,), (0,)), ((), ())), preferred_element_type=jnp.float32)


def dot_nt(a, b):
    return lax.dot_general(a, b, (((1,), (1,)), ((), ())), preferred_element_type=jnp.float32)


def dot_tn(a, b):
    return lax.dot_general(a, b, (((0,), (0,)), ((), ())), preferred_element_type=jnp.float32)


def half_masks(count):
    lane = lax.broadcasted_iota(jnp.int32, (PAIR, count * HEAD), 1)
    return [(lane // HEAD) == i for i in range(count)]


def choose(masks, parts):
    return parts[0] if len(parts) == 1 else jnp.where(masks[0], parts[0], parts[1])


def only(masks, i, x):
    return x if len(masks) == 1 else jnp.where(masks[i], x, jnp.zeros_like(x))


def work():
    for pair in range(STEP // PAIR):
        for unit in UNITS:
            yield (pair, slice(pair * PAIR, (pair + 1) * PAIR), *unit)


def assemble(arrived, out):
    sources, rows, _ = arrived.shape
    band = rows // 4
    for source in range(sources):
        for i in range(4):
            at = (i * sources + source) * band
            out[at : at + band, :] = arrived[source, i * band : (i + 1) * band, :QKV]


def assemble_out(arrived, wide, out):
    sources = arrived.shape[0]
    for source in range(sources):
        at = source * 24
        for tile in range(8):
            cols = slice(tile * LANES, (tile + 1) * LANES)
            tall = arrived[source, tile * 16 : (tile + 1) * 16, QKV:]
            wide[at : at + 16, cols] = tall.astype(jnp.float32)
            low = [
                arrived[source, i * 64 + tile * 8 : i * 64 + tile * 8 + 8, QKV - 64 : QKV]
                for i in range(2)
            ]
            wide[at + 16 : at + 24, cols] = jnp.concatenate(low, axis=1).astype(jnp.float32)
    out[...] = wide[...].astype(jnp.bfloat16)


def forward_kernel(
    two, other, embed_w, embed_b, gain, arrived, bias, label,
    proj_out, prob_out, xhat_out, inv_out, grad_out, weights, bias_pair, scores, att, grad_acc
):
    step = pl.program_id(0)
    width = gain.shape[1]

    @pl.when(step == 0)
    def _():
        assemble(arrived, weights)
        for head in range(bias.shape[0]):
            row = jnp.concatenate([bias[head], bias[head]], axis=1)
            bias_pair[head] = jnp.concatenate([row, row], axis=0)

    cells = jnp.where(step < 2, two[...], other[...])
    cot = cells[:, :width]
    tokens = dot_nn(cells[:, width:], embed_w[...]) + embed_b[...]
    tokens = tokens.astype(jnp.bfloat16).astype(jnp.float32)
    centered = tokens - jnp.mean(tokens, axis=-1, keepdims=True)
    inv = lax.rsqrt(jnp.mean(centered * centered, axis=-1, keepdims=True) + norm_epsilon)
    xhat = centered * inv
    xhat_out[...] = xhat
    inv_out[...] = jnp.broadcast_to(inv, inv_out.shape)
    normed = (xhat * gain[...]).astype(jnp.bfloat16)
    proj_out[...] = dot_nn(normed, weights[...]).astype(jnp.bfloat16)
    heads = bias.shape[0]
    for pair, rows, q_at, k_at, v_at, at, count in work():
        q = proj_out[rows, q_at : q_at + count * HEAD]
        k = proj_out[rows, k_at : k_at + count * HEAD]
        for i in range(count):
            scores[pair * heads + at // HEAD + i] = dot_nt(only(half_masks(count), i, q), k)
    for pair in range(STEP // PAIR):
        line = label[pl.ds(step * (STEP // PAIR) + pair, 1), :]
        wide = jnp.broadcast_to(line, (PAIR, PAIR))
        same = wide == wide.T
        for head in range(heads):
            values = scores[pair * heads + head] * SCALE + bias_pair[head]
            values = jnp.where(same, values, -1e30)
            e = jnp.exp(values - jnp.max(values, axis=-1, keepdims=True))
            prob_out[pair, head] = e * (1.0 / jnp.sum(e, axis=-1, keepdims=True))
    for pair, rows, q_at, k_at, v_at, at, count in work():
        v = proj_out[rows, v_at : v_at + count * HEAD]
        parts = [
            dot_nn(prob_out[pair, at // HEAD + i].astype(jnp.bfloat16), v) for i in range(count)
        ]
        att[rows, at : at + count * HEAD] = choose(half_masks(count), parts).astype(jnp.bfloat16)
    grad = dot_tn(att[...], cot)

    @pl.when(step == 0)
    def _():
        grad_acc[...] = grad

    @pl.when(step > 0)
    def _():
        grad_acc[...] += grad

    @pl.when(step == pl.num_programs(0) - 1)
    def _():
        grad_out[...] = grad_acc[...].astype(grad_out.dtype)


def scores_kernel(
    two, other, proj, prob_in, arrived, dproj, table_out, wide, wo, table, datt, d_probs, lows
):
    step = pl.program_id(0)
    width = wo.shape[1]
    heads = prob_in.shape[1]

    @pl.when(step == 0)
    def _():
        assemble_out(arrived, wide, wo)
        table[...] = jnp.zeros_like(table)

    cot = jnp.where(step < 2, two[:, :width], other[:, :width])
    datt[...] = dot_nt(cot, wo[...]).astype(jnp.bfloat16)
    dproj[:, QKV - HEAD :] = jnp.zeros((STEP, HEAD), jnp.bfloat16)
    for pair, rows, q_at, k_at, v_at, at, count in work():
        v = proj[rows, v_at : v_at + count * HEAD]
        d_out = datt[rows, at : at + count * HEAD]
        for i in range(count):
            d_probs[pair * heads + at // HEAD + i] = dot_nt(only(half_masks(count), i, d_out), v)
    for head in range(heads):
        total = table[head]
        for pair in range(STEP // PAIR):
            prob, d_prob = prob_in[pair, head], d_probs[pair * heads + head]
            weighted = prob * d_prob
            d_scores = weighted - prob * jnp.sum(weighted, axis=-1, keepdims=True)
            total = total + d_scores
            lows[pair * heads + head] = d_scores.astype(jnp.bfloat16)
        table[head] = total
    for pair, rows, q_at, k_at, v_at, at, count in work():
        width_in = count * HEAD
        masks = half_masks(count)
        q = proj[rows, q_at : q_at + width_in]
        k = proj[rows, k_at : k_at + width_in]
        d_out = datt[rows, at : at + width_in]
        qs, ks, vs = [], [], []
        for i in range(count):
            head = at // HEAD + i
            low = lows[pair * heads + head]
            qs.append(dot_nn(low, k))
            ks.append(dot_tn(low, q))
            vs.append(dot_tn(prob_in[pair, head].astype(jnp.bfloat16), d_out))
        dproj[rows, q_at : q_at + width_in] = (choose(masks, qs) * SCALE).astype(jnp.bfloat16)
        dproj[rows, k_at : k_at + width_in] = (choose(masks, ks) * SCALE).astype(jnp.bfloat16)
        dproj[rows, v_at : v_at + width_in] = choose(masks, vs).astype(jnp.bfloat16)

    @pl.when(step == pl.num_programs(0) - 1)
    def _():
        for head in range(heads):
            full = table[head]
            table_out[head] = full[:CELLS, :CELLS] + full[CELLS:, CELLS:]


def norm_kernel(
    two, other, dproj, xhat, inv, gain, arrived, line_out, weights, dn, branch, embed, bias, gains
):
    step = pl.program_id(0)
    width = gain.shape[1]
    chunk = 32
    cells = jnp.where(step < 2, two[...], other[...])
    patches = cells[:, width:]

    @pl.when(step == 0)
    def _():
        assemble(arrived, weights)
        cot = cells[:, :width]
        embed[...] = dot_tn(patches, cot)
        bias[...] = cot.astype(jnp.float32).reshape(STEP // 8, 8, width).sum(axis=0)
        gains[...] = jnp.zeros_like(gains)

    dn[...] = dot_nt(dproj[...], weights[...])
    bias_sum, gain_sum = bias[...], gains[...]
    for i in range(STEP // chunk):
        rows = slice(i * chunk, (i + 1) * chunk)
        d, x = dn[rows, :], xhat[rows, :]
        gain_sum = gain_sum + (d * x).reshape(chunk // 8, 8, width).sum(axis=0)
        g = d * gain[...]
        mean = jnp.mean(g, axis=-1, keepdims=True)
        along = jnp.mean(g * x, axis=-1, keepdims=True)
        out = (inv[rows, 0:1] * (g - mean - x * along)).astype(jnp.bfloat16)
        branch[rows, :] = out
        bias_sum = bias_sum + out.astype(jnp.float32).reshape(chunk // 8, 8, width).sum(axis=0)
    bias[...] = bias_sum
    gains[...] = gain_sum
    embed[...] += dot_tn(patches, branch[...])

    @pl.when(step == pl.num_programs(0) - 1)
    def _():
        depth = 48
        line_out[:depth, :] = embed[:depth, :].astype(line_out.dtype)
        row = lax.broadcasted_iota(jnp.int32, (16, width), 0)
        sums = jnp.where(row == 0, jnp.sum(bias[...], axis=0, keepdims=True), 0.0)
        sums = jnp.where(row == 1, jnp.sum(gains[...], axis=0, keepdims=True), sums)
        line_out[depth:, :] = sums.astype(line_out.dtype)


def stepped(shape):
    rest = len(shape) - 1
    return pl.BlockSpec(shape, lambda i: (i,) + (0,) * rest)


def whole(shape):
    return pl.BlockSpec(shape, lambda i: (0,) * len(shape))


def cell_specs(width):
    return [
        pl.BlockSpec((STEP, width), lambda i: (jnp.minimum(i, 1), 0)),
        pl.BlockSpec((STEP, width), lambda i: (jnp.maximum(i - 2, 0), 0)),
    ]


def call(kernel, cells, in_specs, out_specs, out_shape, scratch, flops):
    return pl.pallas_call(
        kernel,
        grid=(cells // STEP,),
        in_specs=in_specs,
        out_specs=out_specs,
        out_shape=out_shape,
        scratch_shapes=scratch,
        compiler_params=pltpu.CompilerParams(
            dimension_semantics=("arbitrary",), vmem_limit_bytes=56 * 1024 * 1024
        ),
        cost_estimate=pl.CostEstimate(flops=flops, transcendentals=0, bytes_accessed=8 << 20),
    )


def run_forward(two, other, embed_w, embed_b, gain, arrived, bias, label):
    cells, width = 2 * two.shape[0], gain.shape[1]
    heads = bias.shape[0]
    features = heads * HEAD
    units = heads * (STEP // PAIR)
    f32, bf16 = jnp.float32, jnp.bfloat16
    return call(
        forward_kernel, cells,
        [
            *cell_specs(two.shape[1]), whole((LANES, width)), whole((1, width)), whole((1, width)),
            whole(arrived.shape), whole(bias.shape), whole(label.shape),
        ],
        [
            stepped((STEP, QKV)), stepped((STEP // PAIR, heads, PAIR, PAIR)),
            stepped((STEP, width)), stepped((STEP, LANES)), whole((features, width)),
        ],
        [
            jax.ShapeDtypeStruct((cells, QKV), bf16),
            jax.ShapeDtypeStruct((cells // PAIR, heads, PAIR, PAIR), f32),
            jax.ShapeDtypeStruct((cells, width), f32),
            jax.ShapeDtypeStruct((cells, LANES), f32),
            jax.ShapeDtypeStruct((features, width), bf16),
        ],
        [
            pltpu.VMEM((width, QKV), bf16), pltpu.VMEM((heads, PAIR, PAIR), f32),
            pltpu.VMEM((units, PAIR, PAIR), f32), pltpu.VMEM((STEP, features), bf16),
            pltpu.VMEM((features, width), f32),
        ],
        4 << 30,
    )(two, other, embed_w, embed_b, gain, arrived, bias, label)


def run_scores(two, other, proj, prob, arrived, width):
    cells = proj.shape[0]
    heads = prob.shape[1]
    features = heads * HEAD
    units = heads * (STEP // PAIR)
    f32, bf16 = jnp.float32, jnp.bfloat16
    return call(
        scores_kernel, cells,
        [
            *cell_specs(two.shape[1]), stepped((STEP, QKV)),
            stepped((STEP // PAIR, heads, PAIR, PAIR)), whole(arrived.shape),
        ],
        [stepped((STEP, QKV)), whole((heads, CELLS, CELLS))],
        [
            jax.ShapeDtypeStruct((cells, QKV), bf16),
            jax.ShapeDtypeStruct((heads, CELLS, CELLS), f32),
        ],
        [
            pltpu.VMEM((features, width), f32), pltpu.VMEM((features, width), bf16),
            pltpu.VMEM((heads, PAIR, PAIR), f32), pltpu.VMEM((STEP, features), bf16),
            pltpu.VMEM((units, PAIR, PAIR), f32), pltpu.VMEM((units, PAIR, PAIR), bf16),
        ],
        4 << 30,
    )(two, other, proj, prob, arrived)


def run_norm(two, other, dproj, xhat, inv, gain, arrived):
    cells, width = xhat.shape
    f32, bf16 = jnp.float32, jnp.bfloat16
    return call(
        norm_kernel, cells,
        [
            *cell_specs(two.shape[1]), stepped((STEP, QKV)), stepped((STEP, width)),
            stepped((STEP, LANES)), whole((1, width)), whole(arrived.shape),
        ],
        whole((64, width)),
        jax.ShapeDtypeStruct((64, width), bf16),
        [
            pltpu.VMEM((width, QKV), bf16), pltpu.VMEM((STEP, width), f32),
            pltpu.VMEM((STEP, width), bf16), pltpu.VMEM((LANES, width), f32),
            pltpu.VMEM((8, width), f32), pltpu.VMEM((8, width), f32),
        ],
        4 << 30,
    )(two, other, dproj, xhat, inv, gain, arrived)


ROW = ("yl", "x", "core")
COL = ("col", "dp")
CHIP_ROW = ("x", "core")
FAR = ("yl", "col", "dp")


def exchange(blocks, axis):
    return lax.all_to_all(blocks, axis, split_axis=0, concat_axis=0, tiled=True)


def spread(line, axis):
    copies = jnp.broadcast_to(line[None], (lax.axis_size(axis), *line.shape))
    return exchange(copies, axis)


def from_behind(value, axis):
    count = lax.axis_size(axis)
    return lax.ppermute(value, axis, [(source, (source - 1) % count) for source in range(count)])


def swap(value, axis):
    count = lax.axis_size(axis)
    return lax.ppermute(value, axis, [(source, source ^ 1) for source in range(count)])


def make_patches(pixel_block):
    channels, pixel_rows, pixel_cols = pixel_block.shape
    grid_rows = pixel_rows // PATCH
    grid_cols = pixel_cols // PATCH
    shaped = pixel_block.reshape(channels, grid_rows, PATCH, grid_cols, PATCH)
    return shaped.transpose(1, 3, 0, 2, 4).reshape(grid_rows, grid_cols, channels * PATCH * PATCH)


def window_split(block):
    rows_all, cols_all, features = block.shape
    shaped = block.reshape(rows_all // WIN, WIN, cols_all // WIN, WIN, features)
    return shaped.transpose(0, 2, 1, 3, 4).reshape(-1, features)


def splice_after(own, borrowed, offset, dim):
    joined = jnp.concatenate([own, borrowed], dim)
    return lax.dynamic_slice_in_dim(joined, offset, own.shape[dim], dim)


def pack_out(rows):
    tall = rows[:16].reshape(16, 8, LANES).transpose(1, 0, 2).reshape(LANES, LANES)
    low = rows[16:].reshape(8, 8, LANES).transpose(1, 0, 2).reshape(64, 2, 64)
    return jnp.concatenate([low.transpose(1, 0, 2).reshape(LANES, 64), tall], axis=1)


def gather_weights(qkv_weight, out_weight, half, own):
    split = qkv_weight.size // LANES
    line = jnp.concatenate([qkv_weight.reshape(-1, LANES), out_weight.reshape(-1, LANES)])
    lines = spread(line, FAR)
    bands = lax.axis_size("yl")
    cols = lines.shape[0] // bands
    rows_w, rows_o = qkv_weight.shape[0], out_weight.shape[0]
    qkv = lines[:, :split].reshape(bands, cols, *qkv_weight.shape).transpose(0, 2, 1, 3)
    qkv = qkv.reshape(bands * rows_w, 3, -1)
    out = lines[:, split:].reshape(bands, cols, *out_weight.shape).transpose(0, 2, 1, 3)
    out = out.reshape(bands, rows_o, -1)
    features = qkv.shape[2]
    mine = lax.dynamic_slice_in_dim(qkv, half * (features // 2), features // 2, 2)
    out = lax.dynamic_slice_in_dim(out, half * 2, 2, 0)
    group = features // 4
    blocks = []
    for core in range(2):
        part = mine[:, :, core * group : (core + 1) * group]
        pieces = [part[:, i, :LANES] for i in range(3)] + [part[:, i, LANES:] for i in range(3)]
        blocks.append(jnp.concatenate([*pieces, pack_out(out[core])], axis=1))
    both = jnp.stack(blocks)
    chips = lax.axis_size("x")
    sent = jnp.broadcast_to(both[None], (chips, *both.shape)).reshape(2 * chips, *both.shape[1:])
    sent, own = lax.optimization_barrier((sent, own))
    arrived = exchange(sent, CHIP_ROW)
    return arrived, own


def on_device(
    pixels,
    cotangent,
    embed_weight,
    embed_bias,
    layer_norm_gain,
    qkv_weight,
    out_weight,
    bias_table,
    rel_index,
    shifts,
):
    cotangent, pixels = cotangent[0], pixels[0]
    rows_dev, cols_dev, width = cotangent.shape
    all_heads, table_size = bias_table.shape
    heads = all_heads // 4
    grid_rows = rows_dev * lax.axis_size(ROW)
    grid_cols = cols_dev * lax.axis_size("col")
    row_shift, col_shift = shifts[0, 0], shifts[0, 1]
    row_at, col_at, core = lax.axis_index(ROW), lax.axis_index("col"), lax.axis_index("core")
    half = col_at % 2
    group = 2 * half + core

    depth = embed_weight.shape[0]
    patches = make_patches(pixels)
    patches = jnp.pad(patches, ((0, 0), (0, 0), (0, LANES - depth)))
    block = jnp.concatenate([cotangent, patches], axis=-1)
    below = from_behind(block[: WIN - 1], ROW)
    block = splice_after(block, below, row_shift, 0)
    block = splice_after(block, from_behind(block[:, :WIN], "col"), col_shift, 1)
    arrived, own = gather_weights(qkv_weight, out_weight, half, window_split(block))
    beside = swap(own, "col")
    two = jnp.concatenate([own, beside])
    other = swap(two, "core")
    cells = 2 * two.shape[0]

    labels = []
    for row_flip, col_flip in ((0, 0), (0, 1), (1, 0), (1, 1)):
        row_ids = (row_at ^ row_flip) * rows_dev + jnp.arange(rows_dev, dtype=jnp.int32)
        col_ids = (col_at ^ col_flip) * cols_dev + jnp.arange(cols_dev, dtype=jnp.int32)
        row_part = (row_ids >= grid_rows - row_shift).astype(jnp.int32)
        col_part = (col_ids >= grid_cols - col_shift).astype(jnp.int32)
        region = 2 * row_part[:, None] + col_part[None, :]
        labels.append(window_split(region[:, :, None])[:, 0])
    label = jnp.concatenate(labels) + 4 * (jnp.arange(cells, dtype=jnp.int32) // CELLS)
    label = label.astype(jnp.float32).reshape(-1, PAIR)
    selector = (
        rel_index.reshape(-1)[:, None] == jnp.arange(table_size, dtype=jnp.int32)[None, :]
    ).astype(jnp.float32)
    my_table = lax.dynamic_slice_in_dim(bias_table, group * heads, heads, 0)
    bias = jnp.dot(selector, my_table.T, precision=lax.Precision.HIGHEST).T
    bias = bias.reshape(heads, CELLS, CELLS)
    embed_w = jnp.pad(embed_weight, ((0, LANES - depth), (0, 0)))
    gain = layer_norm_gain[None]

    proj, prob, xhat, inv, out_grad = run_forward(
        two, other, embed_w, embed_bias[None], gain, arrived, bias, label
    )
    count = lax.axis_size(CHIP_ROW)
    held = exchange(out_grad.reshape(count, -1, width), CHIP_ROW)
    dproj, table_part = run_scores(two, other, proj, prob, arrived, width)
    held = held.reshape(count // 2, 2, -1, width).astype(jnp.float32).sum(axis=0)
    held = held.astype(jnp.bfloat16)
    none = jnp.zeros_like(held)
    bands = jnp.concatenate([jnp.where(half == i, held, none) for i in range(2)])
    bands = exchange(bands, "yl")
    line = run_norm(two, other, dproj, xhat, inv, gain, arrived)
    my_grad = jnp.dot(table_part.reshape(heads, -1), selector, precision=lax.Precision.HIGHEST)
    wide = 256
    my_grad = jnp.pad(my_grad, ((0, 0), (0, wide - table_size)))
    table_grad = lax.dynamic_update_slice_in_dim(
        jnp.zeros((all_heads, wide), jnp.float32), my_grad, group * heads, 0
    )
    table_rows = table_grad.astype(jnp.bfloat16).reshape(-1, width)
    line = lax.dynamic_update_slice(line, table_rows, (depth + 2, 0))
    line, bands = lax.optimization_barrier((line, bands))
    chunks = lax.axis_size(ROW)
    tall = line.shape[0]
    tiles = line.reshape(tall // 8, 8, width // LANES, LANES).transpose(0, 2, 1, 3)
    tiles = tiles.reshape(chunks, -1, LANES)
    mine = exchange(tiles, ROW)
    mine = mine.astype(jnp.float32).sum(axis=0).astype(jnp.bfloat16)
    rows_o = bands.shape[1]
    bands = bands.astype(jnp.float32).sum(axis=0).astype(jnp.bfloat16)
    spans = lax.axis_size(COL)
    bands = bands.reshape(rows_o, spans, -1).transpose(1, 0, 2).reshape(spans, -1, LANES)
    held = mine.shape[0]
    mine = jnp.broadcast_to(mine[None], (spans, held, LANES))
    both = exchange(jnp.concatenate([mine, bands], axis=1), COL)
    both = both.astype(jnp.float32).sum(axis=0)
    out_weight_grad = both[held:].reshape(rows_o, -1)
    total = spread(both[:held].astype(jnp.bfloat16), ROW)
    total = total.reshape(tall // 8, width // LANES, 8, LANES).transpose(0, 2, 1, 3)
    total = total.reshape(tall, width).astype(jnp.float32)
    table_grad = total[depth + 2 : depth + 5].reshape(all_heads, wide)[:, :table_size]
    return (out_weight_grad, total[:depth], total[depth], total[depth + 1], table_grad)


def solution(mesh):
    sizes = mesh.devices.shape
    names = ("yl", "x", "core", "col", "dp")
    fine = Mesh(mesh.devices.reshape(-1, 4, 2, *sizes[1:]), names)
    return jax.shard_map(
        on_device,
        mesh=fine,
        in_specs=(
            P("dp", None, ROW, "col"),
            P("dp", ROW, "col", None),
            P(),
            P(),
            P(),
            P(ROW, COL),
            P(ROW, COL),
            P(),
            P(),
            P("dp", None),
        ),
        out_specs=(P(ROW, COL), P(), P(), P(), P()),
        check_vma=False,
    )
```

time: 214 us -> 185 us (0.86)
  Pallas kernels: 38.3 us -> 27.7 us
  waiting for transfers between devices: 39.6 us -> 31.1 us
  local copies, waits for them, and re-layouts: 30.9 us -> 24.4 us
  other arithmetic: 8.53 us -> 2.41 us
  starting transfers between devices: 61.6 us -> 67.1 us
    pallas_call x2 -> x3, Pallas kernels: 38.3 us -> 27.7 us  [the longest x1 11.2 us: run_forward(): call(forward_kernel, cells, [*cell_specs(two.shape[1]), whole((LANES, wid...]
    all_to_all x5 -> x6, waiting for transfers between devices: 32.3 us -> 23.1 us  [exchange(): return lax.all_to_all(blocks, axis, split_axis=0, concat_axis=0, tiled=True)]
    broadcast_in_dim x10 -> x2, local copies, waits for them, and re-layouts: 3.23 us -> 0.02 us  [the longest x1 0.01 us: on_device(): mine = jnp.broadcast_to(mine[None], (spans, held, LANES))]
    all_to_all x5 -> x6, starting transfers between devices: 47.5 us -> 50.4 us  [exchange(): return lax.all_to_all(blocks, axis, split_axis=0, concat_axis=0, tiled=True)]
    transpose x1, local copies, waits for them, and re-layouts: 2.71 us -> 0.03 us  [on_device(): bands.reshape(rows_o, spans, -1).transpose(1, 0, 2)]
    ppermute x2, starting transfers between devices: 6.86 us -> 9.44 us  [swap(): lax.ppermute(value, axis, [(source, source ^ 1) for source in range(count)])]
    concatenate x5 -> x1, other arithmetic: 2.6 us -> 0.02 us  [on_device(): both = exchange(jnp.concatenate([mine, bands], axis=1), COL)]
    reduce_sum x6 -> x3, other arithmetic: 2.4 us -> 0.16 us  [the longest x1 0.06 us: on_device(): both = both.astype(jnp.float32).sum(axis=0)]
  transfers between devices with their start and end apart: 9 -> 10, of which waited for: 6 -> 5; matrix products, arithmetic and copies ran while one was open for 11% -> 8% of each run, Pallas kernels for 0% -> 9%
where the time goes in v5:
time: 185 us; the launch traced here: 184 us
  starting transfers between devices  67.1 us (36%)
  waiting for transfers between devices  31.1 us (17%)
  Pallas kernels  27.7 us (15%)
  local copies, waits for them, and re-layouts  24.4 us (13%)
  blocking collectives  21.5 us (12%)
  between operations  6.4 us (3%)
  matrix products  3.59 us (2%)
  other arithmetic  2.41 us (1%)
    all_to_all x6, starting transfers between devices, exchange(): return lax.all_to_all(blocks, axis, split_axis=0, concat_axis=0, tiled=True)  50.4 us
    all_to_all x6, waiting for transfers between devices, exchange(): return lax.all_to_all(blocks, axis, split_axis=0, concat_axis=0, tiled=True)  23.1 us
    all_to_all x1, blocking collectives, exchange(): return lax.all_to_all(blocks, axis, split_axis=0, concat_axis=0, tiled=True)  21.5 us
    pallas_call x1, Pallas kernels, run_forward(): call(forward_kernel, cells, [*cell_specs(two.shape[1]), whole((LANES, wid...  11.2 us
    ppermute x2, starting transfers between devices, swap(): lax.ppermute(value, axis, [(source, source ^ 1) for source in range(count)])  9.44 us
    pallas_call x1, Pallas kernels, run_norm(): call(norm_kernel, cells, [*cell_specs(two.shape[1]), stepped((STEP, QKV))...  8.7 us
    ppermute x2, waiting for transfers between devices, from_behind(): lax.ppermute(value, axis, [(source, (source - 1) % count) for source in r...  7.97 us
    pallas_call x1, Pallas kernels, run_scores(): call(scores_kernel, cells, [*cell_specs(two.shape[1]), stepped((STEP, QKV...  7.81 us
  transfers between devices with their start and end apart: 10, of which 5 were waited for; matrix products, arithmetic and copies ran while one was open for 8% of the time, Pallas kernels for 9%

profile of v5, /device:TPU:1, one launch (start us, length us, event | category | flops | bytes accessed | tf_op | source)
XLA Modules:
  0.0 184.1 jit_solution(13344968436321284470)
XLA Ops:
  0.6 0.8 reshape.236
  1.5 0.8 reshape.237
  2.3 1.0 broadcast_in_dim.16
  3.3 17.1 %all-to-all-start = ((bf16[64,48,128]{2,1,0:T(8,128)(2,1)}), bf16[64,48,128]{2,1,0:T(8,128)(2,1)S(1)}, u32[]{:S(2)}, u32[]{:S(2)}) async-start(bf16[64,48,128]{2,1,0:T(8,128)(2,1)} %broadcast_in_dim.16), calls=%async_computation | async-start | bytes 1572864 | tf_op jit(solution)/shard_map/all_to_all | solution.py:351
  20.4 1.7 reshape_squeeze.3
  22.1 0.7 copy.228
  23.0 2.9 %collective-permute-start = (bf16[7,32,1152]{2,1,0:T(8,128)(2,1)S(1)}, bf16[7,32,1152]{2,1,0:T(8,128)(2,1)S(1)}, u32[]{:S(2)}, u32[]{:S(2)}) collective-permute-start(bf16[7,32,1152]{2,1,0:T(8,128)(2,1)S(1)} %pad_maximum_fusion), channel_id=1, source_target_pairs={{0,496},{16,0},{32,16},{48,32},{64,48},{80,64},{96,80},{112,96},{1... | collective-permute-start | bytes 1548296 | tf_op jit(solution)/shard_map/ppermute | solution.py:361
  25.9 0.6 fusion.17
  28.4 5.6 %collective-permute-done = bf16[7,32,1152]{2,1,0:T(8,128)(2,1)S(1)} collective-permute-done((bf16[7,32,1152]{2,1,0:T(8,128)(2,1)S(1)}, bf16[7,32,1152]{2,1,0:T(8,128)(2,1)S(1)}, u32[]{:S(2)}, u32[]{:S(2)}) %collective-permute-start) | collective-permute-done | bytes 516128 | tf_op jit(solution)/shard_map/ppermute | solution.py:361
  34.4 4.4 %collective-permute-start.1 = (bf16[8,8,1152]{2,1,0:T(8,128)(2,1)S(1)}, bf16[8,8,1152]{2,1,0:T(8,128)(2,1)S(1)}, u32[]{:S(2)}, u32[]{:S(2)}) collective-permute-start(bf16[8,8,1152]{2,1,0:T(8,128)(2,1)S(1)} %slice.147), channel_id=1, source_target_pairs={{0,14},{2,0},{4,2},{6,4},{8,6},{10,8},{12,10},{14,12},{1,15},{3,1}... | collective-permute-start | bytes 442376 | tf_op jit(solution)/shard_map/ppermute | solution.py:361
  40.8 2.4 %collective-permute-done.1 = bf16[8,8,1152]{2,1,0:T(8,128)(2,1)S(1)} collective-permute-done((bf16[8,8,1152]{2,1,0:T(8,128)(2,1)S(1)}, bf16[8,8,1152]{2,1,0:T(8,128)(2,1)S(1)}, u32[]{:S(2)}, u32[]{:S(2)}) %collective-permute-start.1) | collective-permute-done | bytes 147488 | tf_op jit(solution)/shard_map/ppermute | solution.py:361
  43.1 0.3 fusion.5
  43.6 1.6 reshape.238
  45.2 0.6 copy.210
  45.8 1.8 %reshape.239 = bf16[128,3,768]{2,1,0:T(4,128)(2,1)S(1)} reshape(bf16[4,32,16,144]{3,2,1,0:T(8,128)(2,1)S(1)} %copy.210) | data formatting | bytes 1179648 | tf_op jit(solution)/shard_map/reshape | solution.py:402
  48.6 0.7 constant_dynamic-slice_fusion.6
  49.3 0.6 constant_dynamic-slice_fusion.2
  50.3 1.3 broadcast_in_dim.17
  51.6 3.8 %collective-permute-start.2 = (bf16[256,1152]{1,0:T(8,128)(2,1)S(1)}, bf16[256,1152]{1,0:T(8,128)(2,1)S(1)}, u32[]{:S(2)}, u32[]{:S(2)}) collective-permute-start(bf16[256,1152]{1,0:T(8,128)(2,1)S(1)} %bitcast.126), channel_id=1, source_target_pairs={{0,2},{2,0},{4,6},{6,4},{8,10},{10,8},{12,14},{14,12},{1,3},{3,1},... | collective-permute-start | bytes 1769480 | tf_op jit(solution)/shard_map/ppermute | solution.py:366
  55.4 11.4 %all-to-all-start.1 = ((bf16[8,128,768]{2,1,0:T(8,128)(2,1)}), bf16[8,128,768]{2,1,0:T(8,128)(2,1)S(1)}, u32[]{:S(2)}, u32[]{:S(2)}) async-start(bf16[8,128,768]{2,1,0:T(8,128)(2,1)} %bitcast.28), calls=%async_computation.1 | async-start | bytes 3145728 | tf_op jit(solution)/shard_map/all_to_all | solution.py:351
  66.7 0.9 constant_dynamic-update-slice_fusion.1
  67.6 0.9 constant_dynamic-update-slice_fusion.two
  68.4 5.7 %collective-permute-start.3 = (bf16[512,1152]{1,0:T(8,128)(2,1)}, bf16[512,1152]{1,0:T(8,128)(2,1)}, u32[]{:S(2)}, u32[]{:S(2)}) collective-permute-start(bf16[512,1152]{1,0:T(8,128)(2,1)} %constant_dynamic-update-slice_fusion.two), channel_id=1, source_target_pairs={{0,16},{16,0},{1,17},{17,1},{2,18},{18,2},{3,19},{19,3},{4,20},{20... | collective-permute-start | bytes 3538952 | tf_op jit(solution)/shard_map/ppermute | solution.py:366
  76.0 2.2 %fusion.1 = f32[3,4096]{1,0:T(4,128)S(1)} fusion(s32[4096]{0:T(1024)S(1)} %eq.23, f32[12,225]{1,0:T(8,128)S(1)} %copy-done, s32[]{:T(128)S(6)} %select_n.48), kind=kOutput, calls=%fused_computation.2 | convolution fusion | flops 34099200 | bytes 69636 | tf_op jit(solution)/shard_map/dot_general | solution.py:472
  78.2 0.8 reshape.256.bias
  78.9 0.7 pad.13.embed_w
  79.7 0.6 fusion.11.label
  80.3 7.0 %all-to-all-done.1.arrived = bf16[8,128,768]{2,1,0:T(8,128)(2,1)S(1)} async-done(((bf16[8,128,768]{2,1,0:T(8,128)(2,1)}), bf16[8,128,768]{2,1,0:T(8,128)(2,1)S(1)}, u32[]{:S(2)}, u32[]{:S(2)}) %all-to-all-start.1) | async-done | bytes 1572896 | tf_op jit(solution)/shard_map/all_to_all | solution.py:351
  87.3 1.2 copy-done.2
  88.5 11.2 %shard_map.137 = (bf16[1024,640]{1,0:T(8,128)(2,1)}, f32[8,3,128,128]{3,2,1,0:T(8,128)}, f32[1024,1024]{1,0:T(8,128)}, f32[1024,128]{1,0:T(8,128)}, bf16[192,1024]{1,0:T(8,128)(2,1)}) custom-call(bf16[512,1152]{1,0:T(8,128)(2,1)} %constant_dynamic-update-slice_fusion.two, bf16[512,1152]{1,0:T(8,128)(2,1)} %collective-permute-done.3.other, ...), custom_call_target="tpu_custom_call" | custom-call | flops 4294967296 | bytes 8388608 | tf_op jit(solution)/shard_map/pallas_call | solution.py:272
  99.6 4.3 %all-to-all-start.2 = ((bf16[8,24,1024]{2,1,0:T(8,128)(2,1)}), bf16[8,24,1024]{2,1,0:T(8,128)(2,1)S(1)}, u32[]{:S(2)}, u32[]{:S(2)}) async-start(bf16[8,24,1024]{2,1,0:T(8,128)(2,1)} %bitcast.135), calls=%async_computation.2 | async-start | bytes 786432 | tf_op jit(solution)/shard_map/all_to_all | solution.py:351
  104.0 7.8 %shard_map.138 = (bf16[1024,640]{1,0:T(8,128)(2,1)}, f32[3,64,64]{2,1,0:T(8,128)}) custom-call(bf16[512,1152]{1,0:T(8,128)(2,1)} %constant_dynamic-update-slice_fusion.two, bf16[512,1152]{1,0:T(8,128)(2,1)} %collective-permute-done.3.other, bf16[1024,640]{1,0:T(8,128)(2,1)} %get-tuple-element.18.proj, f32[8,3,128,128]{3,2,1,0:T(8,128)} %get-tuple-element.19.prob_in, ...), custom_call_target="tpu_custom_call" | custom-call | flops 4294967296 | bytes 8388608 | tf_op jit(solution)/shard_map/pallas_call | solution.py:304
  111.8 1.0 reshape.257
  112.8 1.4 fusion
  114.5 0.7 pad_maximum_fusion.2
  115.2 3.8 %all-to-all-start.3 = ((bf16[4,24,1024]{2,1,0:T(8,128)(2,1)}), bf16[4,24,1024]{2,1,0:T(8,128)(2,1)S(1)}, u32[]{:S(2)}, u32[]{:S(2)}) async-start(bf16[4,24,1024]{2,1,0:T(8,128)(2,1)} %pad_maximum_fusion.2), calls=%async_computation.3 | async-start | bytes 393216 | tf_op jit(solution)/shard_map/all_to_all | solution.py:351
  119.0 8.7 %shard_map.139 = bf16[64,1024]{1,0:T(8,128)(2,1)} custom-call(bf16[512,1152]{1,0:T(8,128)(2,1)} %constant_dynamic-update-slice_fusion.two, bf16[512,1152]{1,0:T(8,128)(2,1)} %collective-permute-done.3.other, bf16[1024,640]{1,0:T(8,128)(2,1)} %get-tuple-element.20.dproj, f32[1024,1024]{1,0:T(8,128)} %get-tuple-element.21.xhat, ...), custom_call_target="tpu_custom_call" | custom-call | flops 4294967296 | bytes 8388608 | tf_op jit(solution)/shard_map/pallas_call | solution.py:327
  127.7 1.4 dynamic_update_slice.7
  129.1 8.5 %all-to-all-start.4 = ((bf16[32,16,128]{2,1,0:T(8,128)(2,1)}), bf16[32,16,128]{2,1,0:T(8,128)(2,1)S(1)}, u32[]{:S(2)}, u32[]{:S(2)}) async-start(bf16[32,16,128]{2,1,0:T(8,128)(2,1)} %bitcast.142), calls=%async_computation.4 | async-start | bytes 262144 | tf_op jit(solution)/shard_map/all_to_all | solution.py:351
  137.9 8.2 %all-to-all-done.4 = bf16[32,16,128]{2,1,0:T(8,128)(2,1)S(1)} async-done(((bf16[32,16,128]{2,1,0:T(8,128)(2,1)}), bf16[32,16,128]{2,1,0:T(8,128)(2,1)S(1)}, u32[]{:S(2)}, u32[]{:S(2)}) %all-to-all-start.4) | async-done | bytes 131104 | tf_op jit(solution)/shard_map/all_to_all | solution.py:351
  146.2 21.5 %all_to_all.35 = bf16[16,28,128]{2,1,0:T(8,128)(2,1)S(1)} all-to-all(bf16[16,28,128]{2,1,0:T(8,128)(2,1)S(1)} %pad_maximum_fusion.3), channel_id=1, replica_groups=mesh['yl'=4,'x'=4,'core'=2,'col'=8,'dp'=2] {'col','dp'}, dimensions={0} | all-to-all | bytes 229376 | tf_op jit(solution)/shard_map/all_to_all | solution.py:351
  167.7 0.7 broadcast_in_dim.23
  168.4 5.2 %all-to-all-start.6 = ((bf16[32,16,128]{2,1,0:T(8,128)(2,1)}), bf16[32,16,128]{2,1,0:T(8,128)(2,1)S(1)}, u32[]{:S(2)}, u32[]{:S(2)}) async-start(bf16[32,16,128]{2,1,0:T(8,128)(2,1)} %broadcast_in_dim.23), calls=%async_computation.6 | async-start | bytes 262144 | tf_op jit(solution)/shard_map/all_to_all | solution.py:351
  173.6 0.7 reshape.265
  174.3 7.8 %all-to-all-done.6 = bf16[32,16,128]{2,1,0:T(8,128)(2,1)S(1)} async-done(((bf16[32,16,128]{2,1,0:T(8,128)(2,1)}), bf16[32,16,128]{2,1,0:T(8,128)(2,1)S(1)}, u32[]{:S(2)}, u32[]{:S(2)}) %all-to-all-start.6) | async-done | bytes 131104 | tf_op jit(solution)/shard_map/all_to_all | solution.py:351
  182.2 0.6 fusion.16
  182.8 0.7 slice_bitcast_fusion
  183.5 0.6 reshape.266
  (75 shorter events, 3.1 us)
Async XLA Ops:
  0.6 75.3 %copy-start = (f32[12,225]{1,0:T(8,128)S(1)}, f32[12,225]{1,0:T(8,128)}, u32[]{:S(2)}) copy-start(f32[12,225]{1,0:T(8,128)} %param.17) | copy-start | bytes 32404
  2.3 18.2 %copy-start.5 = (bf16[1,3,32,128]{3,2,1,0:T(8,128)(2,1)S(1)}, bf16[1,3,32,128]{3,2,1,0:T(8,128)(2,1)}, u32[]{:S(2)}) copy-start(bf16[1,3,32,128]{3,2,1,0:T(8,128)(2,1)} %param.10) | copy-start | bytes 73732
  3.3 40.2 %all-to-all-start = ((bf16[64,48,128]{2,1,0:T(8,128)(2,1)}), bf16[64,48,128]{2,1,0:T(8,128)(2,1)S(1)}, u32[]{:S(2)}, u32[]{:S(2)}) async-start(bf16[64,48,128]{2,1,0:T(8,128)(2,1)} %broadcast_in_dim.16), calls=%async_computation | async-start | bytes 1572864 | tf_op jit(solution)/shard_map/all_to_all | solution.py:351
  20.4 2.5 %copy-start.1 = (bf16[1,8,32,1024]{3,2,1,0:T(8,128)(2,1)S(1)}, bf16[1,8,32,1024]{3,2,1,0:T(8,128)(2,1)}, u32[]{:S(2)}) copy-start(bf16[1,8,32,1024]{3,2,1,0:T(8,128)(2,1)} %param.11) | copy-start | bytes 1572868
  22.1 3.8 %copy-start.6 = (s32[1,2]{1,0:T(1,128)S(1)}, s32[1,2]{1,0:T(1,128)}, u32[]{:S(2)}) copy-start(s32[1,2]{1,0:T(1,128)} %param.19) | copy-start | bytes 28
  23.0 11.0 %collective-permute-start = (bf16[7,32,1152]{2,1,0:T(8,128)(2,1)S(1)}, bf16[7,32,1152]{2,1,0:T(8,128)(2,1)S(1)}, u32[]{:S(2)}, u32[]{:S(2)}) collective-permute-start(bf16[7,32,1152]{2,1,0:T(8,128)(2,1)S(1)} %pad_maximum_fusion), channel_id=1, source_target_pairs={{0,496},{16,0},{32,16},{48,32},{64,48},{80,64},{96,80},{112,96},{1... | collective-permute-start | bytes 1548296 | tf_op jit(solution)/shard_map/ppermute | solution.py:361
  34.4 8.7 %collective-permute-start.1 = (bf16[8,8,1152]{2,1,0:T(8,128)(2,1)S(1)}, bf16[8,8,1152]{2,1,0:T(8,128)(2,1)S(1)}, u32[]{:S(2)}, u32[]{:S(2)}) collective-permute-start(bf16[8,8,1152]{2,1,0:T(8,128)(2,1)S(1)} %slice.147), channel_id=1, source_target_pairs={{0,14},{2,0},{4,2},{6,4},{8,6},{10,8},{12,10},{14,12},{1,15},{3,1}... | collective-permute-start | bytes 442376 | tf_op jit(solution)/shard_map/ppermute | solution.py:361
  51.6 16.0 %collective-permute-start.2 = (bf16[256,1152]{1,0:T(8,128)(2,1)S(1)}, bf16[256,1152]{1,0:T(8,128)(2,1)S(1)}, u32[]{:S(2)}, u32[]{:S(2)}) collective-permute-start(bf16[256,1152]{1,0:T(8,128)(2,1)S(1)} %bitcast.126), channel_id=1, source_target_pairs={{0,2},{2,0},{4,6},{6,4},{8,10},{10,8},{12,14},{14,12},{1,3},{3,1},... | collective-permute-start | bytes 1769480 | tf_op jit(solution)/shard_map/ppermute | solution.py:366
  55.4 31.9 %all-to-all-start.1 = ((bf16[8,128,768]{2,1,0:T(8,128)(2,1)}), bf16[8,128,768]{2,1,0:T(8,128)(2,1)S(1)}, u32[]{:S(2)}, u32[]{:S(2)}) async-start(bf16[8,128,768]{2,1,0:T(8,128)(2,1)} %bitcast.28), calls=%async_computation.1 | async-start | bytes 3145728 | tf_op jit(solution)/shard_map/all_to_all | solution.py:351
  66.7 9.2 %copy-start.4 = (s32[64,64]{1,0:T(8,128)S(1)}, s32[64,64]{1,0:T(8,128)}, u32[]{:S(2)}) copy-start(s32[64,64]{1,0:T(8,128)} %param.18) | copy-start | bytes 49156
  67.6 11.4 %copy-start.3 = (bf16[48,1024]{1,0:T(8,128)(2,1)S(1)}, bf16[48,1024]{1,0:T(8,128)(2,1)}, u32[]{:S(2)}) copy-start(bf16[48,1024]{1,0:T(8,128)(2,1)} %param.12) | copy-start | bytes 294916
  68.4 18.9 %collective-permute-start.3 = (bf16[512,1152]{1,0:T(8,128)(2,1)}, bf16[512,1152]{1,0:T(8,128)(2,1)}, u32[]{:S(2)}, u32[]{:S(2)}) collective-permute-start(bf16[512,1152]{1,0:T(8,128)(2,1)} %constant_dynamic-update-slice_fusion.two), channel_id=1, source_target_pairs={{0,16},{16,0},{1,17},{17,1},{2,18},{18,2},{3,19},{19,3},{4,20},{20... | collective-permute-start | bytes 3538952 | tf_op jit(solution)/shard_map/ppermute | solution.py:366
  87.3 1.2 copy-start.2
  99.6 14.7 %all-to-all-start.2 = ((bf16[8,24,1024]{2,1,0:T(8,128)(2,1)}), bf16[8,24,1024]{2,1,0:T(8,128)(2,1)S(1)}, u32[]{:S(2)}, u32[]{:S(2)}) async-start(bf16[8,24,1024]{2,1,0:T(8,128)(2,1)} %bitcast.135), calls=%async_computation.2 | async-start | bytes 786432 | tf_op jit(solution)/shard_map/all_to_all | solution.py:351
  115.2 13.9 %all-to-all-start.3 = ((bf16[4,24,1024]{2,1,0:T(8,128)(2,1)}), bf16[4,24,1024]{2,1,0:T(8,128)(2,1)S(1)}, u32[]{:S(2)}, u32[]{:S(2)}) async-start(bf16[4,24,1024]{2,1,0:T(8,128)(2,1)} %pad_maximum_fusion.2), calls=%async_computation.3 | async-start | bytes 393216 | tf_op jit(solution)/shard_map/all_to_all | solution.py:351
  129.1 17.0 %all-to-all-start.4 = ((bf16[32,16,128]{2,1,0:T(8,128)(2,1)}), bf16[32,16,128]{2,1,0:T(8,128)(2,1)S(1)}, u32[]{:S(2)}, u32[]{:S(2)}) async-start(bf16[32,16,128]{2,1,0:T(8,128)(2,1)} %bitcast.142), calls=%async_computation.4 | async-start | bytes 262144 | tf_op jit(solution)/shard_map/all_to_all | solution.py:351
  168.4 13.7 %all-to-all-start.6 = ((bf16[32,16,128]{2,1,0:T(8,128)(2,1)}), bf16[32,16,128]{2,1,0:T(8,128)(2,1)S(1)}, u32[]{:S(2)}, u32[]{:S(2)}) async-start(bf16[32,16,128]{2,1,0:T(8,128)(2,1)} %broadcast_in_dim.23), calls=%async_computation.6 | async-start | bytes 262144 | tf_op jit(solution)/shard_map/all_to_all | solution.py:351

commit v6 on v5

--- a/solution.py
+++ b/solution.py
@@ -75,31 +75,34 @@
     out[...] = wide[...].astype(jnp.bfloat16)
 
 
-def forward_kernel(
-    two, other, embed_w, embed_b, gain, arrived, bias, label,
-    proj_out, prob_out, xhat_out, inv_out, grad_out, weights, bias_pair, scores, att, grad_acc
-):
+def tokens_kernel(two, other, embed_w, embed_b, gain, normed_out, xhat_out, inv_out):
     step = pl.program_id(0)
-    width = gain.shape[1]
-
-    @pl.when(step == 0)
-    def _():
-        assemble(arrived, weights)
-        for head in range(bias.shape[0]):
-            row = jnp.concatenate([bias[head], bias[head]], axis=1)
-            bias_pair[head] = jnp.concatenate([row, row], axis=0)
-
-    cells = jnp.where(step < 2, two[...], other[...])
-    cot = cells[:, :width]
-    tokens = dot_nn(cells[:, width:], embed_w[...]) + embed_b[...]
+    patches = jnp.where(step < 2, two[...], other[...])
+    tokens = dot_nn(patches, embed_w[...]) + embed_b[...]
     tokens = tokens.astype(jnp.bfloat16).astype(jnp.float32)
     centered = tokens - jnp.mean(tokens, axis=-1, keepdims=True)
     inv = lax.rsqrt(jnp.mean(centered * centered, axis=-1, keepdims=True) + norm_epsilon)
     xhat = centered * inv
     xhat_out[...] = xhat
     inv_out[...] = jnp.broadcast_to(inv, inv_out.shape)
-    normed = (xhat * gain[...]).astype(jnp.bfloat16)
-    proj_out[...] = dot_nn(normed, weights[...]).astype(jnp.bfloat16)
+    normed_out[...] = (xhat * gain[...]).astype(jnp.bfloat16)
+
+
+def forward_kernel(
+    two, other, normed, arrived, bias, label,
+    proj_out, prob_out, grad_out, weights, bias_pair, scores, att, grad_acc
+):
+    step = pl.program_id(0)
+
+    @pl.when(step == 0)
+    def _():
+        assemble(arrived, weights)
+        for head in range(bias.shape[0]):
+            row = jnp.concatenate([bias[head], bias[head]], axis=1)
+            bias_pair[head] = jnp.concatenate([row, row], axis=0)
+
+    cot = jnp.where(step < 2, two[...], other[...])
+    proj_out[...] = dot_nn(normed[...], weights[...]).astype(jnp.bfloat16)
     heads = bias.shape[0]
     for pair, rows, q_at, k_at, v_at, at, count in work():
         q = proj_out[rows, q_at : q_at + count * HEAD]
@@ -140,7 +143,6 @@
     two, other, proj, prob_in, arrived, dproj, table_out, wide, wo, table, datt, d_probs, lows
 ):
     step = pl.program_id(0)
-    width = wo.shape[1]
     heads = prob_in.shape[1]
 
     @pl.when(step == 0)
@@ -148,7 +150,7 @@
         assemble_out(arrived, wide, wo)
         table[...] = jnp.zeros_like(table)
 
-    cot = jnp.where(step < 2, two[:, :width], other[:, :width])
+    cot = jnp.where(step < 2, two[...], other[...])
     datt[...] = dot_nt(cot, wo[...]).astype(jnp.bfloat16)
     dproj[:, QKV - HEAD :] = jnp.zeros((STEP, HEAD), jnp.bfloat16)
     for pair, rows, q_at, k_at, v_at, at, count in work():
@@ -241,10 +243,10 @@
     return pl.BlockSpec(shape, lambda i: (0,) * len(shape))
 
 
-def cell_specs(width):
+def cell_specs(width, at=0):
     return [
-        pl.BlockSpec((STEP, width), lambda i: (jnp.minimum(i, 1), 0)),
-        pl.BlockSpec((STEP, width), lambda i: (jnp.maximum(i - 2, 0), 0)),
+        pl.BlockSpec((STEP, width), lambda i: (jnp.minimum(i, 1), at)),
+        pl.BlockSpec((STEP, width), lambda i: (jnp.maximum(i - 2, 0), at)),
     ]
 
 
@@ -263,8 +265,28 @@
     )
 
 
-def run_forward(two, other, embed_w, embed_b, gain, arrived, bias, label):
+def run_tokens(two, other, embed_w, embed_b, gain):
     cells, width = 2 * two.shape[0], gain.shape[1]
+    f32, bf16 = jnp.float32, jnp.bfloat16
+    return call(
+        tokens_kernel, cells,
+        [
+            *cell_specs(LANES, width // LANES), whole((LANES, width)), whole((1, width)),
+            whole((1, width)),
+        ],
+        [stepped((STEP, width)), stepped((STEP, width)), stepped((STEP, LANES))],
+        [
+            jax.ShapeDtypeStruct((cells, width), bf16),
+            jax.ShapeDtypeStruct((cells, width), f32),
+            jax.ShapeDtypeStruct((cells, LANES), f32),
+        ],
+        [],
+        2 << 30,
+    )(two, other, embed_w, embed_b, gain)
+
+
+def run_forward(two, other, normed, arrived, bias, label):
+    cells, width = normed.shape
     heads = bias.shape[0]
     features = heads * HEAD
     units = heads * (STEP // PAIR)
@@ -272,18 +294,16 @@
     return call(
         forward_kernel, cells,
         [
-            *cell_specs(two.shape[1]), whole((LANES, width)), whole((1, width)), whole((1, width)),
+            *cell_specs(width), stepped((STEP, width)),
             whole(arrived.shape), whole(bias.shape), whole(label.shape),
         ],
         [
             stepped((STEP, QKV)), stepped((STEP // PAIR, heads, PAIR, PAIR)),
-            stepped((STEP, width)), stepped((STEP, LANES)), whole((features, width)),
+            whole((features, width)),
         ],
         [
             jax.ShapeDtypeStruct((cells, QKV), bf16),
             jax.ShapeDtypeStruct((cells // PAIR, heads, PAIR, PAIR), f32),
-            jax.ShapeDtypeStruct((cells, width), f32),
-            jax.ShapeDtypeStruct((cells, LANES), f32),
             jax.ShapeDtypeStruct((features, width), bf16),
         ],
         [
@@ -292,7 +312,7 @@
             pltpu.VMEM((features, width), f32),
         ],
         4 << 30,
-    )(two, other, embed_w, embed_b, gain, arrived, bias, label)
+    )(two, other, normed, arrived, bias, label)
 
 
 def run_scores(two, other, proj, prob, arrived, width):
@@ -304,7 +324,7 @@
     return call(
         scores_kernel, cells,
         [
-            *cell_specs(two.shape[1]), stepped((STEP, QKV)),
+            *cell_specs(width), stepped((STEP, QKV)),
             stepped((STEP // PAIR, heads, PAIR, PAIR)), whole(arrived.shape),
         ],
         [stepped((STEP, QKV)), whole((heads, CELLS, CELLS))],
@@ -343,6 +363,7 @@
 
 ROW = ("yl", "x", "core")
 COL = ("col", "dp")
+RING = ("yl", "dp")
 CHIP_ROW = ("x", "core")
 FAR = ("yl", "col", "dp")
 
@@ -391,7 +412,7 @@
     return jnp.concatenate([low.transpose(1, 0, 2).reshape(LANES, 64), tall], axis=1)
 
 
-def gather_weights(qkv_weight, out_weight, half, own):
+def gather_weights(qkv_weight, out_weight, half):
     split = qkv_weight.size // LANES
     line = jnp.concatenate([qkv_weight.reshape(-1, LANES), out_weight.reshape(-1, LANES)])
     lines = spread(line, FAR)
@@ -414,9 +435,8 @@
     both = jnp.stack(blocks)
     chips = lax.axis_size("x")
     sent = jnp.broadcast_to(both[None], (chips, *both.shape)).reshape(2 * chips, *both.shape[1:])
-    sent, own = lax.optimization_barrier((sent, own))
     arrived = exchange(sent, CHIP_ROW)
-    return arrived, own
+    return arrived
 
 
 def on_device(
@@ -449,7 +469,8 @@
     below = from_behind(block[: WIN - 1], ROW)
     block = splice_after(block, below, row_shift, 0)
     block = splice_after(block, from_behind(block[:, :WIN], "col"), col_shift, 1)
-    arrived, own = gather_weights(qkv_weight, out_weight, half, window_split(block))
+    own = window_split(block)
+    arrived = gather_weights(qkv_weight, out_weight, half)
     beside = swap(own, "col")
     two = jnp.concatenate([own, beside])
     other = swap(two, "core")
@@ -474,17 +495,20 @@
     embed_w = jnp.pad(embed_weight, ((0, LANES - depth), (0, 0)))
     gain = layer_norm_gain[None]
 
-    proj, prob, xhat, inv, out_grad = run_forward(
-        two, other, embed_w, embed_bias[None], gain, arrived, bias, label
-    )
+    normed, xhat, inv = run_tokens(two, other, embed_w, embed_bias[None], gain)
+    proj, prob, out_grad = run_forward(two, other, normed, arrived, bias, label)
     count = lax.axis_size(CHIP_ROW)
     held = exchange(out_grad.reshape(count, -1, width), CHIP_ROW)
     dproj, table_part = run_scores(two, other, proj, prob, arrived, width)
     held = held.reshape(count // 2, 2, -1, width).astype(jnp.float32).sum(axis=0)
     held = held.astype(jnp.bfloat16)
+    rows_o, deep = held.shape[1], lax.axis_size("col")
+    ring = lax.axis_size(RING)
+    held = held.reshape(2, rows_o, deep, ring // 4, -1).transpose(0, 3, 2, 1, 4)
+    held = held.reshape(2, ring // 4, -1, LANES)
     none = jnp.zeros_like(held)
     bands = jnp.concatenate([jnp.where(half == i, held, none) for i in range(2)])
-    bands = exchange(bands, "yl")
+    bands = exchange(bands.reshape(ring, -1, LANES), RING)
     line = run_norm(two, other, dproj, xhat, inv, gain, arrived)
     my_grad = jnp.dot(table_part.reshape(heads, -1), selector, precision=lax.Precision.HIGHEST)
     wide = 256
@@ -500,14 +524,14 @@
     tiles = line.reshape(tall // 8, 8, width // LANES, LANES).transpose(0, 2, 1, 3)
     tiles = tiles.reshape(chunks, -1, LANES)
     mine = exchange(tiles, ROW)
-    mine = mine.astype(jnp.float32).sum(axis=0).astype(jnp.bfloat16)
-    rows_o = bands.shape[1]
+    mine = mine.astype(jnp.float32).sum(axis=0)
+    mine = mine + swap(mine, "dp")
+    mine = mine.astype(jnp.bfloat16)
     bands = bands.astype(jnp.float32).sum(axis=0).astype(jnp.bfloat16)
-    spans = lax.axis_size(COL)
-    bands = bands.reshape(rows_o, spans, -1).transpose(1, 0, 2).reshape(spans, -1, LANES)
+    bands = bands.reshape(deep, -1, LANES)
     held = mine.shape[0]
-    mine = jnp.broadcast_to(mine[None], (spans, held, LANES))
-    both = exchange(jnp.concatenate([mine, bands], axis=1), COL)
+    mine = jnp.broadcast_to(mine[None], (deep, held, LANES))
+    both = exchange(jnp.concatenate([mine, bands], axis=1), "col")
     both = both.astype(jnp.float32).sum(axis=0)
     out_weight_grad = both[held:].reshape(rows_o, -1)
     total = spread(both[:held].astype(jnp.bfloat16), ROW)

time: 185 us -> 201 us (1.086)
  waiting for transfers between devices: 31.1 us -> 49.2 us
  starting transfers between devices: 67.1 us -> 53.9 us
  blocking collectives: 21.5 us -> 29.6 us
  Pallas kernels: 27.7 us -> 30.8 us
    all_to_all x6 -> x5, starting transfers between devices: 50.4 us -> 30.8 us  [exchange(): return lax.all_to_all(blocks, axis, split_axis=0, concat_axis=0, tiled=True)]
    ppermute x2 -> x3, waiting for transfers between devices: 0.01 us -> 17.5 us  [swap(): lax.ppermute(value, axis, [(source, source ^ 1) for source in range(count)])]
    all_to_all x1 -> x2, blocking collectives: 21.5 us -> 29.6 us  [exchange(): return lax.all_to_all(blocks, axis, split_axis=0, concat_axis=0, tiled=True)]
    ppermute x2, waiting for transfers between devices: 7.97 us -> 14.8 us  [from_behind(): lax.ppermute(value, axis, [(source, (source - 1) % count) for source in r...]
    all_to_all x6 -> x5, waiting for transfers between devices: 23.1 us -> 16.8 us  [exchange(): return lax.all_to_all(blocks, axis, split_axis=0, concat_axis=0, tiled=True)]
    ppermute x2, starting transfers between devices: 7.28 us -> 12.9 us  [from_behind(): lax.ppermute(value, axis, [(source, (source - 1) % count) for source in r...]
    pallas_call x2 -> x3, Pallas kernels: 19 us -> 22.1 us  [the longest x1 8.81 us: run_forward(): call(forward_kernel, cells, [*cell_specs(width), stepped((STEP, width)),...]
    ppermute x2 -> x3, starting transfers between devices: 9.44 us -> 10.2 us  [swap(): lax.ppermute(value, axis, [(source, source ^ 1) for source in range(count)])]
  transfers between devices with their start and end apart: 10 -> 10, of which waited for: 5 -> 5; matrix products, arithmetic and copies ran while one was open for 8% -> 10% of each run, Pallas kernels for 9% -> 11%
where the time goes in v6:
time: 201 us; the launch traced here: 199 us
  starting transfers between devices  53.9 us (27%)
  waiting for transfers between devices  49.2 us (24%)
  Pallas kernels  30.8 us (15%)
  blocking collectives  29.6 us (15%)
  local copies, waits for them, and re-layouts  22.5 us (11%)
  between operations  6.48 us (3%)
  matrix products  3.59 us (2%)
  other arithmetic  3.49 us (2%)
    all_to_all x5, starting transfers between devices, exchange(): return lax.all_to_all(blocks, axis, split_axis=0, concat_axis=0, tiled=True)  30.8 us
    all_to_all x2, blocking collectives, exchange(): return lax.all_to_all(blocks, axis, split_axis=0, concat_axis=0, tiled=True)  29.6 us
    ppermute x3, waiting for transfers between devices, swap(): lax.ppermute(value, axis, [(source, source ^ 1) for source in range(count)])  17.5 us
    all_to_all x5, waiting for transfers between devices, exchange(): return lax.all_to_all(blocks, axis, split_axis=0, concat_axis=0, tiled=True)  16.8 us
    ppermute x2, waiting for transfers between devices, from_behind(): lax.ppermute(value, axis, [(source, (source - 1) % count) for source in r...  14.8 us
    ppermute x2, starting transfers between devices, from_behind(): lax.ppermute(value, axis, [(source, (source - 1) % count) for source in r...  12.9 us
    ppermute x3, starting transfers between devices, swap(): lax.ppermute(value, axis, [(source, source ^ 1) for source in range(count)])  10.2 us
    pallas_call x1, Pallas kernels, run_forward(): call(forward_kernel, cells, [*cell_specs(width), stepped((STEP, width)),...  8.81 us
  transfers between devices with their start and end apart: 10, of which 5 were waited for; matrix products, arithmetic and copies ran while one was open for 10% of the time, Pallas kernels for 11%

profile of v6, /device:TPU:1, one launch (start us, length us, event | category | flops | bytes accessed | tf_op | source)
XLA Modules:
  0.0 199.4 jit_solution(18400679254938894180)
XLA Ops:
  0.7 2.5 %reshape_squeeze.3 = bf16[3,8,4,32,4]{4,3,2,1,0:T(8,128)(2,1)S(1)} reshape(bf16[1,3,32,128]{3,2,1,0:T(8,128)(2,1)} %param.10) | data formatting | bytes 49152 | tf_op jit(solution)/shard_map/reshape;squeeze | solution.py:394
  3.2 0.7 copy.217
  4.1 8.7 %collective-permute-start = (bf16[7,32,1152]{2,1,0:T(8,128)(2,1)S(1)}, bf16[7,32,1152]{2,1,0:T(8,128)(2,1)S(1)}, u32[]{:S(2)}, u32[]{:S(2)}) collective-permute-start(bf16[7,32,1152]{2,1,0:T(8,128)(2,1)S(1)} %pad_maximum_fusion.1), channel_id=1, source_target_pairs={{0,496},{16,0},{32,16},{48,32},{64,48},{80,64},{96,80},{112,96},{1... | collective-permute-start | bytes 1548296 | tf_op jit(solution)/shard_map/ppermute | solution.py:382
  13.0 1.0 broadcast_in_dim.18
  14.0 11.0 %all-to-all-start = ((bf16[64,48,128]{2,1,0:T(8,128)(2,1)}), bf16[64,48,128]{2,1,0:T(8,128)(2,1)S(1)}, u32[]{:S(2)}, u32[]{:S(2)}) async-start(bf16[64,48,128]{2,1,0:T(8,128)(2,1)} %broadcast_in_dim.18), calls=%async_computation | async-start | bytes 1572864 | tf_op jit(solution)/shard_map/all_to_all | solution.py:372
  25.0 0.6 fusion.17
  27.6 0.3 fusion.7
  27.9 4.1 %collective-permute-start.1 = (bf16[8,8,1152]{2,1,0:T(8,128)(2,1)S(1)}, bf16[8,8,1152]{2,1,0:T(8,128)(2,1)S(1)}, u32[]{:S(2)}, u32[]{:S(2)}) collective-permute-start(bf16[8,8,1152]{2,1,0:T(8,128)(2,1)S(1)} %slice.145), channel_id=1, source_target_pairs={{0,14},{2,0},{4,2},{6,4},{8,6},{10,8},{12,10},{14,12},{1,15},{3,1}... | collective-permute-start | bytes 442376 | tf_op jit(solution)/shard_map/ppermute | solution.py:382
  34.0 14.8 %collective-permute-done.1 = bf16[8,8,1152]{2,1,0:T(8,128)(2,1)S(1)} collective-permute-done((bf16[8,8,1152]{2,1,0:T(8,128)(2,1)S(1)}, bf16[8,8,1152]{2,1,0:T(8,128)(2,1)S(1)}, u32[]{:S(2)}, u32[]{:S(2)}) %collective-permute-start.1) | collective-permute-done | bytes 147488 | tf_op jit(solution)/shard_map/ppermute | solution.py:382
  48.8 0.3 fusion.5
  49.2 2.8 %collective-permute-start.2 = (bf16[256,1152]{1,0:T(8,128)(2,1)S(1)}, bf16[256,1152]{1,0:T(8,128)(2,1)S(1)}, u32[]{:S(2)}, u32[]{:S(2)}) collective-permute-start(bf16[256,1152]{1,0:T(8,128)(2,1)S(1)} %bitcast.132), channel_id=1, source_target_pairs={{0,2},{2,0},{4,6},{6,4},{8,10},{10,8},{12,14},{14,12},{1,3},{3,1},... | collective-permute-start | bytes 1769480 | tf_op jit(solution)/shard_map/ppermute | solution.py:387
  52.0 13.6 %collective-permute-done.2 = bf16[256,1152]{1,0:T(8,128)(2,1)S(1)} collective-permute-done((bf16[256,1152]{1,0:T(8,128)(2,1)S(1)}, bf16[256,1152]{1,0:T(8,128)(2,1)S(1)}, u32[]{:S(2)}, u32[]{:S(2)}) %collective-permute-start.2) | collective-permute-done | bytes 589856 | tf_op jit(solution)/shard_map/ppermute | solution.py:387
  65.6 1.1 pad_maximum_fusion.two
  66.7 3.1 %collective-permute-start.3 = (bf16[512,1152]{1,0:T(8,128)(2,1)}, bf16[512,1152]{1,0:T(8,128)(2,1)}, u32[]{:S(2)}, u32[]{:S(2)}) collective-permute-start(bf16[512,1152]{1,0:T(8,128)(2,1)} %pad_maximum_fusion.two), channel_id=1, source_target_pairs={{0,16},{16,0},{1,17},{17,1},{2,18},{18,2},{3,19},{19,3},{4,20},{20... | collective-permute-start | bytes 3538952 | tf_op jit(solution)/shard_map/ppermute | solution.py:387
  69.9 1.6 reshape.255
  71.5 0.6 copy.220
  72.1 1.8 reshape.256
  74.9 0.7 constant_dynamic-slice_fusion.5
  75.6 0.6 constant_dynamic-slice_fusion.1
  76.6 1.3 broadcast_in_dim.19
  77.8 3.9 %all-to-all-start.1 = ((bf16[8,128,768]{2,1,0:T(8,128)(2,1)}), bf16[8,128,768]{2,1,0:T(8,128)(2,1)S(1)}, u32[]{:S(2)}, u32[]{:S(2)}) async-start(bf16[8,128,768]{2,1,0:T(8,128)(2,1)} %bitcast.38), calls=%async_computation.1 | async-start | bytes 3145728 | tf_op jit(solution)/shard_map/all_to_all | solution.py:372
  83.6 2.2 %fusion.1 = f32[3,4096]{1,0:T(4,128)S(1)} fusion(s32[4096]{0:T(1024)S(1)} %eq.23, f32[12,225]{1,0:T(8,128)S(1)} %copy-done, s32[]{:T(128)S(6)} %select_n.66), kind=kOutput, calls=%fused_computation.2 | convolution fusion | flops 34099200 | bytes 69636 | tf_op jit(solution)/shard_map/dot_general | solution.py:493
  85.8 0.8 reshape.270.bias
  86.5 0.7 pad.13.embed_w
  87.3 0.6 fusion.11.label
  87.9 5.5 %shard_map.137 = (bf16[1024,1024]{1,0:T(8,128)(2,1)}, f32[1024,1024]{1,0:T(8,128)}, f32[1024,128]{1,0:T(8,128)}) custom-call(bf16[512,1152]{1,0:T(8,128)(2,1)} %pad_maximum_fusion.two, bf16[512,1152]{1,0:T(8,128)(2,1)} %collective-permute-done.3.other, bf16[128,1024]{1,0:T(8,128)(2,1)} %pad.13.embed_w, f32[1,1024]{1,0:T(1,128)} %bitcast.157, f32[1,1024]{1,0:T(1,128)} %bitcast.158), custom_call_target="tpu_custom_call" | custom-call | flops 2147483648 | bytes 8388608 | tf_op jit(solution)/shard_map/pallas_call | solution.py:271
  93.4 8.9 %all-to-all-done.1.arrived = bf16[8,128,768]{2,1,0:T(8,128)(2,1)S(1)} async-done(((bf16[8,128,768]{2,1,0:T(8,128)(2,1)}), bf16[8,128,768]{2,1,0:T(8,128)(2,1)S(1)}, u32[]{:S(2)}, u32[]{:S(2)}) %all-to-all-start.1) | async-done | bytes 1572896 | tf_op jit(solution)/shard_map/all_to_all | solution.py:372
  102.3 1.1 copy-done.2
  103.4 8.8 %shard_map.138 = (bf16[1024,640]{1,0:T(8,128)(2,1)}, f32[8,3,128,128]{3,2,1,0:T(8,128)}, bf16[192,1024]{1,0:T(8,128)(2,1)}) custom-call(bf16[512,1152]{1,0:T(8,128)(2,1)} %pad_maximum_fusion.two, bf16[512,1152]{1,0:T(8,128)(2,1)} %collective-permute-done.3.other, bf16[1024,1024]{1,0:T(8,128)(2,1)} %get-tuple-element.15.normed, ...), custom_call_target="tpu_custom_call" | custom-call | flops 4294967296 | bytes 8388608 | tf_op jit(solution)/shard_map/pallas_call | solution.py:294
  112.2 4.3 %all-to-all-start.2 = ((bf16[8,24,1024]{2,1,0:T(8,128)(2,1)}), bf16[8,24,1024]{2,1,0:T(8,128)(2,1)S(1)}, u32[]{:S(2)}, u32[]{:S(2)}) async-start(bf16[8,24,1024]{2,1,0:T(8,128)(2,1)} %bitcast.143), calls=%async_computation.2 | async-start | bytes 786432 | tf_op jit(solution)/shard_map/all_to_all | solution.py:372
  116.6 7.7 %shard_map.139 = (bf16[1024,640]{1,0:T(8,128)(2,1)}, f32[3,64,64]{2,1,0:T(8,128)}) custom-call(bf16[512,1152]{1,0:T(8,128)(2,1)} %pad_maximum_fusion.two, bf16[512,1152]{1,0:T(8,128)(2,1)} %collective-permute-done.3.other, bf16[1024,640]{1,0:T(8,128)(2,1)} %get-tuple-element.16.proj, f32[8,3,128,128]{3,2,1,0:T(8,128)} %get-tuple-element.17.prob_in, ...), custom_call_target="tpu_custom_call" | custom-call | flops 4294967296 | bytes 8388608 | tf_op jit(solution)/shard_map/pallas_call | solution.py:324
  124.3 1.0 reshape.271
  125.3 1.4 fusion
  127.8 0.7 pad_maximum_fusion.3
  128.5 5.3 %all-to-all-start.3 = ((bf16[8,96,128]{2,1,0:T(8,128)(2,1)}), bf16[8,96,128]{2,1,0:T(8,128)(2,1)S(1)}, u32[]{:S(2)}, u32[]{:S(2)}) async-start(bf16[8,96,128]{2,1,0:T(8,128)(2,1)} %bitcast.47), calls=%async_computation.3 | async-start | bytes 393216 | tf_op jit(solution)/shard_map/all_to_all | solution.py:372
  133.8 8.7 %shard_map.140 = bf16[64,1024]{1,0:T(8,128)(2,1)} custom-call(bf16[512,1152]{1,0:T(8,128)(2,1)} %pad_maximum_fusion.two, bf16[512,1152]{1,0:T(8,128)(2,1)} %collective-permute-done.3.other, bf16[1024,640]{1,0:T(8,128)(2,1)} %get-tuple-element.18.dproj, f32[1024,1024]{1,0:T(8,128)} %get-tuple-element.19.xhat, f32[1024,128]{1,0:T(8,128)} %get-tuple-element.20.inv, ...), custom_call_target="tpu_custom_call" | custom-call | flops 4294967296 | bytes 8388608 | tf_op jit(solution)/shard_map/pallas_call | solution.py:347
  142.5 1.4 dynamic_update_slice.7
  143.8 17.0 %all_to_all.35 = bf16[32,16,128]{2,1,0:T(8,128)(2,1)S(1)} all-to-all(bf16[32,16,128]{2,1,0:T(8,128)(2,1)} %bitcast.149), channel_id=1, replica_groups=mesh['yl'=4,'x'=4,'core'=2,'col'=8,'dp'=2] {'yl','x','core'}, dimensions={0} | all-to-all | bytes 262144 | tf_op jit(solution)/shard_map/all_to_all | solution.py:372
  160.9 4.3 %collective-permute-start.4 = (f32[16,128]{1,0:T(8,128)S(1)}, f32[16,128]{1,0:T(8,128)S(1)}, u32[]{:S(2)}, u32[]{:S(2)}) collective-permute-start(f32[16,128]{1,0:T(8,128)S(1)} %convert_reduce_fusion), channel_id=1, source_target_pairs={{0,1},{1,0},{2,3},{3,2},{4,5},{5,4},{6,7},{7,6},{8,9},{9,8},{10,11... | collective-permute-start | bytes 24584 | tf_op jit(solution)/shard_map/ppermute | solution.py:387
  165.3 3.9 %collective-permute-done.4 = f32[16,128]{1,0:T(8,128)S(1)} collective-permute-done((f32[16,128]{1,0:T(8,128)S(1)}, f32[16,128]{1,0:T(8,128)S(1)}, u32[]{:S(2)}, u32[]{:S(2)}) %collective-permute-start.4) | collective-permute-done | bytes 8224 | tf_op jit(solution)/shard_map/ppermute | solution.py:387
  169.2 12.6 %all_to_all.36 = bf16[8,28,128]{2,1,0:T(8,128)(2,1)S(1)} all-to-all(bf16[8,28,128]{2,1,0:T(8,128)(2,1)S(1)} %pad_maximum_fusion.4), channel_id=1, replica_groups=mesh['yl'=4,'x'=4,'core'=2,'col'=8,'dp'=2] {'col'}, dimensions={0} | all-to-all | bytes 114688 | tf_op jit(solution)/shard_map/all_to_all | solution.py:372
  181.9 0.7 broadcast_in_dim.23
  182.6 6.3 %all-to-all-start.6 = ((bf16[32,16,128]{2,1,0:T(8,128)(2,1)}), bf16[32,16,128]{2,1,0:T(8,128)(2,1)S(1)}, u32[]{:S(2)}, u32[]{:S(2)}) async-start(bf16[32,16,128]{2,1,0:T(8,128)(2,1)} %broadcast_in_dim.23), calls=%async_computation.6 | async-start | bytes 262144 | tf_op jit(solution)/shard_map/all_to_all | solution.py:372
  188.9 0.7 reshape.279
  189.5 8.0 %all-to-all-done.6 = bf16[32,16,128]{2,1,0:T(8,128)(2,1)S(1)} async-done(((bf16[32,16,128]{2,1,0:T(8,128)(2,1)}), bf16[32,16,128]{2,1,0:T(8,128)(2,1)S(1)}, u32[]{:S(2)}, u32[]{:S(2)}) %all-to-all-start.6) | async-done | bytes 131104 | tf_op jit(solution)/shard_map/all_to_all | solution.py:372
  197.5 0.6 fusion.16
  198.1 0.7 slice_bitcast_fusion
  198.8 0.6 reshape.280
  (83 shorter events, 3.4 us)
Async XLA Ops:
  0.6 83.0 %copy-start = (f32[12,225]{1,0:T(8,128)S(1)}, f32[12,225]{1,0:T(8,128)}, u32[]{:S(2)}) copy-start(f32[12,225]{1,0:T(8,128)} %param.17) | copy-start | bytes 32404
  0.6 3.3 %copy-start.1 = (bf16[1,8,32,1024]{3,2,1,0:T(8,128)(2,1)S(1)}, bf16[1,8,32,1024]{3,2,1,0:T(8,128)(2,1)}, u32[]{:S(2)}) copy-start(bf16[1,8,32,1024]{3,2,1,0:T(8,128)(2,1)} %param.11) | copy-start | bytes 1572868
  3.1 9.7 %copy-start.5 = (bf16[32,144]{1,0:T(8,128)(2,1)S(1)}, bf16[32,144]{1,0:T(8,128)(2,1)}, u32[]{:S(2)}) copy-start(bf16[32,144]{1,0:T(8,128)(2,1)} %param.15) | copy-start | bytes 27652
  3.1 9.8 %copy-start.6 = (bf16[24,64]{1,0:T(8,128)(2,1)S(1)}, bf16[24,64]{1,0:T(8,128)(2,1)}, u32[]{:S(2)}) copy-start(bf16[24,64]{1,0:T(8,128)(2,1)} %param.16) | copy-start | bytes 9220
  4.1 23.5 %collective-permute-start = (bf16[7,32,1152]{2,1,0:T(8,128)(2,1)S(1)}, bf16[7,32,1152]{2,1,0:T(8,128)(2,1)S(1)}, u32[]{:S(2)}, u32[]{:S(2)}) collective-permute-start(bf16[7,32,1152]{2,1,0:T(8,128)(2,1)S(1)} %pad_maximum_fusion.1), channel_id=1, source_target_pairs={{0,496},{16,0},{32,16},{48,32},{64,48},{80,64},{96,80},{112,96},{1... | collective-permute-start | bytes 1548296 | tf_op jit(solution)/shard_map/ppermute | solution.py:382
  13.0 12.0 %copy-start.7 = (s32[1,2]{1,0:T(1,128)S(1)}, s32[1,2]{1,0:T(1,128)}, u32[]{:S(2)}) copy-start(s32[1,2]{1,0:T(1,128)} %param.19) | copy-start | bytes 28
  14.0 55.8 %all-to-all-start = ((bf16[64,48,128]{2,1,0:T(8,128)(2,1)}), bf16[64,48,128]{2,1,0:T(8,128)(2,1)S(1)}, u32[]{:S(2)}, u32[]{:S(2)}) async-start(bf16[64,48,128]{2,1,0:T(8,128)(2,1)} %broadcast_in_dim.18), calls=%async_computation | async-start | bytes 1572864 | tf_op jit(solution)/shard_map/all_to_all | solution.py:372
  27.9 20.9 %collective-permute-start.1 = (bf16[8,8,1152]{2,1,0:T(8,128)(2,1)S(1)}, bf16[8,8,1152]{2,1,0:T(8,128)(2,1)S(1)}, u32[]{:S(2)}, u32[]{:S(2)}) collective-permute-start(bf16[8,8,1152]{2,1,0:T(8,128)(2,1)S(1)} %slice.145), channel_id=1, source_target_pairs={{0,14},{2,0},{4,2},{6,4},{8,6},{10,8},{12,10},{14,12},{1,15},{3,1}... | collective-permute-start | bytes 442376 | tf_op jit(solution)/shard_map/ppermute | solution.py:382
  49.2 16.4 %collective-permute-start.2 = (bf16[256,1152]{1,0:T(8,128)(2,1)S(1)}, bf16[256,1152]{1,0:T(8,128)(2,1)S(1)}, u32[]{:S(2)}, u32[]{:S(2)}) collective-permute-start(bf16[256,1152]{1,0:T(8,128)(2,1)S(1)} %bitcast.132), channel_id=1, source_target_pairs={{0,2},{2,0},{4,6},{6,4},{8,10},{10,8},{12,14},{14,12},{1,3},{3,1},... | collective-permute-start | bytes 1769480 | tf_op jit(solution)/shard_map/ppermute | solution.py:387
  66.7 21.2 %collective-permute-start.3 = (bf16[512,1152]{1,0:T(8,128)(2,1)}, bf16[512,1152]{1,0:T(8,128)(2,1)}, u32[]{:S(2)}, u32[]{:S(2)}) collective-permute-start(bf16[512,1152]{1,0:T(8,128)(2,1)} %pad_maximum_fusion.two), channel_id=1, source_target_pairs={{0,16},{16,0},{1,17},{17,1},{2,18},{18,2},{3,19},{19,3},{4,20},{20... | collective-permute-start | bytes 3538952 | tf_op jit(solution)/shard_map/ppermute | solution.py:387
  77.8 5.7 %copy-start.4 = (s32[64,64]{1,0:T(8,128)S(1)}, s32[64,64]{1,0:T(8,128)}, u32[]{:S(2)}) copy-start(s32[64,64]{1,0:T(8,128)} %param.18) | copy-start | bytes 49156
  77.8 24.5 %all-to-all-start.1 = ((bf16[8,128,768]{2,1,0:T(8,128)(2,1)}), bf16[8,128,768]{2,1,0:T(8,128)(2,1)S(1)}, u32[]{:S(2)}, u32[]{:S(2)}) async-start(bf16[8,128,768]{2,1,0:T(8,128)(2,1)} %bitcast.38), calls=%async_computation.1 | async-start | bytes 3145728 | tf_op jit(solution)/shard_map/all_to_all | solution.py:372
  81.7 4.9 %copy-start.3 = (bf16[48,1024]{1,0:T(8,128)(2,1)S(1)}, bf16[48,1024]{1,0:T(8,128)(2,1)}, u32[]{:S(2)}) copy-start(bf16[48,1024]{1,0:T(8,128)(2,1)} %param.12) | copy-start | bytes 294916
  102.3 1.1 copy-start.2
  112.2 14.7 %all-to-all-start.2 = ((bf16[8,24,1024]{2,1,0:T(8,128)(2,1)}), bf16[8,24,1024]{2,1,0:T(8,128)(2,1)S(1)}, u32[]{:S(2)}, u32[]{:S(2)}) async-start(bf16[8,24,1024]{2,1,0:T(8,128)(2,1)} %bitcast.143), calls=%async_computation.2 | async-start | bytes 786432 | tf_op jit(solution)/shard_map/all_to_all | solution.py:372
  128.5 15.4 %all-to-all-start.3 = ((bf16[8,96,128]{2,1,0:T(8,128)(2,1)}), bf16[8,96,128]{2,1,0:T(8,128)(2,1)S(1)}, u32[]{:S(2)}, u32[]{:S(2)}) async-start(bf16[8,96,128]{2,1,0:T(8,128)(2,1)} %bitcast.47), calls=%async_computation.3 | async-start | bytes 393216 | tf_op jit(solution)/shard_map/all_to_all | solution.py:372
  160.9 8.3 %collective-permute-start.4 = (f32[16,128]{1,0:T(8,128)S(1)}, f32[16,128]{1,0:T(8,128)S(1)}, u32[]{:S(2)}, u32[]{:S(2)}) collective-permute-start(f32[16,128]{1,0:T(8,128)S(1)} %convert_reduce_fusion), channel_id=1, source_target_pairs={{0,1},{1,0},{2,3},{3,2},{4,5},{5,4},{6,7},{7,6},{8,9},{9,8},{10,11... | collective-permute-start | bytes 24584 | tf_op jit(solution)/shard_map/ppermute | solution.py:387
  182.6 14.9 %all-to-all-start.6 = ((bf16[32,16,128]{2,1,0:T(8,128)(2,1)}), bf16[32,16,128]{2,1,0:T(8,128)(2,1)S(1)}, u32[]{:S(2)}, u32[]{:S(2)}) async-start(bf16[32,16,128]{2,1,0:T(8,128)(2,1)} %broadcast_in_dim.23), calls=%async_computation.6 | async-start | bytes 262144 | tf_op jit(solution)/shard_map/all_to_all | solution.py:372

commit v7 on v6

--- a/solution.py
+++ b/solution.py
@@ -67,11 +67,11 @@
             cols = slice(tile * LANES, (tile + 1) * LANES)
             tall = arrived[source, tile * 16 : (tile + 1) * 16, QKV:]
             wide[at : at + 16, cols] = tall.astype(jnp.float32)
-            low = [
-                arrived[source, i * 64 + tile * 8 : i * 64 + tile * 8 + 8, QKV - 64 : QKV]
-                for i in range(2)
-            ]
-            wide[at + 16 : at + 24, cols] = jnp.concatenate(low, axis=1).astype(jnp.float32)
+            for i in range(2):
+                low = arrived[source, i * 64 + tile * 8 : i * 64 + tile * 8 + 8, QKV - 64 : QKV]
+                low = low.astype(jnp.float32)
+                low = jnp.concatenate([low[:4], low[4:]], axis=1)
+                wide[at + 16 + 4 * i : at + 20 + 4 * i, cols] = low
     out[...] = wide[...].astype(jnp.bfloat16)
 
 
@@ -363,7 +363,6 @@
 
 ROW = ("yl", "x", "core")
 COL = ("col", "dp")
-RING = ("yl", "dp")
 CHIP_ROW = ("x", "core")
 FAR = ("yl", "col", "dp")
 
@@ -406,37 +405,82 @@
     return lax.dynamic_slice_in_dim(joined, offset, own.shape[dim], dim)
 
 
-def pack_out(rows):
-    tall = rows[:16].reshape(16, 8, LANES).transpose(1, 0, 2).reshape(LANES, LANES)
-    low = rows[16:].reshape(8, 8, LANES).transpose(1, 0, 2).reshape(64, 2, 64)
-    return jnp.concatenate([low.transpose(1, 0, 2).reshape(LANES, 64), tall], axis=1)
-
-
-def gather_weights(qkv_weight, out_weight, half):
-    split = qkv_weight.size // LANES
-    line = jnp.concatenate([qkv_weight.reshape(-1, LANES), out_weight.reshape(-1, LANES)])
+UNIT = 16
+
+
+def runs_of(units):
+    runs = []
+    for unit in units:
+        shard, i = divmod(unit, 9)
+        source = ("rest", 0) if i == 8 else ("main", shard)
+        start = shard * UNIT if i == 8 else i * UNIT
+        if runs and runs[-1][0] == source and runs[-1][2] == start:
+            runs[-1][2] += UNIT
+        else:
+            runs.append([source, start, start + UNIT])
+    return runs
+
+
+def deal_kernel(lines, rest, out):
+    groups = 4
+    shards = lines.shape[0] // 4
+
+    def part(source, start, end):
+        if source[0] == "rest":
+            return rest[:, start:end]
+        rows = [lines[band * shards + source[1], 0:32, start:end] for band in range(4)]
+        return jnp.concatenate(rows, axis=0)
+
+    def columns(units):
+        return [part(*run) for run in runs_of(units)]
+
+    for group in range(groups):
+        first = [48 * t + 12 * group for t in range(3)]
+        tiles = [columns(range(u, u + 8)) for u in first]
+        tiles.append(columns(range(first[0] + 8, first[0] + 12)))
+        tiles[-1] += columns(range(first[1] + 8, first[1] + 12))
+        low = jnp.concatenate(
+            [lines[group * shards + shard, 44:48, :].astype(jnp.float32) for shard in range(shards)]
+        )
+        low = jnp.concatenate([low[:, :HEAD], low[:, HEAD:]], axis=0).astype(jnp.bfloat16)
+        tiles.append(columns(range(first[2] + 8, first[2] + 12)) + [low])
+        tall = []
+        for shard in range(0, shards, 2):
+            left = lines[group * shards + shard, 36:44, :].astype(jnp.float32)
+            right = lines[group * shards + shard + 1, 36:44, :].astype(jnp.float32)
+            tall.append(jnp.concatenate([left[:, :HEAD], right[:, :HEAD]], axis=1))
+            tall.append(jnp.concatenate([left[:, HEAD:], right[:, HEAD:]], axis=1))
+        tiles.append([jnp.concatenate(tall, axis=0).astype(jnp.bfloat16)])
+        for i, pieces in enumerate(tiles):
+            tile = pieces[0] if len(pieces) == 1 else jnp.concatenate(pieces, axis=1)
+            for copy in range(out.shape[0] // groups):
+                out[copy * groups + group, :, i * LANES : (i + 1) * LANES] = tile
+
+
+def deal(lines, rest, count):
+    return call(
+        deal_kernel, STEP,
+        [whole(lines.shape), whole(rest.shape)],
+        whole((count, LANES, QKV + LANES)),
+        jax.ShapeDtypeStruct((count, LANES, QKV + LANES), jnp.bfloat16),
+        [],
+        1 << 30,
+    )(lines, rest)
+
+
+def gather_weights(qkv_weight, out_weight):
+    rows_w = qkv_weight.shape[0]
+    last = qkv_weight[:, LANES:].reshape(-1, LANES)
+    high = jnp.concatenate([out_weight[:8], out_weight[8:16]], axis=1)
+    low = jnp.concatenate([out_weight[16:20], out_weight[20:]], axis=1)
+    line = jnp.concatenate([qkv_weight[:, :LANES], last, high, low])
     lines = spread(line, FAR)
     bands = lax.axis_size("yl")
-    cols = lines.shape[0] // bands
-    rows_w, rows_o = qkv_weight.shape[0], out_weight.shape[0]
-    qkv = lines[:, :split].reshape(bands, cols, *qkv_weight.shape).transpose(0, 2, 1, 3)
-    qkv = qkv.reshape(bands * rows_w, 3, -1)
-    out = lines[:, split:].reshape(bands, cols, *out_weight.shape).transpose(0, 2, 1, 3)
-    out = out.reshape(bands, rows_o, -1)
-    features = qkv.shape[2]
-    mine = lax.dynamic_slice_in_dim(qkv, half * (features // 2), features // 2, 2)
-    out = lax.dynamic_slice_in_dim(out, half * 2, 2, 0)
-    group = features // 4
-    blocks = []
-    for core in range(2):
-        part = mine[:, :, core * group : (core + 1) * group]
-        pieces = [part[:, i, :LANES] for i in range(3)] + [part[:, i, LANES:] for i in range(3)]
-        blocks.append(jnp.concatenate([*pieces, pack_out(out[core])], axis=1))
-    both = jnp.stack(blocks)
-    chips = lax.axis_size("x")
-    sent = jnp.broadcast_to(both[None], (chips, *both.shape)).reshape(2 * chips, *both.shape[1:])
-    arrived = exchange(sent, CHIP_ROW)
-    return arrived
+    count = lines.shape[0] // bands
+    rest = lines[:, rows_w : rows_w + last.shape[0]].reshape(bands, count, rows_w, UNIT)
+    rest = rest.transpose(0, 2, 1, 3).reshape(bands * rows_w, count * UNIT)
+    sent = deal(lines, rest, lax.axis_size(CHIP_ROW))
+    return exchange(sent, CHIP_ROW)
 
 
 def on_device(
@@ -459,27 +503,26 @@
     grid_cols = cols_dev * lax.axis_size("col")
     row_shift, col_shift = shifts[0, 0], shifts[0, 1]
     row_at, col_at, core = lax.axis_index(ROW), lax.axis_index("col"), lax.axis_index("core")
-    half = col_at % 2
-    group = 2 * half + core
+    group = 2 * (lax.axis_index("x") % 2) + core
 
     depth = embed_weight.shape[0]
     patches = make_patches(pixels)
     patches = jnp.pad(patches, ((0, 0), (0, 0), (0, LANES - depth)))
     block = jnp.concatenate([cotangent, patches], axis=-1)
+    beside = from_behind(block[:, :WIN], "col")
+    block = splice_after(block, beside, col_shift, 1)
     below = from_behind(block[: WIN - 1], ROW)
-    block = splice_after(block, below, row_shift, 0)
-    block = splice_after(block, from_behind(block[:, :WIN], "col"), col_shift, 1)
-    own = window_split(block)
-    arrived = gather_weights(qkv_weight, out_weight, half)
-    beside = swap(own, "col")
+    own = window_split(splice_after(block, below, row_shift, 0))
+    arrived = gather_weights(qkv_weight, out_weight)
+    beside = swap(own, "x")
     two = jnp.concatenate([own, beside])
     other = swap(two, "core")
     cells = 2 * two.shape[0]
 
     labels = []
-    for row_flip, col_flip in ((0, 0), (0, 1), (1, 0), (1, 1)):
+    for row_flip in (0, 2, 1, 3):
         row_ids = (row_at ^ row_flip) * rows_dev + jnp.arange(rows_dev, dtype=jnp.int32)
-        col_ids = (col_at ^ col_flip) * cols_dev + jnp.arange(cols_dev, dtype=jnp.int32)
+        col_ids = col_at * cols_dev + jnp.arange(cols_dev, dtype=jnp.int32)
         row_part = (row_ids >= grid_rows - row_shift).astype(jnp.int32)
         col_part = (col_ids >= grid_cols - col_shift).astype(jnp.int32)
         region = 2 * row_part[:, None] + col_part[None, :]
@@ -500,15 +543,8 @@
     count = lax.axis_size(CHIP_ROW)
     held = exchange(out_grad.reshape(count, -1, width), CHIP_ROW)
     dproj, table_part = run_scores(two, other, proj, prob, arrived, width)
-    held = held.reshape(count // 2, 2, -1, width).astype(jnp.float32).sum(axis=0)
-    held = held.astype(jnp.bfloat16)
-    rows_o, deep = held.shape[1], lax.axis_size("col")
-    ring = lax.axis_size(RING)
-    held = held.reshape(2, rows_o, deep, ring // 4, -1).transpose(0, 3, 2, 1, 4)
-    held = held.reshape(2, ring // 4, -1, LANES)
-    none = jnp.zeros_like(held)
-    bands = jnp.concatenate([jnp.where(half == i, held, none) for i in range(2)])
-    bands = exchange(bands.reshape(ring, -1, LANES), RING)
+    held = held.reshape(2, count // 2, -1, width).astype(jnp.float32).sum(axis=0)
+    bands = exchange(held.astype(jnp.bfloat16), "yl")
     line = run_norm(two, other, dproj, xhat, inv, gain, arrived)
     my_grad = jnp.dot(table_part.reshape(heads, -1), selector, precision=lax.Precision.HIGHEST)
     wide = 256
@@ -524,14 +560,14 @@
     tiles = line.reshape(tall // 8, 8, width // LANES, LANES).transpose(0, 2, 1, 3)
     tiles = tiles.reshape(chunks, -1, LANES)
     mine = exchange(tiles, ROW)
-    mine = mine.astype(jnp.float32).sum(axis=0)
-    mine = mine + swap(mine, "dp")
-    mine = mine.astype(jnp.bfloat16)
+    mine = mine.astype(jnp.float32).sum(axis=0).astype(jnp.bfloat16)
+    rows_o = bands.shape[1]
     bands = bands.astype(jnp.float32).sum(axis=0).astype(jnp.bfloat16)
-    bands = bands.reshape(deep, -1, LANES)
+    spans = lax.axis_size(COL)
+    bands = bands.reshape(rows_o, spans, -1).transpose(1, 0, 2).reshape(spans, -1, LANES)
     held = mine.shape[0]
-    mine = jnp.broadcast_to(mine[None], (deep, held, LANES))
-    both = exchange(jnp.concatenate([mine, bands], axis=1), "col")
+    mine = jnp.broadcast_to(mine[None], (spans, held, LANES))
+    both = exchange(jnp.concatenate([mine, bands], axis=1), COL)
     both = both.astype(jnp.float32).sum(axis=0)
     out_weight_grad = both[held:].reshape(rows_o, -1)
     total = spread(both[:held].astype(jnp.bfloat16), ROW)

time: 201 us -> 182 us (0.905)
  waiting for transfers between devices: 49.2 us -> 37.1 us
  blocking collectives: 29.6 us -> 19.5 us
  starting transfers between devices: 53.9 us -> 62.1 us
  local copies, waits for them, and re-layouts: 22.5 us -> 15.8 us
  Pallas kernels: 30.8 us -> 33.6 us
    ppermute x2, waiting for transfers between devices: 14.8 us -> 0.01 us  [from_behind(): lax.ppermute(value, axis, [(source, (source - 1) % count) for source in r...]
    all_to_all x2 -> x1, blocking collectives: 29.6 us -> 19.5 us  [exchange(): return lax.all_to_all(blocks, axis, split_axis=0, concat_axis=0, tiled=True)]
    all_to_all x5 -> x6, starting transfers between devices: 30.8 us -> 40.1 us  [exchange(): return lax.all_to_all(blocks, axis, split_axis=0, concat_axis=0, tiled=True)]
    all_to_all x5 -> x6, waiting for transfers between devices: 16.8 us -> 24.9 us  [exchange(): return lax.all_to_all(blocks, axis, split_axis=0, concat_axis=0, tiled=True)]
    ppermute x3 -> x2, waiting for transfers between devices: 17.5 us -> 12.2 us  [swap(): lax.ppermute(value, axis, [(source, source ^ 1) for source in range(count)])]
    ppermute x3 -> x2, starting transfers between devices: 10.2 us -> 7.36 us  [swap(): lax.ppermute(value, axis, [(source, source ^ 1) for source in range(count)])]
    pallas_call x0 -> x1, Pallas kernels: none -> 2.74 us  [deal(): call(deal_kernel, STEP, [whole(lines.shape), whole(rest.shape)], whole((c...]
    reshape x9 -> x6, local copies, waits for them, and re-layouts: 4.29 us -> 1.59 us  [the longest x2 0.91 us: gather_weights(): rest = rest.transpose(0, 2, 1, 3).reshape(bands * rows_w, count * UNIT)]
  transfers between devices with their start and end apart: 10 -> 10, of which waited for: 5 -> 4; matrix products, arithmetic and copies ran while one was open for 10% -> 7% of each run, Pallas kernels for 11% -> 14%
where the time goes in v7:
time: 182 us; the launch traced here: 181 us
  starting transfers between devices  62.1 us (34%)
  waiting for transfers between devices  37.1 us (20%)
  Pallas kernels  33.6 us (18%)
  blocking collectives  19.5 us (11%)
  local copies, waits for them, and re-layouts  15.8 us (9%)
  between operations  6.32 us (3%)
  matrix products  3.59 us (2%)
  other arithmetic  2.52 us (1%)
    all_to_all x6, starting transfers between devices, exchange(): return lax.all_to_all(blocks, axis, split_axis=0, concat_axis=0, tiled=True)  40.1 us
    all_to_all x6, waiting for transfers between devices, exchange(): return lax.all_to_all(blocks, axis, split_axis=0, concat_axis=0, tiled=True)  24.9 us
    all_to_all x1, blocking collectives, exchange(): return lax.all_to_all(blocks, axis, split_axis=0, concat_axis=0, tiled=True)  19.5 us
    ppermute x2, starting transfers between devices, from_behind(): lax.ppermute(value, axis, [(source, (source - 1) % count) for source in r...  14.7 us
    ppermute x2, waiting for transfers between devices, swap(): lax.ppermute(value, axis, [(source, source ^ 1) for source in range(count)])  12.2 us
    pallas_call x1, Pallas kernels, run_forward(): call(forward_kernel, cells, [*cell_specs(width), stepped((STEP, width)),...  8.85 us
    pallas_call x1, Pallas kernels, run_norm(): call(norm_kernel, cells, [*cell_specs(two.shape[1]), stepped((STEP, QKV))...  8.72 us
    pallas_call x1, Pallas kernels, run_scores(): call(scores_kernel, cells, [*cell_specs(width), stepped((STEP, QKV)), ste...  7.8 us
  transfers between devices with their start and end apart: 10, of which 4 were waited for; matrix products, arithmetic and copies ran while one was open for 7% of the time, Pallas kernels for 14%

profile of v7, /device:TPU:1, one launch (start us, length us, event | category | flops | bytes accessed | tf_op | source)
XLA Modules:
  0.0 180.6 jit_solution(3000177369145059368)
XLA Ops:
  0.7 2.5 %reshape_squeeze.3 = bf16[3,8,4,32,4]{4,3,2,1,0:T(8,128)(2,1)S(1)} reshape(bf16[1,3,32,128]{3,2,1,0:T(8,128)(2,1)} %param.10) | data formatting | bytes 49152 | tf_op jit(solution)/shard_map/reshape;squeeze | solution.py:393
  3.2 0.7 copy.37
  3.8 0.1 copy.44
  4.0 11.5 %collective-permute-start = (bf16[8,8,1152]{2,1,0:T(8,128)(2,1)S(1)}, bf16[8,8,1152]{2,1,0:T(8,128)(2,1)S(1)}, u32[]{:S(2)}, u32[]{:S(2)}) collective-permute-start(bf16[8,8,1152]{2,1,0:T(8,128)(2,1)S(1)} %pad_maximum_fusion.1), channel_id=1, source_target_pairs={{0,14},{2,0},{4,2},{6,4},{8,6},{10,8},{12,10},{14,12},{1,15},{3,1}... | collective-permute-start | bytes 442376 | tf_op jit(solution)/shard_map/ppermute | solution.py:381
  15.5 0.6 fusion.20
  18.2 0.4 fusion.5
  18.7 3.2 %collective-permute-start.1 = (bf16[7,32,1152]{2,1,0:T(8,128)(2,1)S(1)}, bf16[7,32,1152]{2,1,0:T(8,128)(2,1)S(1)}, u32[]{:S(2)}, u32[]{:S(2)}) collective-permute-start(bf16[7,32,1152]{2,1,0:T(8,128)(2,1)S(1)} %slice.77), channel_id=1, source_target_pairs={{0,496},{16,0},{32,16},{48,32},{64,48},{80,64},{96,80},{112,96},{1... | collective-permute-start | bytes 1548296 | tf_op jit(solution)/shard_map/ppermute | solution.py:381
  22.0 1.0 broadcast_in_dim.14
  23.0 11.0 %all-to-all-start = ((bf16[64,48,128]{2,1,0:T(8,128)(2,1)}), bf16[64,48,128]{2,1,0:T(8,128)(2,1)S(1)}, u32[]{:S(2)}, u32[]{:S(2)}) async-start(bf16[64,48,128]{2,1,0:T(8,128)(2,1)} %broadcast_in_dim.14), calls=%async_computation | async-start | bytes 1572864 | tf_op jit(solution)/shard_map/all_to_all | solution.py:371
  35.9 0.2 fusion.7
  36.3 3.1 %collective-permute-start.2 = (bf16[256,1152]{1,0:T(8,128)(2,1)S(1)}, bf16[256,1152]{1,0:T(8,128)(2,1)S(1)}, u32[]{:S(2)}, u32[]{:S(2)}) collective-permute-start(bf16[256,1152]{1,0:T(8,128)(2,1)S(1)} %bitcast.63), channel_id=1, source_target_pairs={{0,32},{32,0},{64,96},{96,64},{1,33},{33,1},{65,97},{97,65},{2,34}... | collective-permute-start | bytes 1769480 | tf_op jit(solution)/shard_map/ppermute | solution.py:386
  39.4 12.2 %collective-permute-done.2 = bf16[256,1152]{1,0:T(8,128)(2,1)S(1)} collective-permute-done((bf16[256,1152]{1,0:T(8,128)(2,1)S(1)}, bf16[256,1152]{1,0:T(8,128)(2,1)S(1)}, u32[]{:S(2)}, u32[]{:S(2)}) %collective-permute-start.2) | collective-permute-done | bytes 589856 | tf_op jit(solution)/shard_map/ppermute | solution.py:386
  51.7 4.2 %collective-permute-start.3 = (bf16[512,1152]{1,0:T(8,128)(2,1)S(1)}, bf16[512,1152]{1,0:T(8,128)(2,1)}, u32[]{:S(2)}, u32[]{:S(2)}) collective-permute-start(bf16[512,1152]{1,0:T(8,128)(2,1)S(1)} %pad_maximum_fusion.two), channel_id=1, source_target_pairs={{0,16},{16,0},{1,17},{17,1},{2,18},{18,2},{3,19},{19,3},{4,20},{20... | collective-permute-start | bytes 3538952 | tf_op jit(solution)/shard_map/ppermute | solution.py:386
  56.0 0.4 reshape.197
  56.3 0.3 copy.40
  56.6 0.2 reshape.198
  56.8 0.7 copy.41.rest
  57.5 2.7 %shard_map.138 = bf16[8,128,768]{2,1,0:T(8,128)(2,1)} custom-call(bf16[64,48,128]{2,1,0:T(8,128)(2,1)} %copy-done.4, bf16[128,256]{1,0:T(8,128)(2,1)} %copy.41.rest), custom_call_target="tpu_custom_call" | custom-call | flops 1073741824 | bytes 8388608 | tf_op jit(solution)/shard_map/pallas_call | solution.py:461
  60.3 8.0 %all-to-all-start.1 = ((bf16[8,128,768]{2,1,0:T(8,128)(2,1)}), bf16[8,128,768]{2,1,0:T(8,128)(2,1)S(1)}, u32[]{:S(2)}, u32[]{:S(2)}) async-start(bf16[8,128,768]{2,1,0:T(8,128)(2,1)} %shard_map.138), calls=%async_computation.1 | async-start | bytes 3145728 | tf_op jit(solution)/shard_map/all_to_all | solution.py:371
  70.2 2.2 %fusion.1 = f32[3,4096]{1,0:T(4,128)S(1)} fusion(s32[4096]{0:T(1024)S(1)} %eq.17, f32[12,225]{1,0:T(8,128)S(1)} %copy-done, s32[]{:T(128)S(6)} %select_n.26), kind=kOutput, calls=%fused_computation.2 | convolution fusion | flops 34099200 | bytes 69636 | tf_op jit(solution)/shard_map/dot_general | solution.py:536
  72.4 0.8 reshape.199.bias
  73.2 0.7 pad.13.embed_w
  73.9 0.6 fusion.11.label
  74.5 5.5 %shard_map.137 = (bf16[1024,1024]{1,0:T(8,128)(2,1)}, f32[1024,1024]{1,0:T(8,128)}, f32[1024,128]{1,0:T(8,128)}) custom-call(bf16[512,1152]{1,0:T(8,128)(2,1)} %copy-done.3, bf16[512,1152]{1,0:T(8,128)(2,1)} %collective-permute-done.3.other, bf16[128,1024]{1,0:T(8,128)(2,1)} %pad.13.embed_w, f32[1,1024]{1,0:T(1,128)} %bitcast.77, f32[1,1024]{1,0:T(1,128)} %bitcast.78), custom_call_target="tpu_custom_call" | custom-call | flops 2147483648 | bytes 8388608 | tf_op jit(solution)/shard_map/pallas_call | solution.py:271
  80.0 8.8 %all-to-all-done.1.arrived = bf16[8,128,768]{2,1,0:T(8,128)(2,1)S(1)} async-done(((bf16[8,128,768]{2,1,0:T(8,128)(2,1)}), bf16[8,128,768]{2,1,0:T(8,128)(2,1)S(1)}, u32[]{:S(2)}, u32[]{:S(2)}) %all-to-all-start.1) | async-done | bytes 1572896 | tf_op jit(solution)/shard_map/all_to_all | solution.py:371
  88.9 1.2 copy-done.2
  90.0 8.8 %shard_map.139 = (bf16[1024,640]{1,0:T(8,128)(2,1)}, f32[8,3,128,128]{3,2,1,0:T(8,128)}, bf16[192,1024]{1,0:T(8,128)(2,1)}) custom-call(bf16[512,1152]{1,0:T(8,128)(2,1)} %copy-done.3, bf16[512,1152]{1,0:T(8,128)(2,1)} %collective-permute-done.3.other, bf16[1024,1024]{1,0:T(8,128)(2,1)} %get-tuple-element.15.normed, bf16[8,128,768]{2,1,0:T(8,128)(2,1)} %copy-done.2, ...), custom_call_target="tpu_custom_call" | custom-call | flops 4294967296 | bytes 8388608 | tf_op jit(solution)/shard_map/pallas_call | solution.py:294
  98.9 4.3 %all-to-all-start.2 = ((bf16[8,24,1024]{2,1,0:T(8,128)(2,1)}), bf16[8,24,1024]{2,1,0:T(8,128)(2,1)S(1)}, u32[]{:S(2)}, u32[]{:S(2)}) async-start(bf16[8,24,1024]{2,1,0:T(8,128)(2,1)} %bitcast.70), calls=%async_computation.2 | async-start | bytes 786432 | tf_op jit(solution)/shard_map/all_to_all | solution.py:371
  103.2 7.8 %shard_map.140 = (bf16[1024,640]{1,0:T(8,128)(2,1)}, f32[3,64,64]{2,1,0:T(8,128)}) custom-call(bf16[512,1152]{1,0:T(8,128)(2,1)} %copy-done.3, bf16[512,1152]{1,0:T(8,128)(2,1)} %collective-permute-done.3.other, bf16[1024,640]{1,0:T(8,128)(2,1)} %get-tuple-element.16.proj, f32[8,3,128,128]{3,2,1,0:T(8,128)} %get-tuple-element.17.prob_in, ...), custom_call_target="tpu_custom_call" | custom-call | flops 4294967296 | bytes 8388608 | tf_op jit(solution)/shard_map/pallas_call | solution.py:324
  111.0 1.0 reshape.200
  112.0 1.4 fusion
  113.5 0.1 dynamic_update_slice.6
  113.6 0.8 reduce_sum.45
  114.4 3.5 %all-to-all-start.3 = ((bf16[4,24,1024]{2,1,0:T(8,128)(2,1)}), bf16[4,24,1024]{2,1,0:T(8,128)(2,1)S(1)}, u32[]{:S(2)}, u32[]{:S(2)}) async-start(bf16[4,24,1024]{2,1,0:T(8,128)(2,1)} %reduce_sum.45), calls=%async_computation.3 | async-start | bytes 393216 | tf_op jit(solution)/shard_map/all_to_all | solution.py:371
  118.0 8.7 %shard_map.141 = bf16[64,1024]{1,0:T(8,128)(2,1)} custom-call(bf16[512,1152]{1,0:T(8,128)(2,1)} %copy-done.3, bf16[512,1152]{1,0:T(8,128)(2,1)} %collective-permute-done.3.other, bf16[1024,640]{1,0:T(8,128)(2,1)} %get-tuple-element.18.dproj, f32[1024,1024]{1,0:T(8,128)} %get-tuple-element.19.xhat, f32[1024,128]{1,0:T(8,128)} %get-tuple-element.20.inv, ...), custom_call_target="tpu_custom_call" | custom-call | flops 4294967296 | bytes 8388608 | tf_op jit(solution)/shard_map/pallas_call | solution.py:347
  126.7 1.4 dynamic_update_slice.7
  128.0 8.0 %all-to-all-start.4 = ((bf16[32,16,128]{2,1,0:T(8,128)(2,1)}), bf16[32,16,128]{2,1,0:T(8,128)(2,1)S(1)}, u32[]{:S(2)}, u32[]{:S(2)}) async-start(bf16[32,16,128]{2,1,0:T(8,128)(2,1)} %bitcast.73), calls=%async_computation.4 | async-start | bytes 262144 | tf_op jit(solution)/shard_map/all_to_all | solution.py:371
  136.1 0.1 reshape.206
  136.3 0.1 reshape.207
  136.4 8.2 %all-to-all-done.4 = bf16[32,16,128]{2,1,0:T(8,128)(2,1)S(1)} async-done(((bf16[32,16,128]{2,1,0:T(8,128)(2,1)}), bf16[32,16,128]{2,1,0:T(8,128)(2,1)S(1)}, u32[]{:S(2)}, u32[]{:S(2)}) %all-to-all-start.4) | async-done | bytes 131104 | tf_op jit(solution)/shard_map/all_to_all | solution.py:371
  144.7 19.5 %all_to_all.35 = bf16[16,28,128]{2,1,0:T(8,128)(2,1)S(1)} all-to-all(bf16[16,28,128]{2,1,0:T(8,128)(2,1)S(1)} %pad_maximum_fusion.2), channel_id=1, replica_groups=mesh['yl'=4,'x'=4,'core'=2,'col'=8,'dp'=2] {'col','dp'}, dimensions={0} | all-to-all | bytes 229376 | tf_op jit(solution)/shard_map/all_to_all | solution.py:371
  164.2 0.7 broadcast_in_dim.17
  164.9 5.2 %all-to-all-start.6 = ((bf16[32,16,128]{2,1,0:T(8,128)(2,1)}), bf16[32,16,128]{2,1,0:T(8,128)(2,1)S(1)}, u32[]{:S(2)}, u32[]{:S(2)}) async-start(bf16[32,16,128]{2,1,0:T(8,128)(2,1)} %broadcast_in_dim.17), calls=%async_computation.6 | async-start | bytes 262144 | tf_op jit(solution)/shard_map/all_to_all | solution.py:371
  170.1 0.7 reshape.208
  170.7 7.8 %all-to-all-done.6 = bf16[32,16,128]{2,1,0:T(8,128)(2,1)S(1)} async-done(((bf16[32,16,128]{2,1,0:T(8,128)(2,1)}), bf16[32,16,128]{2,1,0:T(8,128)(2,1)S(1)}, u32[]{:S(2)}, u32[]{:S(2)}) %all-to-all-start.6) | async-done | bytes 131104 | tf_op jit(solution)/shard_map/all_to_all | solution.py:371
  178.6 0.6 fusion.17
  179.3 0.7 slice_bitcast_fusion
  179.9 0.6 reshape.209
  (59 shorter events, 1.3 us)
Async XLA Ops:
  0.6 69.6 %copy-start = (f32[12,225]{1,0:T(8,128)S(1)}, f32[12,225]{1,0:T(8,128)}, u32[]{:S(2)}) copy-start(f32[12,225]{1,0:T(8,128)} %param.17) | copy-start | bytes 32404
  0.6 3.4 %copy-start.1 = (bf16[1,8,32,1024]{3,2,1,0:T(8,128)(2,1)S(1)}, bf16[1,8,32,1024]{3,2,1,0:T(8,128)(2,1)}, u32[]{:S(2)}) copy-start(bf16[1,8,32,1024]{3,2,1,0:T(8,128)(2,1)} %param.11) | copy-start | bytes 1572868
  0.7 16.8 %slice-start = ((bf16[32,144]{1,0:T(8,128)(2,1)}), bf16[32,16]{1,0:T(8,128)(2,1)S(1)}, s32[]{:S(2)}) async-start(bf16[32,144]{1,0:T(8,128)(2,1)} %param.15), calls=%async_computation.7 | async-start | bytes 16384 | tf_op jit(solution)/shard_map/slice | solution.py:473
  0.7 14.9 %copy-start.8 = (s32[1,2]{1,0:T(1,128)S(1)}, s32[1,2]{1,0:T(1,128)}, u32[]{:S(2)}) copy-start(s32[1,2]{1,0:T(1,128)} %param.19) | copy-start | bytes 28
  0.7 16.8 %copy-start.7 = (bf16[24,64]{1,0:T(8,128)(2,1)S(1)}, bf16[24,64]{1,0:T(8,128)(2,1)}, u32[]{:S(2)}) copy-start(bf16[24,64]{1,0:T(8,128)(2,1)} %param.16) | copy-start | bytes 9220
  4.0 17.9 %slice-start.1 = ((bf16[32,144]{1,0:T(8,128)(2,1)}), bf16[32,128]{1,0:T(8,128)(2,1)S(1)}, s32[]{:S(2)}) async-start(bf16[32,144]{1,0:T(8,128)(2,1)} %param.15), calls=%async_computation.8 | async-start | bytes 16384 | tf_op jit(solution)/shard_map/slice | solution.py:476
  4.0 14.2 %collective-permute-start = (bf16[8,8,1152]{2,1,0:T(8,128)(2,1)S(1)}, bf16[8,8,1152]{2,1,0:T(8,128)(2,1)S(1)}, u32[]{:S(2)}, u32[]{:S(2)}) collective-permute-start(bf16[8,8,1152]{2,1,0:T(8,128)(2,1)S(1)} %pad_maximum_fusion.1), channel_id=1, source_target_pairs={{0,14},{2,0},{4,2},{6,4},{8,6},{10,8},{12,10},{14,12},{1,15},{3,1}... | collective-permute-start | bytes 442376 | tf_op jit(solution)/shard_map/ppermute | solution.py:381
  18.7 17.3 %collective-permute-start.1 = (bf16[7,32,1152]{2,1,0:T(8,128)(2,1)S(1)}, bf16[7,32,1152]{2,1,0:T(8,128)(2,1)S(1)}, u32[]{:S(2)}, u32[]{:S(2)}) collective-permute-start(bf16[7,32,1152]{2,1,0:T(8,128)(2,1)S(1)} %slice.77), channel_id=1, source_target_pairs={{0,496},{16,0},{32,16},{48,32},{64,48},{80,64},{96,80},{112,96},{1... | collective-permute-start | bytes 1548296 | tf_op jit(solution)/shard_map/ppermute | solution.py:381
  23.0 32.9 %all-to-all-start = ((bf16[64,48,128]{2,1,0:T(8,128)(2,1)}), bf16[64,48,128]{2,1,0:T(8,128)(2,1)S(1)}, u32[]{:S(2)}, u32[]{:S(2)}) async-start(bf16[64,48,128]{2,1,0:T(8,128)(2,1)} %broadcast_in_dim.14), calls=%async_computation | async-start | bytes 1572864 | tf_op jit(solution)/shard_map/all_to_all | solution.py:371
  36.3 15.3 %collective-permute-start.2 = (bf16[256,1152]{1,0:T(8,128)(2,1)S(1)}, bf16[256,1152]{1,0:T(8,128)(2,1)S(1)}, u32[]{:S(2)}, u32[]{:S(2)}) collective-permute-start(bf16[256,1152]{1,0:T(8,128)(2,1)S(1)} %bitcast.63), channel_id=1, source_target_pairs={{0,32},{32,0},{64,96},{96,64},{1,33},{33,1},{65,97},{97,65},{2,34}... | collective-permute-start | bytes 1769480 | tf_op jit(solution)/shard_map/ppermute | solution.py:386
  51.7 8.6 %copy-start.3 = (bf16[512,1152]{1,0:T(8,128)(2,1)}, bf16[512,1152]{1,0:T(8,128)(2,1)S(1)}, u32[]{:S(2)}) copy-start(bf16[512,1152]{1,0:T(8,128)(2,1)S(1)} %pad_maximum_fusion.two) | copy-start | bytes 3538948
  51.7 22.9 %collective-permute-start.3 = (bf16[512,1152]{1,0:T(8,128)(2,1)S(1)}, bf16[512,1152]{1,0:T(8,128)(2,1)}, u32[]{:S(2)}, u32[]{:S(2)}) collective-permute-start(bf16[512,1152]{1,0:T(8,128)(2,1)S(1)} %pad_maximum_fusion.two), channel_id=1, source_target_pairs={{0,16},{16,0},{1,17},{17,1},{2,18},{18,2},{3,19},{19,3},{4,20},{20... | collective-permute-start | bytes 3538952 | tf_op jit(solution)/shard_map/ppermute | solution.py:386
  56.0 1.6 copy-start.4
  60.3 9.9 %copy-start.6 = (s32[64,64]{1,0:T(8,128)S(1)}, s32[64,64]{1,0:T(8,128)}, u32[]{:S(2)}) copy-start(s32[64,64]{1,0:T(8,128)} %param.18) | copy-start | bytes 49156
  60.3 28.6 %all-to-all-start.1 = ((bf16[8,128,768]{2,1,0:T(8,128)(2,1)}), bf16[8,128,768]{2,1,0:T(8,128)(2,1)S(1)}, u32[]{:S(2)}, u32[]{:S(2)}) async-start(bf16[8,128,768]{2,1,0:T(8,128)(2,1)} %shard_map.138), calls=%async_computation.1 | async-start | bytes 3145728 | tf_op jit(solution)/shard_map/all_to_all | solution.py:371
  68.3 4.9 %copy-start.5 = (bf16[48,1024]{1,0:T(8,128)(2,1)S(1)}, bf16[48,1024]{1,0:T(8,128)(2,1)}, u32[]{:S(2)}) copy-start(bf16[48,1024]{1,0:T(8,128)(2,1)} %param.12) | copy-start | bytes 294916
  88.9 1.2 copy-start.2
  98.9 14.7 %all-to-all-start.2 = ((bf16[8,24,1024]{2,1,0:T(8,128)(2,1)}), bf16[8,24,1024]{2,1,0:T(8,128)(2,1)S(1)}, u32[]{:S(2)}, u32[]{:S(2)}) async-start(bf16[8,24,1024]{2,1,0:T(8,128)(2,1)} %bitcast.70), calls=%async_computation.2 | async-start | bytes 786432 | tf_op jit(solution)/shard_map/all_to_all | solution.py:371
  114.4 13.6 %all-to-all-start.3 = ((bf16[4,24,1024]{2,1,0:T(8,128)(2,1)}), bf16[4,24,1024]{2,1,0:T(8,128)(2,1)S(1)}, u32[]{:S(2)}, u32[]{:S(2)}) async-start(bf16[4,24,1024]{2,1,0:T(8,128)(2,1)} %reduce_sum.45), calls=%async_computation.3 | async-start | bytes 393216 | tf_op jit(solution)/shard_map/all_to_all | solution.py:371
  128.0 16.5 %all-to-all-start.4 = ((bf16[32,16,128]{2,1,0:T(8,128)(2,1)}), bf16[32,16,128]{2,1,0:T(8,128)(2,1)S(1)}, u32[]{:S(2)}, u32[]{:S(2)}) async-start(bf16[32,16,128]{2,1,0:T(8,128)(2,1)} %bitcast.73), calls=%async_computation.4 | async-start | bytes 262144 | tf_op jit(solution)/shard_map/all_to_all | solution.py:371
  164.9 13.7 %all-to-all-start.6 = ((bf16[32,16,128]{2,1,0:T(8,128)(2,1)}), bf16[32,16,128]{2,1,0:T(8,128)(2,1)S(1)}, u32[]{:S(2)}, u32[]{:S(2)}) async-start(bf16[32,16,128]{2,1,0:T(8,128)(2,1)} %broadcast_in_dim.17), calls=%async_computation.6 | async-start | bytes 262144 | tf_op jit(solution)/shard_map/all_to_all | solution.py:371

commit v8 on v7

--- a/solution.py
+++ b/solution.py
@@ -10,7 +10,9 @@
 CELLS = WIN * WIN
 norm_epsilon = 1e-05
 
-STEP = 256
+STEP = 512
+OWN = 256
+HALF = 2 * OWN // STEP
 PAIR = 128
 HEAD = 64
 LANES = 128
@@ -77,7 +79,7 @@
 
 def tokens_kernel(two, other, embed_w, embed_b, gain, normed_out, xhat_out, inv_out):
     step = pl.program_id(0)
-    patches = jnp.where(step < 2, two[...], other[...])
+    patches = jnp.where(step < HALF, two[...], other[...])
     tokens = dot_nn(patches, embed_w[...]) + embed_b[...]
     tokens = tokens.astype(jnp.bfloat16).astype(jnp.float32)
     centered = tokens - jnp.mean(tokens, axis=-1, keepdims=True)
@@ -90,18 +92,19 @@
 
 def forward_kernel(
     two, other, normed, arrived, bias, label,
-    proj_out, prob_out, grad_out, weights, bias_pair, scores, att, grad_acc
+    proj_out, prob_out, grad_out, weights, wo, bias_pair, scores, att, grad_acc, wide_rows
 ):
     step = pl.program_id(0)
 
     @pl.when(step == 0)
     def _():
         assemble(arrived, weights)
+        assemble_out(arrived, wide_rows, wo)
         for head in range(bias.shape[0]):
             row = jnp.concatenate([bias[head], bias[head]], axis=1)
             bias_pair[head] = jnp.concatenate([row, row], axis=0)
 
-    cot = jnp.where(step < 2, two[...], other[...])
+    cot = jnp.where(step < HALF, two[...], other[...])
     proj_out[...] = dot_nn(normed[...], weights[...]).astype(jnp.bfloat16)
     heads = bias.shape[0]
     for pair, rows, q_at, k_at, v_at, at, count in work():
@@ -140,17 +143,16 @@
 
 
 def scores_kernel(
-    two, other, proj, prob_in, arrived, dproj, table_out, wide, wo, table, datt, d_probs, lows
+    two, other, proj, prob_in, wo, dproj, table_out, table, datt, d_probs, lows
 ):
     step = pl.program_id(0)
     heads = prob_in.shape[1]
 
     @pl.when(step == 0)
     def _():
-        assemble_out(arrived, wide, wo)
         table[...] = jnp.zeros_like(table)
 
-    cot = jnp.where(step < 2, two[...], other[...])
+    cot = jnp.where(step < HALF, two[...], other[...])
     datt[...] = dot_nt(cot, wo[...]).astype(jnp.bfloat16)
     dproj[:, QKV - HEAD :] = jnp.zeros((STEP, HEAD), jnp.bfloat16)
     for pair, rows, q_at, k_at, v_at, at, count in work():
@@ -188,24 +190,25 @@
     def _():
         for head in range(heads):
             full = table[head]
-            table_out[head] = full[:CELLS, :CELLS] + full[CELLS:, CELLS:]
+            full = full[:CELLS, :CELLS] + full[CELLS:, CELLS:]
+            for row in range(0, CELLS, 2):
+                pair_row = jnp.concatenate([full[row : row + 1], full[row + 1 : row + 2]], axis=1)
+                table_out[head : head + 1, row * CELLS : (row + 2) * CELLS] = pair_row
 
 
 def norm_kernel(
-    two, other, dproj, xhat, inv, gain, arrived, line_out, weights, dn, branch, embed, bias, gains
+    two, other, own, dproj, xhat, inv, gain, weights, table, line_out, dn, branch, embed, bias, gains
 ):
     step = pl.program_id(0)
     width = gain.shape[1]
     chunk = 32
-    cells = jnp.where(step < 2, two[...], other[...])
-    patches = cells[:, width:]
+    patches = jnp.where(step < HALF, two[...], other[...])
 
     @pl.when(step == 0)
     def _():
-        assemble(arrived, weights)
-        cot = cells[:, :width]
-        embed[...] = dot_tn(patches, cot)
-        bias[...] = cot.astype(jnp.float32).reshape(STEP // 8, 8, width).sum(axis=0)
+        cot = own[...]
+        embed[...] = dot_tn(patches[:OWN], cot)
+        bias[...] = cot.astype(jnp.float32).reshape(OWN // 8, 8, width).sum(axis=0)
         gains[...] = jnp.zeros_like(gains)
 
     dn[...] = dot_nt(dproj[...], weights[...])
@@ -231,7 +234,7 @@
         row = lax.broadcasted_iota(jnp.int32, (16, width), 0)
         sums = jnp.where(row == 0, jnp.sum(bias[...], axis=0, keepdims=True), 0.0)
         sums = jnp.where(row == 1, jnp.sum(gains[...], axis=0, keepdims=True), sums)
-        line_out[depth:, :] = sums.astype(line_out.dtype)
+        line_out[depth:, :] = (sums + table[...]).astype(line_out.dtype)
 
 
 def stepped(shape):
@@ -245,8 +248,8 @@
 
 def cell_specs(width, at=0):
     return [
-        pl.BlockSpec((STEP, width), lambda i: (jnp.minimum(i, 1), at)),
-        pl.BlockSpec((STEP, width), lambda i: (jnp.maximum(i - 2, 0), at)),
+        pl.BlockSpec((STEP, width), lambda i: (jnp.minimum(i, HALF - 1), at)),
+        pl.BlockSpec((STEP, width), lambda i: (jnp.maximum(i - HALF, 0), at)),
     ]
 
 
@@ -259,7 +262,7 @@
         out_shape=out_shape,
         scratch_shapes=scratch,
         compiler_params=pltpu.CompilerParams(
-            dimension_semantics=("arbitrary",), vmem_limit_bytes=56 * 1024 * 1024
+            dimension_semantics=("arbitrary",), vmem_limit_bytes=20 * 1024 * 1024
         ),
         cost_estimate=pl.CostEstimate(flops=flops, transcendentals=0, bytes_accessed=8 << 20),
     )
@@ -299,24 +302,26 @@
         ],
         [
             stepped((STEP, QKV)), stepped((STEP // PAIR, heads, PAIR, PAIR)),
-            whole((features, width)),
+            whole((features, width)), whole((width, QKV)), whole((features, width)),
         ],
         [
             jax.ShapeDtypeStruct((cells, QKV), bf16),
             jax.ShapeDtypeStruct((cells // PAIR, heads, PAIR, PAIR), f32),
             jax.ShapeDtypeStruct((features, width), bf16),
-        ],
-        [
-            pltpu.VMEM((width, QKV), bf16), pltpu.VMEM((heads, PAIR, PAIR), f32),
+            jax.ShapeDtypeStruct((width, QKV), bf16),
+            jax.ShapeDtypeStruct((features, width), bf16),
+        ],
+        [
+            pltpu.VMEM((heads, PAIR, PAIR), f32),
             pltpu.VMEM((units, PAIR, PAIR), f32), pltpu.VMEM((STEP, features), bf16),
-            pltpu.VMEM((features, width), f32),
+            pltpu.VMEM((features, width), f32), pltpu.VMEM((features, width), f32),
         ],
         4 << 30,
     )(two, other, normed, arrived, bias, label)
 
 
-def run_scores(two, other, proj, prob, arrived, width):
-    cells = proj.shape[0]
+def run_scores(two, other, proj, prob, wo):
+    cells, width = proj.shape[0], wo.shape[1]
     heads = prob.shape[1]
     features = heads * HEAD
     units = heads * (STEP // PAIR)
@@ -325,40 +330,40 @@
         scores_kernel, cells,
         [
             *cell_specs(width), stepped((STEP, QKV)),
-            stepped((STEP // PAIR, heads, PAIR, PAIR)), whole(arrived.shape),
-        ],
-        [stepped((STEP, QKV)), whole((heads, CELLS, CELLS))],
+            stepped((STEP // PAIR, heads, PAIR, PAIR)), whole(wo.shape),
+        ],
+        [stepped((STEP, QKV)), whole((heads, CELLS * CELLS))],
         [
             jax.ShapeDtypeStruct((cells, QKV), bf16),
-            jax.ShapeDtypeStruct((heads, CELLS, CELLS), f32),
-        ],
-        [
-            pltpu.VMEM((features, width), f32), pltpu.VMEM((features, width), bf16),
+            jax.ShapeDtypeStruct((heads, CELLS * CELLS), f32),
+        ],
+        [
             pltpu.VMEM((heads, PAIR, PAIR), f32), pltpu.VMEM((STEP, features), bf16),
             pltpu.VMEM((units, PAIR, PAIR), f32), pltpu.VMEM((units, PAIR, PAIR), bf16),
         ],
         4 << 30,
-    )(two, other, proj, prob, arrived)
-
-
-def run_norm(two, other, dproj, xhat, inv, gain, arrived):
+    )(two, other, proj, prob, wo)
+
+
+def run_norm(two, other, dproj, xhat, inv, gain, weights, table):
     cells, width = xhat.shape
     f32, bf16 = jnp.float32, jnp.bfloat16
     return call(
         norm_kernel, cells,
         [
-            *cell_specs(two.shape[1]), stepped((STEP, QKV)), stepped((STEP, width)),
-            stepped((STEP, LANES)), whole((1, width)), whole(arrived.shape),
+            *cell_specs(LANES, width // LANES), whole((OWN, width)), stepped((STEP, QKV)),
+            stepped((STEP, width)), stepped((STEP, LANES)), whole((1, width)),
+            whole(weights.shape), whole(table.shape),
         ],
         whole((64, width)),
         jax.ShapeDtypeStruct((64, width), bf16),
         [
-            pltpu.VMEM((width, QKV), bf16), pltpu.VMEM((STEP, width), f32),
+            pltpu.VMEM((STEP, width), f32),
             pltpu.VMEM((STEP, width), bf16), pltpu.VMEM((LANES, width), f32),
             pltpu.VMEM((8, width), f32), pltpu.VMEM((8, width), f32),
         ],
         4 << 30,
-    )(two, other, dproj, xhat, inv, gain, arrived)
+    )(two, other, two, dproj, xhat, inv, gain, weights, table)
 
 
 ROW = ("yl", "x", "core")
@@ -539,21 +544,18 @@
     gain = layer_norm_gain[None]
 
     normed, xhat, inv = run_tokens(two, other, embed_w, embed_bias[None], gain)
-    proj, prob, out_grad = run_forward(two, other, normed, arrived, bias, label)
+    proj, prob, out_grad, weights, wo = run_forward(two, other, normed, arrived, bias, label)
     count = lax.axis_size(CHIP_ROW)
     held = exchange(out_grad.reshape(count, -1, width), CHIP_ROW)
-    dproj, table_part = run_scores(two, other, proj, prob, arrived, width)
+    dproj, table_part = run_scores(two, other, proj, prob, wo)
     held = held.reshape(2, count // 2, -1, width).astype(jnp.float32).sum(axis=0)
     bands = exchange(held.astype(jnp.bfloat16), "yl")
-    line = run_norm(two, other, dproj, xhat, inv, gain, arrived)
-    my_grad = jnp.dot(table_part.reshape(heads, -1), selector, precision=lax.Precision.HIGHEST)
+    my_grad = jnp.dot(table_part, selector, precision=lax.Precision.HIGHEST)
     wide = 256
-    my_grad = jnp.pad(my_grad, ((0, 0), (0, wide - table_size)))
-    table_grad = lax.dynamic_update_slice_in_dim(
-        jnp.zeros((all_heads, wide), jnp.float32), my_grad, group * heads, 0
-    )
-    table_rows = table_grad.astype(jnp.bfloat16).reshape(-1, width)
-    line = lax.dynamic_update_slice(line, table_rows, (depth + 2, 0))
+    rows = jnp.zeros((16 * width // wide, wide), jnp.float32)
+    first_row = 2 * width // wide + group * heads
+    table = lax.dynamic_update_slice(rows, my_grad, (first_row, 0)).reshape(16, width)
+    line = run_norm(two, other, dproj, xhat, inv, gain, weights, table)
     line, bands = lax.optimization_barrier((line, bands))
     chunks = lax.axis_size(ROW)
     tall = line.shape[0]

time: 182 us -> 184 us (1.011)
  local copies, waits for them, and re-layouts: 15.8 us -> 28.1 us
  Pallas kernels: 33.6 us -> 22.1 us
    unnamed x19 -> x45, local copies, waits for them, and re-layouts: 1.34 us -> 17.7 us
    pallas_call x1, Pallas kernels: 7.8 us -> 4.87 us  [run_scores(): call(scores_kernel, cells, [*cell_specs(width), stepped((STEP, QKV)), ste...]
    pallas_call x1, Pallas kernels: 8.72 us -> 5.95 us  [run_norm(): call(norm_kernel, cells, [*cell_specs(LANES, width // LANES), whole((OWN,...]
    pallas_call x1, Pallas kernels: 5.51 us -> 2.96 us  [run_tokens(): call(tokens_kernel, cells, [*cell_specs(LANES, width // LANES), whole((LA...]
    pallas_call x1, Pallas kernels: 8.85 us -> 6.67 us  [run_forward(): call(forward_kernel, cells, [*cell_specs(width), stepped((STEP, width)),...]
  transfers between devices with their start and end apart: 10 -> 10, of which waited for: 4 -> 4; matrix products, arithmetic and copies ran while one was open for 7% -> 5% of each run, Pallas kernels for 14% -> 8%
where the time goes in v8:
time: 184 us; the launch traced here: 183 us
  starting transfers between devices  62.8 us (34%)
  waiting for transfers between devices  37.4 us (20%)
  local copies, waits for them, and re-layouts  28.1 us (15%)
  Pallas kernels  22.1 us (12%)
  blocking collectives  19.4 us (11%)
  between operations  6.41 us (3%)
  matrix products  3.59 us (2%)
  other arithmetic  2.95 us (2%)
    all_to_all x6, starting transfers between devices, exchange(): return lax.all_to_all(blocks, axis, split_axis=0, concat_axis=0, tiled=True)  40.7 us
    all_to_all x6, waiting for transfers between devices, exchange(): return lax.all_to_all(blocks, axis, split_axis=0, concat_axis=0, tiled=True)  25.2 us
    all_to_all x1, blocking collectives, exchange(): return lax.all_to_all(blocks, axis, split_axis=0, concat_axis=0, tiled=True)  19.4 us
    unnamed x45, local copies, waits for them, and re-layouts  17.7 us
    ppermute x2, starting transfers between devices, from_behind(): lax.ppermute(value, axis, [(source, (source - 1) % count) for source in r...  14.7 us
    ppermute x2, waiting for transfers between devices, swap(): lax.ppermute(value, axis, [(source, source ^ 1) for source in range(count)])  12.2 us
    ppermute x2, starting transfers between devices, swap(): lax.ppermute(value, axis, [(source, source ^ 1) for source in range(count)])  7.36 us
    pallas_call x1, Pallas kernels, run_forward(): call(forward_kernel, cells, [*cell_specs(width), stepped((STEP, width)),...  6.67 us
  transfers between devices with their start and end apart: 10, of which 4 were waited for; matrix products, arithmetic and copies ran while one was open for 5% of the time, Pallas kernels for 8%

profile of v8, /device:TPU:1, one launch (start us, length us, event | category | flops | bytes accessed | tf_op | source)
XLA Modules:
  0.0 182.7 jit_solution(13687889084665342725)
XLA Ops:
  0.7 2.5 %reshape_squeeze.3 = bf16[3,8,4,32,4]{4,3,2,1,0:T(8,128)(2,1)S(1)} reshape(bf16[1,3,32,128]{3,2,1,0:T(8,128)(2,1)} %param.10) | data formatting | bytes 49152 | tf_op jit(solution)/shard_map/reshape;squeeze | solution.py:398
  3.2 0.7 copy.37
  4.0 11.5 %collective-permute-start = (bf16[8,8,1152]{2,1,0:T(8,128)(2,1)S(1)}, bf16[8,8,1152]{2,1,0:T(8,128)(2,1)S(1)}, u32[]{:S(2)}, u32[]{:S(2)}) collective-permute-start(bf16[8,8,1152]{2,1,0:T(8,128)(2,1)S(1)} %pad_maximum_fusion.1), channel_id=1, source_target_pairs={{0,14},{2,0},{4,2},{6,4},{8,6},{10,8},{12,10},{14,12},{1,15},{3,1}... | collective-permute-start | bytes 442376 | tf_op jit(solution)/shard_map/ppermute | solution.py:386
  15.5 0.6 fusion.20
  18.2 0.4 fusion.5
  18.7 3.2 %collective-permute-start.1 = (bf16[7,32,1152]{2,1,0:T(8,128)(2,1)S(1)}, bf16[7,32,1152]{2,1,0:T(8,128)(2,1)S(1)}, u32[]{:S(2)}, u32[]{:S(2)}) collective-permute-start(bf16[7,32,1152]{2,1,0:T(8,128)(2,1)S(1)} %slice.77), channel_id=1, source_target_pairs={{0,496},{16,0},{32,16},{48,32},{64,48},{80,64},{96,80},{112,96},{1... | collective-permute-start | bytes 1548296 | tf_op jit(solution)/shard_map/ppermute | solution.py:386
  22.0 1.0 broadcast_in_dim.14
  23.0 11.0 %all-to-all-start = ((bf16[64,48,128]{2,1,0:T(8,128)(2,1)}), bf16[64,48,128]{2,1,0:T(8,128)(2,1)S(1)}, u32[]{:S(2)}, u32[]{:S(2)}) async-start(bf16[64,48,128]{2,1,0:T(8,128)(2,1)} %broadcast_in_dim.14), calls=%async_computation | async-start | bytes 1572864 | tf_op jit(solution)/shard_map/all_to_all | solution.py:376
  36.3 3.1 %collective-permute-start.2 = (bf16[256,1152]{1,0:T(8,128)(2,1)S(1)}, bf16[256,1152]{1,0:T(8,128)(2,1)S(1)}, u32[]{:S(2)}, u32[]{:S(2)}) collective-permute-start(bf16[256,1152]{1,0:T(8,128)(2,1)S(1)} %bitcast.66), channel_id=1, source_target_pairs={{0,32},{32,0},{64,96},{96,64},{1,33},{33,1},{65,97},{97,65},{2,34}... | collective-permute-start | bytes 1769480 | tf_op jit(solution)/shard_map/ppermute | solution.py:391
  39.4 12.2 %collective-permute-done.2 = bf16[256,1152]{1,0:T(8,128)(2,1)S(1)} collective-permute-done((bf16[256,1152]{1,0:T(8,128)(2,1)S(1)}, bf16[256,1152]{1,0:T(8,128)(2,1)S(1)}, u32[]{:S(2)}, u32[]{:S(2)}) %collective-permute-start.2) | collective-permute-done | bytes 589856 | tf_op jit(solution)/shard_map/ppermute | solution.py:391
  51.7 4.2 %collective-permute-start.3 = (bf16[512,1152]{1,0:T(8,128)(2,1)S(1)}, bf16[512,1152]{1,0:T(8,128)(2,1)}, u32[]{:S(2)}, u32[]{:S(2)}) collective-permute-start(bf16[512,1152]{1,0:T(8,128)(2,1)S(1)} %pad_maximum_fusion.two.own), channel_id=1, source_target_pairs={{0,16},{16,0},{1,17},{17,1},{2,18},{18,2},{3,19},{19,3},{4,20},{20... | collective-permute-start | bytes 3538952 | tf_op jit(solution)/shard_map/ppermute | solution.py:391
  56.0 0.4 reshape.194
  56.9 1.6 shard_map.138
  58.5 8.0 %all-to-all-start.1 = ((bf16[8,128,768]{2,1,0:T(8,128)(2,1)}), bf16[8,128,768]{2,1,0:T(8,128)(2,1)S(1)}, u32[]{:S(2)}, u32[]{:S(2)}) async-start(bf16[8,128,768]{2,1,0:T(8,128)(2,1)} %shard_map.138), calls=%async_computation.1 | async-start | bytes 3145728 | tf_op jit(solution)/shard_map/all_to_all | solution.py:376
  68.5 2.2 %fusion.1 = f32[3,4096]{1,0:T(4,128)S(1)} fusion(s32[4096]{0:T(1024)S(1)} %eq.17, f32[12,225]{1,0:T(8,128)S(1)} %copy-done, s32[]{:T(128)S(6)} %select_n.28), kind=kOutput, calls=%fused_computation.2 | convolution fusion | flops 34099200 | bytes 69636 | tf_op jit(solution)/shard_map/dot_general | solution.py:541
  70.9 3.0 %shard_map.137 = (bf16[1024,1024]{1,0:T(8,128)(2,1)S(1)}, f32[1024,1024]{1,0:T(8,128)S(1)}, f32[1024,128]{1,0:T(8,128)S(1)}) custom-call(bf16[512,1152]{1,0:T(8,128)(2,1)S(1)} %pad_maximum_fusion.two.own, bf16[512,1152]{1,0:T(8,128)(2,1)} %collective-permute-done.3.other, bf16[128,1024]{1,0:T(8,128)(2,1)S(1)} %pad.9.embed_w, f32[1,1024]{1,0:T(1,128)S(1)} %bitcast.62, ...), custom_call_target="tpu_custom_call" | custom-call | flops 2147483648 | bytes 8388608 | tf_op jit(solution)/shard_map/pallas_call | solution.py:274
  73.9 2.0 %copy-done.3 = f32[1024,1024]{1,0:T(8,128)} copy-done((f32[1024,1024]{1,0:T(8,128)}, f32[1024,1024]{1,0:T(8,128)S(1)}, u32[]{:S(2)}) %copy-start.3) | copy-done | bytes 4194328
  75.8 1.4 copy-done.5
  77.2 0.8 copy-done.11
  78.0 9.1 %all-to-all-done.1.arrived = bf16[8,128,768]{2,1,0:T(8,128)(2,1)S(1)} async-done(((bf16[8,128,768]{2,1,0:T(8,128)(2,1)}), bf16[8,128,768]{2,1,0:T(8,128)(2,1)S(1)}, u32[]{:S(2)}, u32[]{:S(2)}) %all-to-all-start.1) | async-done | bytes 1572896 | tf_op jit(solution)/shard_map/all_to_all | solution.py:376
  87.1 1.6 copy-done.6
  88.7 6.7 %shard_map.139 = (bf16[1024,640]{1,0:T(8,128)(2,1)S(1)}, f32[8,3,128,128]{3,2,1,0:T(8,128)S(1)}, bf16[192,1024]{1,0:T(8,128)(2,1)}, bf16[1024,640]{1,0:T(8,128)(2,1)S(1)}, bf16[192,1024]{1,0:T(8,128)(2,1)S(1)}) custom-call(bf16[512,1152]{1,0:T(8,128)(2,1)S(1)} %pad_maximum_fusion.two.own, bf16[512,1152]{1,0:T(8,128)(2,1)} %collective-permute-done.3.other, ...), custom_call_target="tpu_custom_call" | custom-call | flops 4294967296 | bytes 8388608 | tf_op jit(solution)/shard_map/pallas_call | solution.py:297
  95.4 1.1 copy-done.7
  96.5 1.2 copy-done.13
  97.6 1.2 copy-done.15
  98.8 4.9 %all-to-all-start.2 = ((bf16[8,24,1024]{2,1,0:T(8,128)(2,1)}), bf16[8,24,1024]{2,1,0:T(8,128)(2,1)}, u32[]{:S(2)}, u32[]{:S(2)}) async-start(bf16[8,24,1024]{2,1,0:T(8,128)(2,1)} %bitcast.15), calls=%async_computation.2 | async-start | bytes 786432 | tf_op jit(solution)/shard_map/all_to_all | solution.py:376
  103.7 1.4 copy-done.14
  105.1 1.3 copy-done.16
  106.5 4.9 %shard_map.140 = (bf16[1024,640]{1,0:T(8,128)(2,1)S(1)}, f32[3,4096]{1,0:T(4,128)S(1)}) custom-call(bf16[512,1152]{1,0:T(8,128)(2,1)S(1)} %pad_maximum_fusion.two.own, bf16[512,1152]{1,0:T(8,128)(2,1)} %collective-permute-done.3.other, bf16[1024,640]{1,0:T(8,128)(2,1)S(1)} %copy-done.16, f32[8,3,128,128]{3,2,1,0:T(8,128)S(1)} %copy-done.14, ...), custom_call_target="tpu_custom_call" | custom-call | flops 4294967296 | bytes 8388608 | tf_op jit(solution)/shard_map/pallas_call | solution.py:329
  111.3 1.1 copy-done.9
  112.4 1.4 fusion
  113.9 0.4 dynamic_update_slice.3
  114.3 1.8 reduce_sum.45
  116.1 3.4 %all-to-all-start.3 = ((bf16[4,24,1024]{2,1,0:T(8,128)(2,1)}), bf16[4,24,1024]{2,1,0:T(8,128)(2,1)S(1)}, u32[]{:S(2)}, u32[]{:S(2)}) async-start(bf16[4,24,1024]{2,1,0:T(8,128)(2,1)} %reduce_sum.45), calls=%async_computation.3 | async-start | bytes 393216 | tf_op jit(solution)/shard_map/all_to_all | solution.py:376
  119.5 2.2 %copy-done.4 = f32[1024,1024]{1,0:T(8,128)S(1)} copy-done((f32[1024,1024]{1,0:T(8,128)S(1)}, f32[1024,1024]{1,0:T(8,128)}, u32[]{:S(2)}) %copy-start.4) | copy-done | bytes 4194328
  121.7 1.3 copy-done.10
  123.0 1.0 copy-done.12
  124.1 5.9 %shard_map.141 = bf16[64,1024]{1,0:T(8,128)(2,1)} custom-call(bf16[512,1152]{1,0:T(8,128)(2,1)S(1)} %pad_maximum_fusion.two.own, bf16[512,1152]{1,0:T(8,128)(2,1)} %collective-permute-done.3.other, bf16[512,1152]{1,0:T(8,128)(2,1)S(1)} %pad_maximum_fusion.two.own, bf16[1024,640]{1,0:T(8,128)(2,1)S(1)} %copy-done.10, f32[1024,1024]{1,0:T(8,128)S(1)} %copy-done.4, ...), custom_call_target="tpu_custom_call" | custom-call | flops 4294967296 | bytes 8388608 | tf_op jit(solution)/shard_map/pallas_call | solution.py:351
  130.0 8.2 %all-to-all-start.4 = ((bf16[32,16,128]{2,1,0:T(8,128)(2,1)}), bf16[32,16,128]{2,1,0:T(8,128)(2,1)S(1)}, u32[]{:S(2)}, u32[]{:S(2)}) async-start(bf16[32,16,128]{2,1,0:T(8,128)(2,1)} %bitcast.19), calls=%async_computation.4 | async-start | bytes 262144 | tf_op jit(solution)/shard_map/all_to_all | solution.py:376
  138.5 8.2 %all-to-all-done.4 = bf16[32,16,128]{2,1,0:T(8,128)(2,1)S(1)} async-done(((bf16[32,16,128]{2,1,0:T(8,128)(2,1)}), bf16[32,16,128]{2,1,0:T(8,128)(2,1)S(1)}, u32[]{:S(2)}, u32[]{:S(2)}) %all-to-all-start.4) | async-done | bytes 131104 | tf_op jit(solution)/shard_map/all_to_all | solution.py:376
  146.8 19.4 %all_to_all.35 = bf16[16,28,128]{2,1,0:T(8,128)(2,1)S(1)} all-to-all(bf16[16,28,128]{2,1,0:T(8,128)(2,1)S(1)} %pad_maximum_fusion.2), channel_id=1, replica_groups=mesh['yl'=4,'x'=4,'core'=2,'col'=8,'dp'=2] {'col','dp'}, dimensions={0} | all-to-all | bytes 229376 | tf_op jit(solution)/shard_map/all_to_all | solution.py:376
  166.3 0.7 broadcast_in_dim.17
  167.0 5.2 %all-to-all-start.6 = ((bf16[32,16,128]{2,1,0:T(8,128)(2,1)}), bf16[32,16,128]{2,1,0:T(8,128)(2,1)S(1)}, u32[]{:S(2)}, u32[]{:S(2)}) async-start(bf16[32,16,128]{2,1,0:T(8,128)(2,1)} %broadcast_in_dim.17), calls=%async_computation.6 | async-start | bytes 262144 | tf_op jit(solution)/shard_map/all_to_all | solution.py:376
  172.2 0.7 reshape.204
  172.9 7.8 %all-to-all-done.6 = bf16[32,16,128]{2,1,0:T(8,128)(2,1)S(1)} async-done(((bf16[32,16,128]{2,1,0:T(8,128)(2,1)}), bf16[32,16,128]{2,1,0:T(8,128)(2,1)S(1)}, u32[]{:S(2)}, u32[]{:S(2)}) %all-to-all-start.6) | async-done | bytes 131104 | tf_op jit(solution)/shard_map/all_to_all | solution.py:376
  180.8 0.6 fusion.17
  181.4 0.7 slice_bitcast_fusion
  182.1 0.6 reshape.205
  (82 shorter events, 2.7 us)
Async XLA Ops:
  0.6 67.8 %copy-start = (f32[12,225]{1,0:T(8,128)S(1)}, f32[12,225]{1,0:T(8,128)}, u32[]{:S(2)}) copy-start(f32[12,225]{1,0:T(8,128)} %param.17) | copy-start | bytes 32404
  0.6 3.4 %copy-start.17 = (bf16[1,8,32,1024]{3,2,1,0:T(8,128)(2,1)S(1)}, bf16[1,8,32,1024]{3,2,1,0:T(8,128)(2,1)}, u32[]{:S(2)}) copy-start(bf16[1,8,32,1024]{3,2,1,0:T(8,128)(2,1)} %param.11) | copy-start | bytes 1572868
  0.7 16.8 %slice-start = ((bf16[32,144]{1,0:T(8,128)(2,1)}), bf16[32,16]{1,0:T(8,128)(2,1)S(1)}, s32[]{:S(2)}) async-start(bf16[32,144]{1,0:T(8,128)(2,1)} %param.15), calls=%async_computation.7 | async-start | bytes 16384 | tf_op jit(solution)/shard_map/slice | solution.py:478
  0.7 14.9 %copy-start.21 = (s32[1,2]{1,0:T(1,128)S(1)}, s32[1,2]{1,0:T(1,128)}, u32[]{:S(2)}) copy-start(s32[1,2]{1,0:T(1,128)} %param.19) | copy-start | bytes 28
  0.7 16.8 %copy-start.20 = (bf16[24,64]{1,0:T(8,128)(2,1)S(1)}, bf16[24,64]{1,0:T(8,128)(2,1)}, u32[]{:S(2)}) copy-start(bf16[24,64]{1,0:T(8,128)(2,1)} %param.16) | copy-start | bytes 9220
  4.0 17.9 %slice-start.1 = ((bf16[32,144]{1,0:T(8,128)(2,1)}), bf16[32,128]{1,0:T(8,128)(2,1)S(1)}, s32[]{:S(2)}) async-start(bf16[32,144]{1,0:T(8,128)(2,1)} %param.15), calls=%async_computation.8 | async-start | bytes 16384 | tf_op jit(solution)/shard_map/slice | solution.py:481
  4.0 14.2 %collective-permute-start = (bf16[8,8,1152]{2,1,0:T(8,128)(2,1)S(1)}, bf16[8,8,1152]{2,1,0:T(8,128)(2,1)S(1)}, u32[]{:S(2)}, u32[]{:S(2)}) collective-permute-start(bf16[8,8,1152]{2,1,0:T(8,128)(2,1)S(1)} %pad_maximum_fusion.1), channel_id=1, source_target_pairs={{0,14},{2,0},{4,2},{6,4},{8,6},{10,8},{12,10},{14,12},{1,15},{3,1}... | collective-permute-start | bytes 442376 | tf_op jit(solution)/shard_map/ppermute | solution.py:386
  18.7 17.2 %collective-permute-start.1 = (bf16[7,32,1152]{2,1,0:T(8,128)(2,1)S(1)}, bf16[7,32,1152]{2,1,0:T(8,128)(2,1)S(1)}, u32[]{:S(2)}, u32[]{:S(2)}) collective-permute-start(bf16[7,32,1152]{2,1,0:T(8,128)(2,1)S(1)} %slice.77), channel_id=1, source_target_pairs={{0,496},{16,0},{32,16},{48,32},{64,48},{80,64},{96,80},{112,96},{1... | collective-permute-start | bytes 1548296 | tf_op jit(solution)/shard_map/ppermute | solution.py:386
  23.0 32.9 %all-to-all-start = ((bf16[64,48,128]{2,1,0:T(8,128)(2,1)}), bf16[64,48,128]{2,1,0:T(8,128)(2,1)S(1)}, u32[]{:S(2)}, u32[]{:S(2)}) async-start(bf16[64,48,128]{2,1,0:T(8,128)(2,1)} %broadcast_in_dim.14), calls=%async_computation | async-start | bytes 1572864 | tf_op jit(solution)/shard_map/all_to_all | solution.py:376
  36.3 15.3 %collective-permute-start.2 = (bf16[256,1152]{1,0:T(8,128)(2,1)S(1)}, bf16[256,1152]{1,0:T(8,128)(2,1)S(1)}, u32[]{:S(2)}, u32[]{:S(2)}) collective-permute-start(bf16[256,1152]{1,0:T(8,128)(2,1)S(1)} %bitcast.66), channel_id=1, source_target_pairs={{0,32},{32,0},{64,96},{96,64},{1,33},{33,1},{65,97},{97,65},{2,34}... | collective-permute-start | bytes 1769480 | tf_op jit(solution)/shard_map/ppermute | solution.py:391
  51.7 19.2 %collective-permute-start.3 = (bf16[512,1152]{1,0:T(8,128)(2,1)S(1)}, bf16[512,1152]{1,0:T(8,128)(2,1)}, u32[]{:S(2)}, u32[]{:S(2)}) collective-permute-start(bf16[512,1152]{1,0:T(8,128)(2,1)S(1)} %pad_maximum_fusion.two.own), channel_id=1, source_target_pairs={{0,16},{16,0},{1,17},{17,1},{2,18},{18,2},{3,19},{19,3},{4,20},{20... | collective-permute-start | bytes 3538952 | tf_op jit(solution)/shard_map/ppermute | solution.py:391
  58.5 9.9 %copy-start.19 = (s32[64,64]{1,0:T(8,128)S(1)}, s32[64,64]{1,0:T(8,128)}, u32[]{:S(2)}) copy-start(s32[64,64]{1,0:T(8,128)} %param.18) | copy-start | bytes 49156
  58.5 28.6 %all-to-all-start.1 = ((bf16[8,128,768]{2,1,0:T(8,128)(2,1)}), bf16[8,128,768]{2,1,0:T(8,128)(2,1)S(1)}, u32[]{:S(2)}, u32[]{:S(2)}) async-start(bf16[8,128,768]{2,1,0:T(8,128)(2,1)} %shard_map.138), calls=%async_computation.1 | async-start | bytes 3145728 | tf_op jit(solution)/shard_map/all_to_all | solution.py:376
  66.5 4.3 %copy-start.18 = (bf16[48,1024]{1,0:T(8,128)(2,1)S(1)}, bf16[48,1024]{1,0:T(8,128)(2,1)}, u32[]{:S(2)}) copy-start(bf16[48,1024]{1,0:T(8,128)(2,1)} %param.12) | copy-start | bytes 294916
  66.5 4.3 %copy-start.1 = (f32[1024]{0:T(1024)S(1)}, f32[1024]{0:T(1024)}, u32[]{:S(2)}) copy-start(f32[1024]{0:T(1024)} %param.13) | copy-start | bytes 12292
  66.5 4.3 %copy-start.2 = (f32[1024]{0:T(1024)S(1)}, f32[1024]{0:T(1024)}, u32[]{:S(2)}) copy-start(f32[1024]{0:T(1024)} %param.14) | copy-start | bytes 12292
  73.8 2.0 %copy-start.3 = (f32[1024,1024]{1,0:T(8,128)}, f32[1024,1024]{1,0:T(8,128)S(1)}, u32[]{:S(2)}) copy-start(f32[1024,1024]{1,0:T(8,128)S(1)} %get-tuple-element.22.xhat) | copy-start | bytes 12582916
  75.8 1.4 copy-start.5
  77.2 0.8 copy-start.11
  87.1 1.6 copy-start.6
  95.4 1.1 copy-start.7
  96.4 1.2 copy-start.13
  97.6 1.2 copy-start.15
  98.8 15.5 %all-to-all-start.2 = ((bf16[8,24,1024]{2,1,0:T(8,128)(2,1)}), bf16[8,24,1024]{2,1,0:T(8,128)(2,1)}, u32[]{:S(2)}, u32[]{:S(2)}) async-start(bf16[8,24,1024]{2,1,0:T(8,128)(2,1)} %bitcast.15), calls=%async_computation.2 | async-start | bytes 786432 | tf_op jit(solution)/shard_map/all_to_all | solution.py:376
  103.7 1.4 copy-start.14
  105.1 1.3 copy-start.16
  111.3 1.1 copy-start.9
  112.4 7.1 %copy-start.8 = (bf16[1024,640]{1,0:T(8,128)(2,1)S(1)}, bf16[1024,640]{1,0:T(8,128)(2,1)}, u32[]{:S(2)}) copy-start(bf16[1024,640]{1,0:T(8,128)(2,1)} %copy-done.7) | copy-start | bytes 3932164
  116.1 13.9 %all-to-all-start.3 = ((bf16[4,24,1024]{2,1,0:T(8,128)(2,1)}), bf16[4,24,1024]{2,1,0:T(8,128)(2,1)S(1)}, u32[]{:S(2)}, u32[]{:S(2)}) async-start(bf16[4,24,1024]{2,1,0:T(8,128)(2,1)} %reduce_sum.45), calls=%async_computation.3 | async-start | bytes 393216 | tf_op jit(solution)/shard_map/all_to_all | solution.py:376
  119.5 2.2 %copy-start.4 = (f32[1024,1024]{1,0:T(8,128)S(1)}, f32[1024,1024]{1,0:T(8,128)}, u32[]{:S(2)}) copy-start(f32[1024,1024]{1,0:T(8,128)} %copy-done.3) | copy-start | bytes 12582916
  121.7 1.3 copy-start.10
  123.0 1.0 copy-start.12
  130.0 16.7 %all-to-all-start.4 = ((bf16[32,16,128]{2,1,0:T(8,128)(2,1)}), bf16[32,16,128]{2,1,0:T(8,128)(2,1)S(1)}, u32[]{:S(2)}, u32[]{:S(2)}) async-start(bf16[32,16,128]{2,1,0:T(8,128)(2,1)} %bitcast.19), calls=%async_computation.4 | async-start | bytes 262144 | tf_op jit(solution)/shard_map/all_to_all | solution.py:376
  167.0 13.7 %all-to-all-start.6 = ((bf16[32,16,128]{2,1,0:T(8,128)(2,1)}), bf16[32,16,128]{2,1,0:T(8,128)(2,1)S(1)}, u32[]{:S(2)}, u32[]{:S(2)}) async-start(bf16[32,16,128]{2,1,0:T(8,128)(2,1)} %broadcast_in_dim.17), calls=%async_computation.6 | async-start | bytes 262144 | tf_op jit(solution)/shard_map/all_to_all | solution.py:376

commit v9 on v8

--- a/solution.py
+++ b/solution.py
@@ -90,26 +90,30 @@
     normed_out[...] = (xhat * gain[...]).astype(jnp.bfloat16)
 
 
-def forward_kernel(
+def attention_kernel(
     two, other, normed, arrived, bias, label,
-    proj_out, prob_out, grad_out, weights, wo, bias_pair, scores, att, grad_acc, wide_rows
+    dproj, table_out, grad_out, weights,
+    wo, wide_rows, bias_pair, proj, scores, probs, lows, att, grad_acc, datt, table
 ):
     step = pl.program_id(0)
+    heads = bias.shape[0]
 
     @pl.when(step == 0)
     def _():
         assemble(arrived, weights)
         assemble_out(arrived, wide_rows, wo)
-        for head in range(bias.shape[0]):
+        table[...] = jnp.zeros_like(table)
+        for head in range(heads):
             row = jnp.concatenate([bias[head], bias[head]], axis=1)
             bias_pair[head] = jnp.concatenate([row, row], axis=0)
 
     cot = jnp.where(step < HALF, two[...], other[...])
-    proj_out[...] = dot_nn(normed[...], weights[...]).astype(jnp.bfloat16)
-    heads = bias.shape[0]
+    proj[...] = dot_nn(normed[...], weights[...]).astype(jnp.bfloat16)
+    datt[...] = dot_nt(cot, wo[...]).astype(jnp.bfloat16)
+    dproj[:, QKV - HEAD :] = jnp.zeros((STEP, HEAD), jnp.bfloat16)
     for pair, rows, q_at, k_at, v_at, at, count in work():
-        q = proj_out[rows, q_at : q_at + count * HEAD]
-        k = proj_out[rows, k_at : k_at + count * HEAD]
+        q = proj[rows, q_at : q_at + count * HEAD]
+        k = proj[rows, k_at : k_at + count * HEAD]
         for i in range(count):
             scores[pair * heads + at // HEAD + i] = dot_nt(only(half_masks(count), i, q), k)
     for pair in range(STEP // PAIR):
@@ -120,54 +124,26 @@
             values = scores[pair * heads + head] * SCALE + bias_pair[head]
             values = jnp.where(same, values, -1e30)
             e = jnp.exp(values - jnp.max(values, axis=-1, keepdims=True))
-            prob_out[pair, head] = e * (1.0 / jnp.sum(e, axis=-1, keepdims=True))
-    for pair, rows, q_at, k_at, v_at, at, count in work():
-        v = proj_out[rows, v_at : v_at + count * HEAD]
-        parts = [
-            dot_nn(prob_out[pair, at // HEAD + i].astype(jnp.bfloat16), v) for i in range(count)
-        ]
-        att[rows, at : at + count * HEAD] = choose(half_masks(count), parts).astype(jnp.bfloat16)
-    grad = dot_tn(att[...], cot)
-
-    @pl.when(step == 0)
-    def _():
-        grad_acc[...] = grad
-
-    @pl.when(step > 0)
-    def _():
-        grad_acc[...] += grad
-
-    @pl.when(step == pl.num_programs(0) - 1)
-    def _():
-        grad_out[...] = grad_acc[...].astype(grad_out.dtype)
-
-
-def scores_kernel(
-    two, other, proj, prob_in, wo, dproj, table_out, table, datt, d_probs, lows
-):
-    step = pl.program_id(0)
-    heads = prob_in.shape[1]
-
-    @pl.when(step == 0)
-    def _():
-        table[...] = jnp.zeros_like(table)
-
-    cot = jnp.where(step < HALF, two[...], other[...])
-    datt[...] = dot_nt(cot, wo[...]).astype(jnp.bfloat16)
-    dproj[:, QKV - HEAD :] = jnp.zeros((STEP, HEAD), jnp.bfloat16)
+            probs[pair * heads + head] = e * (1.0 / jnp.sum(e, axis=-1, keepdims=True))
     for pair, rows, q_at, k_at, v_at, at, count in work():
         v = proj[rows, v_at : v_at + count * HEAD]
         d_out = datt[rows, at : at + count * HEAD]
+        parts = []
         for i in range(count):
-            d_probs[pair * heads + at // HEAD + i] = dot_nt(only(half_masks(count), i, d_out), v)
+            unit = pair * heads + at // HEAD + i
+            parts.append(dot_nn(probs[unit].astype(jnp.bfloat16), v))
+            scores[unit] = dot_nt(only(half_masks(count), i, d_out), v)
+        att[rows, at : at + count * HEAD] = choose(half_masks(count), parts).astype(jnp.bfloat16)
+    grad = dot_tn(att[...], cot)
     for head in range(heads):
         total = table[head]
         for pair in range(STEP // PAIR):
-            prob, d_prob = prob_in[pair, head], d_probs[pair * heads + head]
-            weighted = prob * d_prob
+            unit = pair * heads + head
+            prob = probs[unit]
+            weighted = prob * scores[unit]
             d_scores = weighted - prob * jnp.sum(weighted, axis=-1, keepdims=True)
             total = total + d_scores
-            lows[pair * heads + head] = d_scores.astype(jnp.bfloat16)
+            lows[unit] = d_scores.astype(jnp.bfloat16)
         table[head] = total
     for pair, rows, q_at, k_at, v_at, at, count in work():
         width_in = count * HEAD
@@ -177,17 +153,25 @@
         d_out = datt[rows, at : at + width_in]
         qs, ks, vs = [], [], []
         for i in range(count):
-            head = at // HEAD + i
-            low = lows[pair * heads + head]
-            qs.append(dot_nn(low, k))
-            ks.append(dot_tn(low, q))
-            vs.append(dot_tn(prob_in[pair, head].astype(jnp.bfloat16), d_out))
+            unit = pair * heads + at // HEAD + i
+            qs.append(dot_nn(lows[unit], k))
+            ks.append(dot_tn(lows[unit], q))
+            vs.append(dot_tn(probs[unit].astype(jnp.bfloat16), d_out))
         dproj[rows, q_at : q_at + width_in] = (choose(masks, qs) * SCALE).astype(jnp.bfloat16)
         dproj[rows, k_at : k_at + width_in] = (choose(masks, ks) * SCALE).astype(jnp.bfloat16)
         dproj[rows, v_at : v_at + width_in] = choose(masks, vs).astype(jnp.bfloat16)
 
+    @pl.when(step == 0)
+    def _():
+        grad_acc[...] = grad
+
+    @pl.when(step > 0)
+    def _():
+        grad_acc[...] += grad
+
     @pl.when(step == pl.num_programs(0) - 1)
     def _():
+        grad_out[...] = grad_acc[...].astype(grad_out.dtype)
         for head in range(heads):
             full = table[head]
             full = full[:CELLS, :CELLS] + full[CELLS:, CELLS:]
@@ -253,7 +237,7 @@
     ]
 
 
-def call(kernel, cells, in_specs, out_specs, out_shape, scratch, flops):
+def call(kernel, cells, in_specs, out_specs, out_shape, scratch, flops, grant=56):
     return pl.pallas_call(
         kernel,
         grid=(cells // STEP,),
@@ -262,7 +246,7 @@
         out_shape=out_shape,
         scratch_shapes=scratch,
         compiler_params=pltpu.CompilerParams(
-            dimension_semantics=("arbitrary",), vmem_limit_bytes=20 * 1024 * 1024
+            dimension_semantics=("arbitrary",), vmem_limit_bytes=grant << 20
         ),
         cost_estimate=pl.CostEstimate(flops=flops, transcendentals=0, bytes_accessed=8 << 20),
     )
@@ -288,61 +272,38 @@
     )(two, other, embed_w, embed_b, gain)
 
 
-def run_forward(two, other, normed, arrived, bias, label):
+def run_attention(two, other, normed, arrived, bias, label):
     cells, width = normed.shape
     heads = bias.shape[0]
     features = heads * HEAD
     units = heads * (STEP // PAIR)
     f32, bf16 = jnp.float32, jnp.bfloat16
     return call(
-        forward_kernel, cells,
+        attention_kernel, cells,
         [
             *cell_specs(width), stepped((STEP, width)),
             whole(arrived.shape), whole(bias.shape), whole(label.shape),
         ],
         [
-            stepped((STEP, QKV)), stepped((STEP // PAIR, heads, PAIR, PAIR)),
-            whole((features, width)), whole((width, QKV)), whole((features, width)),
+            stepped((STEP, QKV)), whole((heads, CELLS * CELLS)),
+            whole((features, width)), whole((width, QKV)),
         ],
         [
             jax.ShapeDtypeStruct((cells, QKV), bf16),
-            jax.ShapeDtypeStruct((cells // PAIR, heads, PAIR, PAIR), f32),
+            jax.ShapeDtypeStruct((heads, CELLS * CELLS), f32),
             jax.ShapeDtypeStruct((features, width), bf16),
             jax.ShapeDtypeStruct((width, QKV), bf16),
-            jax.ShapeDtypeStruct((features, width), bf16),
-        ],
-        [
+        ],
+        [
+            pltpu.VMEM((features, width), bf16), pltpu.VMEM((features, width), f32),
+            pltpu.VMEM((heads, PAIR, PAIR), f32), pltpu.VMEM((STEP, QKV), bf16),
+            pltpu.VMEM((units, PAIR, PAIR), f32), pltpu.VMEM((units, PAIR, PAIR), f32),
+            pltpu.VMEM((units, PAIR, PAIR), bf16), pltpu.VMEM((STEP, features), bf16),
+            pltpu.VMEM((features, width), f32), pltpu.VMEM((STEP, features), bf16),
             pltpu.VMEM((heads, PAIR, PAIR), f32),
-            pltpu.VMEM((units, PAIR, PAIR), f32), pltpu.VMEM((STEP, features), bf16),
-            pltpu.VMEM((features, width), f32), pltpu.VMEM((features, width), f32),
-        ],
-        4 << 30,
+        ],
+        8 << 30,
     )(two, other, normed, arrived, bias, label)
-
-
-def run_scores(two, other, proj, prob, wo):
-    cells, width = proj.shape[0], wo.shape[1]
-    heads = prob.shape[1]
-    features = heads * HEAD
-    units = heads * (STEP // PAIR)
-    f32, bf16 = jnp.float32, jnp.bfloat16
-    return call(
-        scores_kernel, cells,
-        [
-            *cell_specs(width), stepped((STEP, QKV)),
-            stepped((STEP // PAIR, heads, PAIR, PAIR)), whole(wo.shape),
-        ],
-        [stepped((STEP, QKV)), whole((heads, CELLS * CELLS))],
-        [
-            jax.ShapeDtypeStruct((cells, QKV), bf16),
-            jax.ShapeDtypeStruct((heads, CELLS * CELLS), f32),
-        ],
-        [
-            pltpu.VMEM((heads, PAIR, PAIR), f32), pltpu.VMEM((STEP, features), bf16),
-            pltpu.VMEM((units, PAIR, PAIR), f32), pltpu.VMEM((units, PAIR, PAIR), bf16),
-        ],
-        4 << 30,
-    )(two, other, proj, prob, wo)
 
 
 def run_norm(two, other, dproj, xhat, inv, gain, weights, table):
@@ -470,6 +431,7 @@
         jax.ShapeDtypeStruct((count, LANES, QKV + LANES), jnp.bfloat16),
         [],
         1 << 30,
+        20,
     )(lines, rest)
 
 
@@ -544,35 +506,40 @@
     gain = layer_norm_gain[None]
 
     normed, xhat, inv = run_tokens(two, other, embed_w, embed_bias[None], gain)
-    proj, prob, out_grad, weights, wo = run_forward(two, other, normed, arrived, bias, label)
+    dproj, table_part, out_grad, weights = run_attention(
+        two, other, normed, arrived, bias, label
+    )
     count = lax.axis_size(CHIP_ROW)
     held = exchange(out_grad.reshape(count, -1, width), CHIP_ROW)
-    dproj, table_part = run_scores(two, other, proj, prob, wo)
-    held = held.reshape(2, count // 2, -1, width).astype(jnp.float32).sum(axis=0)
-    bands = exchange(held.astype(jnp.bfloat16), "yl")
     my_grad = jnp.dot(table_part, selector, precision=lax.Precision.HIGHEST)
     wide = 256
     rows = jnp.zeros((16 * width // wide, wide), jnp.float32)
     first_row = 2 * width // wide + group * heads
     table = lax.dynamic_update_slice(rows, my_grad, (first_row, 0)).reshape(16, width)
     line = run_norm(two, other, dproj, xhat, inv, gain, weights, table)
-    line, bands = lax.optimization_barrier((line, bands))
+    line, held = lax.optimization_barrier((line, held))
     chunks = lax.axis_size(ROW)
     tall = line.shape[0]
     tiles = line.reshape(tall // 8, 8, width // LANES, LANES).transpose(0, 2, 1, 3)
     tiles = tiles.reshape(chunks, -1, LANES)
     mine = exchange(tiles, ROW)
+    bands = held.reshape(2, count // 2, -1, width).astype(jnp.float32).sum(axis=0)
+    groups, rows_o, _ = bands.shape
+    spans = lax.axis_size(COL)
+    bands = bands.astype(jnp.bfloat16).reshape(groups, rows_o, spans, -1).transpose(2, 0, 1, 3)
+    bands = bands.reshape(spans, -1, LANES)
     mine = mine.astype(jnp.float32).sum(axis=0).astype(jnp.bfloat16)
-    rows_o = bands.shape[1]
-    bands = bands.astype(jnp.float32).sum(axis=0).astype(jnp.bfloat16)
-    spans = lax.axis_size(COL)
-    bands = bands.reshape(rows_o, spans, -1).transpose(1, 0, 2).reshape(spans, -1, LANES)
-    held = mine.shape[0]
-    mine = jnp.broadcast_to(mine[None], (spans, held, LANES))
+    depth_s = mine.shape[0]
+    mine = jnp.broadcast_to(mine[None], (spans, depth_s, LANES))
     both = exchange(jnp.concatenate([mine, bands], axis=1), COL)
-    both = both.astype(jnp.float32).sum(axis=0)
-    out_weight_grad = both[held:].reshape(rows_o, -1)
-    total = spread(both[:held].astype(jnp.bfloat16), ROW)
+    both = both.astype(jnp.float32).sum(axis=0).astype(jnp.bfloat16)
+    mine = jnp.broadcast_to(both[None, :depth_s], (chunks, depth_s, LANES))
+    bands = both[depth_s:].reshape(groups, 1, -1, LANES)
+    here = jnp.arange(count, dtype=jnp.int32)[None, :, None, None] == lax.axis_index(CHIP_ROW)
+    bands = jnp.where(here, bands, jnp.zeros_like(bands)).reshape(chunks, -1, LANES)
+    total = exchange(jnp.concatenate([mine, bands], axis=1), ROW)
+    out_weight_grad = total[:, depth_s:].astype(jnp.float32).sum(axis=0).reshape(rows_o, -1)
+    total = total[:, :depth_s]
     total = total.reshape(tall // 8, width // LANES, 8, LANES).transpose(0, 2, 1, 3)
     total = total.reshape(tall, width).astype(jnp.float32)
     table_grad = total[depth + 2 : depth + 5].reshape(all_heads, wide)[:, :table_size]

time: 184 us -> 171 us (0.929)
  local copies, waits for them, and re-layouts: 28.1 us -> 13.5 us
  waiting for transfers between devices: 37.4 us -> 42 us
  starting transfers between devices: 62.8 us -> 58.3 us
  Pallas kernels: 22.1 us -> 25.2 us
    unnamed x45 -> x17, local copies, waits for them, and re-layouts: 17.7 us -> 1.32 us
    all_to_all x6 -> x5, waiting for transfers between devices: 25.2 us -> 29.9 us  [exchange(): return lax.all_to_all(blocks, axis, split_axis=0, concat_axis=0, tiled=True)]
    all_to_all x6 -> x5, starting transfers between devices: 40.7 us -> 36.2 us  [exchange(): return lax.all_to_all(blocks, axis, split_axis=0, concat_axis=0, tiled=True)]
    pallas_call x1, Pallas kernels: 5.95 us -> 8.14 us  [run_norm(): call(norm_kernel, cells, [*cell_specs(LANES, width // LANES), whole((OWN,...]
    pallas_call x1, Pallas kernels: 2.96 us -> 4.9 us  [run_tokens(): call(tokens_kernel, cells, [*cell_specs(LANES, width // LANES), whole((LA...]
    pallas_call x2 -> x1, Pallas kernels: 11.5 us -> 10.5 us  [run_attention(): call(attention_kernel, cells, [*cell_specs(width), stepped((STEP, width))...]
  transfers between devices with their start and end apart: 10 -> 9, of which waited for: 4 -> 4; matrix products, arithmetic and copies ran while one was open for 5% -> 5% of each run, Pallas kernels for 8% -> 9%
where the time goes in v9:
time: 171 us; the launch traced here: 170 us
  starting transfers between devices  58.3 us (34%)
  waiting for transfers between devices  42 us (25%)
  Pallas kernels  25.2 us (15%)
  blocking collectives  18.1 us (11%)
  local copies, waits for them, and re-layouts  13.5 us (8%)
  between operations  6.33 us (4%)
  matrix products  4.43 us (3%)
  other arithmetic  2.68 us (2%)
    all_to_all x5, starting transfers between devices, exchange(): return lax.all_to_all(blocks, axis, split_axis=0, concat_axis=0, tiled=True)  36.2 us
    all_to_all x5, waiting for transfers between devices, exchange(): return lax.all_to_all(blocks, axis, split_axis=0, concat_axis=0, tiled=True)  29.9 us
    all_to_all x1, blocking collectives, exchange(): return lax.all_to_all(blocks, axis, split_axis=0, concat_axis=0, tiled=True)  18.1 us
    ppermute x2, starting transfers between devices, from_behind(): lax.ppermute(value, axis, [(source, (source - 1) % count) for source in r...  14.7 us
    ppermute x2, waiting for transfers between devices, swap(): lax.ppermute(value, axis, [(source, source ^ 1) for source in range(count)])  12.2 us
    pallas_call x1, Pallas kernels, run_attention(): call(attention_kernel, cells, [*cell_specs(width), stepped((STEP, width))...  10.5 us
    pallas_call x1, Pallas kernels, run_norm(): call(norm_kernel, cells, [*cell_specs(LANES, width // LANES), whole((OWN,...  8.14 us
    ppermute x2, starting transfers between devices, swap(): lax.ppermute(value, axis, [(source, source ^ 1) for source in range(count)])  7.36 us
  transfers between devices with their start and end apart: 9, of which 4 were waited for; matrix products, arithmetic and copies ran while one was open for 5% of the time, Pallas kernels for 9%

profile of v9, /device:TPU:1, one launch (start us, length us, event | category | flops | bytes accessed | tf_op | source)
XLA Modules:
  0.0 170.5 jit_solution(10128536831726521362)
XLA Ops:
  0.7 2.5 %reshape_squeeze.3 = bf16[3,8,4,32,4]{4,3,2,1,0:T(8,128)(2,1)S(1)} reshape(bf16[1,3,32,128]{3,2,1,0:T(8,128)(2,1)} %param.10) | data formatting | bytes 49152 | tf_op jit(solution)/shard_map/reshape;squeeze | solution.py:359
  3.2 0.7 copy.22
  3.8 0.1 copy.28
  4.0 11.5 %collective-permute-start = (bf16[8,8,1152]{2,1,0:T(8,128)(2,1)S(1)}, bf16[8,8,1152]{2,1,0:T(8,128)(2,1)S(1)}, u32[]{:S(2)}, u32[]{:S(2)}) collective-permute-start(bf16[8,8,1152]{2,1,0:T(8,128)(2,1)S(1)} %pad_maximum_fusion.3), channel_id=1, source_target_pairs={{0,14},{2,0},{4,2},{6,4},{8,6},{10,8},{12,10},{14,12},{1,15},{3,1}... | collective-permute-start | bytes 442376 | tf_op jit(solution)/shard_map/ppermute | solution.py:347
  15.5 0.6 fusion.20
  18.2 0.4 fusion.5
  18.7 3.2 %collective-permute-start.1 = (bf16[7,32,1152]{2,1,0:T(8,128)(2,1)S(1)}, bf16[7,32,1152]{2,1,0:T(8,128)(2,1)S(1)}, u32[]{:S(2)}, u32[]{:S(2)}) collective-permute-start(bf16[7,32,1152]{2,1,0:T(8,128)(2,1)S(1)} %slice.84), channel_id=1, source_target_pairs={{0,496},{16,0},{32,16},{48,32},{64,48},{80,64},{96,80},{112,96},{1... | collective-permute-start | bytes 1548296 | tf_op jit(solution)/shard_map/ppermute | solution.py:347
  22.0 1.0 broadcast_in_dim.72
  23.0 11.0 %all-to-all-start = ((bf16[64,48,128]{2,1,0:T(8,128)(2,1)}), bf16[64,48,128]{2,1,0:T(8,128)(2,1)S(1)}, u32[]{:S(2)}, u32[]{:S(2)}) async-start(bf16[64,48,128]{2,1,0:T(8,128)(2,1)} %broadcast_in_dim.72), calls=%async_computation | async-start | bytes 1572864 | tf_op jit(solution)/shard_map/all_to_all | solution.py:337
  35.9 0.2 fusion.7
  36.2 3.1 %collective-permute-start.2 = (bf16[256,1152]{1,0:T(8,128)(2,1)S(1)}, bf16[256,1152]{1,0:T(8,128)(2,1)S(1)}, u32[]{:S(2)}, u32[]{:S(2)}) collective-permute-start(bf16[256,1152]{1,0:T(8,128)(2,1)S(1)} %bitcast.67), channel_id=1, source_target_pairs={{0,32},{32,0},{64,96},{96,64},{1,33},{33,1},{65,97},{97,65},{2,34}... | collective-permute-start | bytes 1769480 | tf_op jit(solution)/shard_map/ppermute | solution.py:352
  39.4 12.2 %collective-permute-done.2 = bf16[256,1152]{1,0:T(8,128)(2,1)S(1)} collective-permute-done((bf16[256,1152]{1,0:T(8,128)(2,1)S(1)}, bf16[256,1152]{1,0:T(8,128)(2,1)S(1)}, u32[]{:S(2)}, u32[]{:S(2)}) %collective-permute-start.2) | collective-permute-done | bytes 589856 | tf_op jit(solution)/shard_map/ppermute | solution.py:352
  51.5 0.1 pad_maximum_fusion.two.own
  51.6 4.2 %collective-permute-start.3 = (bf16[512,1152]{1,0:T(8,128)(2,1)S(1)}, bf16[512,1152]{1,0:T(8,128)(2,1)}, u32[]{:S(2)}, u32[]{:S(2)}) collective-permute-start(bf16[512,1152]{1,0:T(8,128)(2,1)S(1)} %pad_maximum_fusion.two.own), channel_id=1, source_target_pairs={{0,16},{16,0},{1,17},{17,1},{2,18},{18,2},{3,19},{19,3},{4,20},{20... | collective-permute-start | bytes 3538952 | tf_op jit(solution)/shard_map/ppermute | solution.py:352
  56.0 0.4 reshape.205
  56.3 0.3 copy.25
  56.6 0.2 reshape.206
  56.8 0.1 copy.26.rest
  56.9 1.6 shard_map.138
  58.5 8.0 %all-to-all-start.1 = ((bf16[8,128,768]{2,1,0:T(8,128)(2,1)}), bf16[8,128,768]{2,1,0:T(8,128)(2,1)S(1)}, u32[]{:S(2)}, u32[]{:S(2)}) async-start(bf16[8,128,768]{2,1,0:T(8,128)(2,1)} %shard_map.138), calls=%async_computation.1 | async-start | bytes 3145728 | tf_op jit(solution)/shard_map/all_to_all | solution.py:337
  68.1 0.1 concatenate.47
  68.4 2.2 %fusion.1 = f32[3,4096]{1,0:T(4,128)S(1)} fusion(s32[4096]{0:T(1024)S(1)} %eq.28, f32[12,225]{1,0:T(8,128)S(1)} %copy-done, s32[]{:T(128)S(6)} %select_n.33), kind=kOutput, calls=%fused_computation.2 | convolution fusion | flops 34099200 | bytes 69636 | tf_op jit(solution)/shard_map/dot_general | solution.py:503
  70.6 0.8 reshape.207.bias
  71.4 0.8 pad.9.embed_w
  72.2 0.6 fusion.11.label
  72.8 4.9 %shard_map.137 = (bf16[1024,1024]{1,0:T(8,128)(2,1)}, f32[1024,1024]{1,0:T(8,128)}, f32[1024,128]{1,0:T(8,128)}) custom-call(bf16[512,1152]{1,0:T(8,128)(2,1)} %copy-done.3, bf16[512,1152]{1,0:T(8,128)(2,1)} %collective-permute-done.3.other, bf16[128,1024]{1,0:T(8,128)(2,1)} %pad.9.embed_w, f32[1,1024]{1,0:T(1,128)} %bitcast.80, f32[1,1024]{1,0:T(1,128)} %bitcast.81), custom_call_target="tpu_custom_call" | custom-call | flops 2147483648 | bytes 8388608 | tf_op jit(solution)/shard_map/pallas_call | solution.py:258
  77.7 9.4 %all-to-all-done.1.arrived = bf16[8,128,768]{2,1,0:T(8,128)(2,1)S(1)} async-done(((bf16[8,128,768]{2,1,0:T(8,128)(2,1)}), bf16[8,128,768]{2,1,0:T(8,128)(2,1)S(1)}, u32[]{:S(2)}, u32[]{:S(2)}) %all-to-all-start.1) | async-done | bytes 1572896 | tf_op jit(solution)/shard_map/all_to_all | solution.py:337
  87.1 1.1 copy-done.2
  88.2 10.5 %shard_map.139 = (bf16[1024,640]{1,0:T(8,128)(2,1)}, f32[3,4096]{1,0:T(4,128)}, bf16[192,1024]{1,0:T(8,128)(2,1)}, bf16[1024,640]{1,0:T(8,128)(2,1)}) custom-call(bf16[512,1152]{1,0:T(8,128)(2,1)} %copy-done.3, bf16[512,1152]{1,0:T(8,128)(2,1)} %collective-permute-done.3.other, bf16[1024,1024]{1,0:T(8,128)(2,1)} %get-tuple-element.14.normed, ...), custom_call_target="tpu_custom_call" | custom-call | flops 8589934592 | bytes 8388608 | tf_op jit(solution)/shard_map/pallas_call | solution.py:281
  98.8 2.2 %fusion = f32[3,225]{1,0:T(4,128)S(1)} fusion(f32[3,4096]{1,0:T(4,128)} %get-tuple-element.19, s32[4096]{0:T(1024)S(1)} %eq.28), kind=kOutput, calls=%fused_computation.1 | convolution fusion | flops 34099200 | bytes 68236 | tf_op jit(solution)/shard_map/dot_general | solution.py:514
  101.0 0.4 dynamic_update_slice.3
  101.5 0.6 reshape.208.table
  102.1 4.3 %all-to-all-start.2 = ((bf16[8,24,1024]{2,1,0:T(8,128)(2,1)}), bf16[8,24,1024]{2,1,0:T(8,128)(2,1)S(1)}, u32[]{:S(2)}, u32[]{:S(2)}) async-start(bf16[8,24,1024]{2,1,0:T(8,128)(2,1)} %bitcast.15), calls=%async_computation.2 | async-start | bytes 786432 | tf_op jit(solution)/shard_map/all_to_all | solution.py:337
  106.4 8.1 %shard_map.140 = bf16[64,1024]{1,0:T(8,128)(2,1)} custom-call(bf16[512,1152]{1,0:T(8,128)(2,1)} %copy-done.3, bf16[512,1152]{1,0:T(8,128)(2,1)} %collective-permute-done.3.other, bf16[512,1152]{1,0:T(8,128)(2,1)} %copy-done.3, bf16[1024,640]{1,0:T(8,128)(2,1)} %get-tuple-element.15.dproj, f32[1024,1024]{1,0:T(8,128)} %get-tuple-element.16.xhat, ...), custom_call_target="tpu_custom_call" | custom-call | flops 4294967296 | bytes 8388608 | tf_op jit(solution)/shard_map/pallas_call | solution.py:312
  114.6 6.1 %all-to-all-start.3 = ((bf16[32,16,128]{2,1,0:T(8,128)(2,1)}), bf16[32,16,128]{2,1,0:T(8,128)(2,1)S(1)}, u32[]{:S(2)}, u32[]{:S(2)}) async-start(bf16[32,16,128]{2,1,0:T(8,128)(2,1)} %bitcast.76), calls=%async_computation.3 | async-start | bytes 262144 | tf_op jit(solution)/shard_map/all_to_all | solution.py:337
  120.8 0.3 reshape.213
  121.1 0.1 copy.27
  121.2 0.2 reshape.214
  121.4 7.8 %all-to-all-done.3 = bf16[32,16,128]{2,1,0:T(8,128)(2,1)S(1)} async-done(((bf16[32,16,128]{2,1,0:T(8,128)(2,1)}), bf16[32,16,128]{2,1,0:T(8,128)(2,1)S(1)}, u32[]{:S(2)}, u32[]{:S(2)}) %all-to-all-start.3) | async-done | bytes 131104 | tf_op jit(solution)/shard_map/all_to_all | solution.py:337
  129.3 0.7 pad_maximum_fusion.1
  130.0 6.7 %all-to-all-start.4 = ((bf16[16,64,128]{2,1,0:T(8,128)(2,1)}), bf16[16,64,128]{2,1,0:T(8,128)(2,1)S(1)}, u32[]{:S(2)}, u32[]{:S(2)}) async-start(bf16[16,64,128]{2,1,0:T(8,128)(2,1)} %pad_maximum_fusion.1), calls=%async_computation.4 | async-start | bytes 524288 | tf_op jit(solution)/shard_map/all_to_all | solution.py:337
  136.9 12.6 %all-to-all-done.4 = bf16[16,64,128]{2,1,0:T(8,128)(2,1)S(1)} async-done(((bf16[16,64,128]{2,1,0:T(8,128)(2,1)}), bf16[16,64,128]{2,1,0:T(8,128)(2,1)S(1)}, u32[]{:S(2)}, u32[]{:S(2)}) %all-to-all-start.4) | async-done | bytes 262176 | tf_op jit(solution)/shard_map/all_to_all | solution.py:337
  149.5 0.1 bitcast_select_fusion
  149.7 18.1 %all_to_all.30 = bf16[32,28,128]{2,1,0:T(8,128)(2,1)S(1)} all-to-all(bf16[32,28,128]{2,1,0:T(8,128)(2,1)S(1)} %pad_maximum_fusion.2), channel_id=1, replica_groups=mesh['yl'=4,'x'=4,'core'=2,'col'=8,'dp'=2] {'yl','x','core'}, dimensions={0} | all-to-all | bytes 458752 | tf_op jit(solution)/shard_map/all_to_all | solution.py:337
  167.9 0.6 fusion.17
  168.5 0.7 slice_bitcast_fusion
  169.2 0.6 reshape.216
  169.8 0.7 reshape.215
  (58 shorter events, 1.3 us)
Async XLA Ops:
  0.6 67.8 %copy-start = (f32[12,225]{1,0:T(8,128)S(1)}, f32[12,225]{1,0:T(8,128)}, u32[]{:S(2)}) copy-start(f32[12,225]{1,0:T(8,128)} %param.17) | copy-start | bytes 32404
  0.6 3.4 %copy-start.1 = (bf16[1,8,32,1024]{3,2,1,0:T(8,128)(2,1)S(1)}, bf16[1,8,32,1024]{3,2,1,0:T(8,128)(2,1)}, u32[]{:S(2)}) copy-start(bf16[1,8,32,1024]{3,2,1,0:T(8,128)(2,1)} %param.11) | copy-start | bytes 1572868
  0.7 16.8 %slice-start = ((bf16[32,144]{1,0:T(8,128)(2,1)}), bf16[32,16]{1,0:T(8,128)(2,1)S(1)}, s32[]{:S(2)}) async-start(bf16[32,144]{1,0:T(8,128)(2,1)} %param.15), calls=%async_computation.6 | async-start | bytes 16384 | tf_op jit(solution)/shard_map/slice | solution.py:440
  0.7 14.9 %copy-start.7 = (s32[1,2]{1,0:T(1,128)S(1)}, s32[1,2]{1,0:T(1,128)}, u32[]{:S(2)}) copy-start(s32[1,2]{1,0:T(1,128)} %param.19) | copy-start | bytes 28
  0.7 16.8 %copy-start.6 = (bf16[24,64]{1,0:T(8,128)(2,1)S(1)}, bf16[24,64]{1,0:T(8,128)(2,1)}, u32[]{:S(2)}) copy-start(bf16[24,64]{1,0:T(8,128)(2,1)} %param.16) | copy-start | bytes 9220
  4.0 17.9 %slice-start.1 = ((bf16[32,144]{1,0:T(8,128)(2,1)}), bf16[32,128]{1,0:T(8,128)(2,1)S(1)}, s32[]{:S(2)}) async-start(bf16[32,144]{1,0:T(8,128)(2,1)} %param.15), calls=%async_computation.7 | async-start | bytes 16384 | tf_op jit(solution)/shard_map/slice | solution.py:443
  4.0 14.2 %collective-permute-start = (bf16[8,8,1152]{2,1,0:T(8,128)(2,1)S(1)}, bf16[8,8,1152]{2,1,0:T(8,128)(2,1)S(1)}, u32[]{:S(2)}, u32[]{:S(2)}) collective-permute-start(bf16[8,8,1152]{2,1,0:T(8,128)(2,1)S(1)} %pad_maximum_fusion.3), channel_id=1, source_target_pairs={{0,14},{2,0},{4,2},{6,4},{8,6},{10,8},{12,10},{14,12},{1,15},{3,1}... | collective-permute-start | bytes 442376 | tf_op jit(solution)/shard_map/ppermute | solution.py:347
  18.7 17.2 %collective-permute-start.1 = (bf16[7,32,1152]{2,1,0:T(8,128)(2,1)S(1)}, bf16[7,32,1152]{2,1,0:T(8,128)(2,1)S(1)}, u32[]{:S(2)}, u32[]{:S(2)}) collective-permute-start(bf16[7,32,1152]{2,1,0:T(8,128)(2,1)S(1)} %slice.84), channel_id=1, source_target_pairs={{0,496},{16,0},{32,16},{48,32},{64,48},{80,64},{96,80},{112,96},{1... | collective-permute-start | bytes 1548296 | tf_op jit(solution)/shard_map/ppermute | solution.py:347
  23.0 32.9 %all-to-all-start = ((bf16[64,48,128]{2,1,0:T(8,128)(2,1)}), bf16[64,48,128]{2,1,0:T(8,128)(2,1)S(1)}, u32[]{:S(2)}, u32[]{:S(2)}) async-start(bf16[64,48,128]{2,1,0:T(8,128)(2,1)} %broadcast_in_dim.72), calls=%async_computation | async-start | bytes 1572864 | tf_op jit(solution)/shard_map/all_to_all | solution.py:337
  36.2 15.3 %collective-permute-start.2 = (bf16[256,1152]{1,0:T(8,128)(2,1)S(1)}, bf16[256,1152]{1,0:T(8,128)(2,1)S(1)}, u32[]{:S(2)}, u32[]{:S(2)}) collective-permute-start(bf16[256,1152]{1,0:T(8,128)(2,1)S(1)} %bitcast.67), channel_id=1, source_target_pairs={{0,32},{32,0},{64,96},{96,64},{1,33},{33,1},{65,97},{97,65},{2,34}... | collective-permute-start | bytes 1769480 | tf_op jit(solution)/shard_map/ppermute | solution.py:352
  51.6 6.8 %copy-start.3 = (bf16[512,1152]{1,0:T(8,128)(2,1)}, bf16[512,1152]{1,0:T(8,128)(2,1)S(1)}, u32[]{:S(2)}) copy-start(bf16[512,1152]{1,0:T(8,128)(2,1)S(1)} %pad_maximum_fusion.two.own) | copy-start | bytes 3538948
  51.6 21.1 %collective-permute-start.3 = (bf16[512,1152]{1,0:T(8,128)(2,1)S(1)}, bf16[512,1152]{1,0:T(8,128)(2,1)}, u32[]{:S(2)}, u32[]{:S(2)}) collective-permute-start(bf16[512,1152]{1,0:T(8,128)(2,1)S(1)} %pad_maximum_fusion.two.own), channel_id=1, source_target_pairs={{0,16},{16,0},{1,17},{17,1},{2,18},{18,2},{3,19},{19,3},{4,20},{20... | collective-permute-start | bytes 3538952 | tf_op jit(solution)/shard_map/ppermute | solution.py:352
  58.5 9.9 %copy-start.5 = (s32[64,64]{1,0:T(8,128)S(1)}, s32[64,64]{1,0:T(8,128)}, u32[]{:S(2)}) copy-start(s32[64,64]{1,0:T(8,128)} %param.18) | copy-start | bytes 49156
  58.5 28.6 %all-to-all-start.1 = ((bf16[8,128,768]{2,1,0:T(8,128)(2,1)}), bf16[8,128,768]{2,1,0:T(8,128)(2,1)S(1)}, u32[]{:S(2)}, u32[]{:S(2)}) async-start(bf16[8,128,768]{2,1,0:T(8,128)(2,1)} %shard_map.138), calls=%async_computation.1 | async-start | bytes 3145728 | tf_op jit(solution)/shard_map/all_to_all | solution.py:337
  66.5 4.9 %copy-start.4 = (bf16[48,1024]{1,0:T(8,128)(2,1)S(1)}, bf16[48,1024]{1,0:T(8,128)(2,1)}, u32[]{:S(2)}) copy-start(bf16[48,1024]{1,0:T(8,128)(2,1)} %param.12) | copy-start | bytes 294916
  87.1 1.1 copy-start.2
  102.1 12.5 %all-to-all-start.2 = ((bf16[8,24,1024]{2,1,0:T(8,128)(2,1)}), bf16[8,24,1024]{2,1,0:T(8,128)(2,1)S(1)}, u32[]{:S(2)}, u32[]{:S(2)}) async-start(bf16[8,24,1024]{2,1,0:T(8,128)(2,1)} %bitcast.15), calls=%async_computation.2 | async-start | bytes 786432 | tf_op jit(solution)/shard_map/all_to_all | solution.py:337
  114.6 14.7 %all-to-all-start.3 = ((bf16[32,16,128]{2,1,0:T(8,128)(2,1)}), bf16[32,16,128]{2,1,0:T(8,128)(2,1)S(1)}, u32[]{:S(2)}, u32[]{:S(2)}) async-start(bf16[32,16,128]{2,1,0:T(8,128)(2,1)} %bitcast.76), calls=%async_computation.3 | async-start | bytes 262144 | tf_op jit(solution)/shard_map/all_to_all | solution.py:337
  130.0 19.4 %all-to-all-start.4 = ((bf16[16,64,128]{2,1,0:T(8,128)(2,1)}), bf16[16,64,128]{2,1,0:T(8,128)(2,1)S(1)}, u32[]{:S(2)}, u32[]{:S(2)}) async-start(bf16[16,64,128]{2,1,0:T(8,128)(2,1)} %pad_maximum_fusion.1), calls=%async_computation.4 | async-start | bytes 524288 | tf_op jit(solution)/shard_map/all_to_all | solution.py:337

commit v10 on v9

--- a/solution.py
+++ b/solution.py
@@ -85,7 +85,7 @@
     centered = tokens - jnp.mean(tokens, axis=-1, keepdims=True)
     inv = lax.rsqrt(jnp.mean(centered * centered, axis=-1, keepdims=True) + norm_epsilon)
     xhat = centered * inv
-    xhat_out[...] = xhat
+    xhat_out[...] = xhat.astype(xhat_out.dtype)
     inv_out[...] = jnp.broadcast_to(inv, inv_out.shape)
     normed_out[...] = (xhat * gain[...]).astype(jnp.bfloat16)
 
@@ -199,7 +199,7 @@
     bias_sum, gain_sum = bias[...], gains[...]
     for i in range(STEP // chunk):
         rows = slice(i * chunk, (i + 1) * chunk)
-        d, x = dn[rows, :], xhat[rows, :]
+        d, x = dn[rows, :], xhat[rows, :].astype(jnp.float32)
         gain_sum = gain_sum + (d * x).reshape(chunk // 8, 8, width).sum(axis=0)
         g = d * gain[...]
         mean = jnp.mean(g, axis=-1, keepdims=True)
@@ -264,7 +264,7 @@
         [stepped((STEP, width)), stepped((STEP, width)), stepped((STEP, LANES))],
         [
             jax.ShapeDtypeStruct((cells, width), bf16),
-            jax.ShapeDtypeStruct((cells, width), f32),
+            jax.ShapeDtypeStruct((cells, width), bf16),
             jax.ShapeDtypeStruct((cells, LANES), f32),
         ],
         [],
@@ -303,6 +303,7 @@
             pltpu.VMEM((heads, PAIR, PAIR), f32),
         ],
         8 << 30,
+        50,
     )(two, other, normed, arrived, bias, label)
 
 
@@ -450,6 +451,45 @@
     return exchange(sent, CHIP_ROW)
 
 
+def finish_kernel(total, embed, bias, gain, table, out):
+    depth = embed.shape[0] // 8
+    small = 2 * 8
+
+    def tile(at):
+        return total[at // 2, (at % 2) * 8 : (at % 2) * 8 + 8, :].astype(jnp.float32)
+
+    for at in range(8 * depth):
+        row, col = divmod(at, 8)
+        embed[row * 8 : row * 8 + 8, col * LANES : (col + 1) * LANES] = tile(at)
+    columns = table.shape[1] - LANES
+    for col in range(8):
+        values = tile(8 * depth + col)
+        cols = slice(col * LANES, (col + 1) * LANES)
+        bias[:, cols] = values[0:1]
+        gain[:, cols] = values[1:2]
+        for i in range(3):
+            row = 4 * i + col // 2
+            line = values[2 + i : 3 + i]
+            if col % 2 == 0:
+                table[row : row + 1, :LANES] = line
+            else:
+                table[row : row + 1, LANES:] = line[:, :columns]
+    sums = total[:, small:, :].astype(jnp.float32).sum(axis=0)
+    for row in range(out.shape[0] // 2):
+        out[2 * row : 2 * row + 1, :] = sums[row : row + 1, :HEAD]
+        out[2 * row + 1 : 2 * row + 2, :] = sums[row : row + 1, HEAD:]
+
+
+def finish(total, depth, table_shape, out_shape):
+    f32, width = jnp.float32, 8 * LANES
+    shapes = [(depth, width), (1, width), (1, width), table_shape, out_shape]
+    return call(
+        finish_kernel, STEP,
+        [whole(total.shape)], [whole(shape) for shape in shapes],
+        [jax.ShapeDtypeStruct(shape, f32) for shape in shapes], [], 1 << 20, 20,
+    )(total)
+
+
 def on_device(
     pixels,
     cotangent,
@@ -511,7 +551,7 @@
     )
     count = lax.axis_size(CHIP_ROW)
     held = exchange(out_grad.reshape(count, -1, width), CHIP_ROW)
-    my_grad = jnp.dot(table_part, selector, precision=lax.Precision.HIGHEST)
+    my_grad = jnp.dot(table_part, selector, precision=lax.Precision.HIGH)
     wide = 256
     rows = jnp.zeros((16 * width // wide, wide), jnp.float32)
     first_row = 2 * width // wide + group * heads
@@ -538,12 +578,10 @@
     here = jnp.arange(count, dtype=jnp.int32)[None, :, None, None] == lax.axis_index(CHIP_ROW)
     bands = jnp.where(here, bands, jnp.zeros_like(bands)).reshape(chunks, -1, LANES)
     total = exchange(jnp.concatenate([mine, bands], axis=1), ROW)
-    out_weight_grad = total[:, depth_s:].astype(jnp.float32).sum(axis=0).reshape(rows_o, -1)
-    total = total[:, :depth_s]
-    total = total.reshape(tall // 8, width // LANES, 8, LANES).transpose(0, 2, 1, 3)
-    total = total.reshape(tall, width).astype(jnp.float32)
-    table_grad = total[depth + 2 : depth + 5].reshape(all_heads, wide)[:, :table_size]
-    return (out_weight_grad, total[:depth], total[depth], total[depth + 1], table_grad)
+    embed_grad, bias_grad, gain_grad, table_grad, out_weight_grad = finish(
+        total, depth, bias_table.shape, out_weight.shape
+    )
+    return (out_weight_grad, embed_grad, bias_grad[0], gain_grad[0], table_grad)
 
 
 def solution(mesh):

time: 171 us -> 169 us (0.988)
  transfers between devices with their start and end apart: 9 -> 9, of which waited for: 4 -> 5; matrix products, arithmetic and copies ran while one was open for 5% -> 5% of each run, Pallas kernels for 9% -> 8%
where the time goes in v10:
time: 169 us; the launch traced here: 168 us
  starting transfers between devices  58.3 us (34%)
  waiting for transfers between devices  42.8 us (25%)
  Pallas kernels  24.6 us (15%)
  blocking collectives  18.1 us (11%)
  local copies, waits for them, and re-layouts  13.2 us (8%)
  between operations  6.32 us (4%)
  matrix products  2.98 us (2%)
  other arithmetic  2.01 us (1%)
    all_to_all x5, starting transfers between devices, exchange(): return lax.all_to_all(blocks, axis, split_axis=0, concat_axis=0, tiled=True)  36.2 us
    all_to_all x5, waiting for transfers between devices, exchange(): return lax.all_to_all(blocks, axis, split_axis=0, concat_axis=0, tiled=True)  30.7 us
    all_to_all x1, blocking collectives, exchange(): return lax.all_to_all(blocks, axis, split_axis=0, concat_axis=0, tiled=True)  18.1 us
    ppermute x2, starting transfers between devices, from_behind(): lax.ppermute(value, axis, [(source, (source - 1) % count) for source in r...  14.7 us
    ppermute x2, waiting for transfers between devices, swap(): lax.ppermute(value, axis, [(source, source ^ 1) for source in range(count)])  12.2 us
    pallas_call x1, Pallas kernels, run_attention(): call(attention_kernel, cells, [*cell_specs(width), stepped((STEP, width))...  10 us
    pallas_call x1, Pallas kernels, run_norm(): call(norm_kernel, cells, [*cell_specs(LANES, width // LANES), whole((OWN,...  7.59 us
    ppermute x2, starting transfers between devices, swap(): lax.ppermute(value, axis, [(source, source ^ 1) for source in range(count)])  7.36 us
  transfers between devices with their start and end apart: 9, of which 5 were waited for; matrix products, arithmetic and copies ran while one was open for 5% of the time, Pallas kernels for 8%

profile of v10, /device:TPU:1, one launch (start us, length us, event | category | flops | bytes accessed | tf_op | source)
XLA Modules:
  0.0 168.3 jit_solution(2172133781639661638)
XLA Ops:
  0.7 2.5 %reshape_squeeze.3 = bf16[3,8,4,32,4]{4,3,2,1,0:T(8,128)(2,1)S(1)} reshape(bf16[1,3,32,128]{3,2,1,0:T(8,128)(2,1)} %param.10) | data formatting | bytes 49152 | tf_op jit(solution)/shard_map/reshape;squeeze | solution.py:360
  3.2 0.7 copy.22
  3.8 0.1 copy.28
  4.0 11.5 %collective-permute-start = (bf16[8,8,1152]{2,1,0:T(8,128)(2,1)S(1)}, bf16[8,8,1152]{2,1,0:T(8,128)(2,1)S(1)}, u32[]{:S(2)}, u32[]{:S(2)}) collective-permute-start(bf16[8,8,1152]{2,1,0:T(8,128)(2,1)S(1)} %pad_maximum_fusion.3), channel_id=1, source_target_pairs={{0,14},{2,0},{4,2},{6,4},{8,6},{10,8},{12,10},{14,12},{1,15},{3,1}... | collective-permute-start | bytes 442376 | tf_op jit(solution)/shard_map/ppermute | solution.py:348
  15.5 0.6 fusion.19
  18.2 0.4 fusion.5
  18.7 3.2 %collective-permute-start.1 = (bf16[7,32,1152]{2,1,0:T(8,128)(2,1)S(1)}, bf16[7,32,1152]{2,1,0:T(8,128)(2,1)S(1)}, u32[]{:S(2)}, u32[]{:S(2)}) collective-permute-start(bf16[7,32,1152]{2,1,0:T(8,128)(2,1)S(1)} %slice.52), channel_id=1, source_target_pairs={{0,496},{16,0},{32,16},{48,32},{64,48},{80,64},{96,80},{112,96},{1... | collective-permute-start | bytes 1548296 | tf_op jit(solution)/shard_map/ppermute | solution.py:348
  22.0 1.0 broadcast_in_dim.72
  23.0 11.0 %all-to-all-start = ((bf16[64,48,128]{2,1,0:T(8,128)(2,1)}), bf16[64,48,128]{2,1,0:T(8,128)(2,1)S(1)}, u32[]{:S(2)}, u32[]{:S(2)}) async-start(bf16[64,48,128]{2,1,0:T(8,128)(2,1)} %broadcast_in_dim.72), calls=%async_computation | async-start | bytes 1572864 | tf_op jit(solution)/shard_map/all_to_all | solution.py:338
  35.9 0.2 fusion.7
  36.3 3.1 %collective-permute-start.2 = (bf16[256,1152]{1,0:T(8,128)(2,1)S(1)}, bf16[256,1152]{1,0:T(8,128)(2,1)S(1)}, u32[]{:S(2)}, u32[]{:S(2)}) collective-permute-start(bf16[256,1152]{1,0:T(8,128)(2,1)S(1)} %bitcast.57), channel_id=1, source_target_pairs={{0,32},{32,0},{64,96},{96,64},{1,33},{33,1},{65,97},{97,65},{2,34}... | collective-permute-start | bytes 1769480 | tf_op jit(solution)/shard_map/ppermute | solution.py:353
  39.4 12.2 %collective-permute-done.2 = bf16[256,1152]{1,0:T(8,128)(2,1)S(1)} collective-permute-done((bf16[256,1152]{1,0:T(8,128)(2,1)S(1)}, bf16[256,1152]{1,0:T(8,128)(2,1)S(1)}, u32[]{:S(2)}, u32[]{:S(2)}) %collective-permute-start.2) | collective-permute-done | bytes 589856 | tf_op jit(solution)/shard_map/ppermute | solution.py:353
  51.6 0.1 pad_maximum_fusion.two.own
  51.7 4.2 %collective-permute-start.3 = (bf16[512,1152]{1,0:T(8,128)(2,1)S(1)}, bf16[512,1152]{1,0:T(8,128)(2,1)S(1)}, u32[]{:S(2)}, u32[]{:S(2)}) collective-permute-start(bf16[512,1152]{1,0:T(8,128)(2,1)S(1)} %pad_maximum_fusion.two.own), channel_id=1, source_target_pairs={{0,16},{16,0},{1,17},{17,1},{2,18},{18,2},{3,19},{19,3},{4,20},{20... | collective-permute-start | bytes 3538952 | tf_op jit(solution)/shard_map/ppermute | solution.py:353
  56.0 1.2 reshape.193
  57.1 1.3 copy.25
  58.5 0.2 reshape.194
  58.6 0.1 copy.26.rest
  58.7 1.6 shard_map.138
  60.3 8.4 %all-to-all-start.1 = ((bf16[8,128,768]{2,1,0:T(8,128)(2,1)}), bf16[8,128,768]{2,1,0:T(8,128)(2,1)}, u32[]{:S(2)}, u32[]{:S(2)}) async-start(bf16[8,128,768]{2,1,0:T(8,128)(2,1)} %shard_map.138), calls=%async_computation.1 | async-start | bytes 3145728 | tf_op jit(solution)/shard_map/all_to_all | solution.py:338
  70.3 0.1 concatenate.47
  70.4 0.1 concatenate.48
  70.5 0.1 concatenate.49
  70.7 2.2 %fusion.1 = f32[3,4096]{1,0:T(4,128)S(1)} fusion(s32[4096]{0:T(1024)S(1)} %eq.28, f32[12,225]{1,0:T(8,128)S(1)} %copy-done, s32[]{:T(128)S(6)} %select_n.33), kind=kOutput, calls=%fused_computation.2 | convolution fusion | flops 34099200 | bytes 69636 | tf_op jit(solution)/shard_map/dot_general | solution.py:543
  72.8 0.1 reshape.195.bias
  73.0 0.7 pad.9.embed_w
  73.7 1.0 copy-done.3
  74.8 4.6 %shard_map.137 = (bf16[1024,1024]{1,0:T(8,128)(2,1)}, bf16[1024,1024]{1,0:T(8,128)(2,1)}, f32[1024,128]{1,0:T(8,128)}) custom-call(bf16[512,1152]{1,0:T(8,128)(2,1)} %copy-done.1, bf16[512,1152]{1,0:T(8,128)(2,1)} %copy-done.3, bf16[128,1024]{1,0:T(8,128)(2,1)} %pad.9.embed_w, f32[1,1024]{1,0:T(1,128)} %bitcast.66, f32[1,1024]{1,0:T(1,128)} %bitcast.67), custom_call_target="tpu_custom_call" | custom-call | flops 2147483648 | bytes 8388608 | tf_op jit(solution)/shard_map/pallas_call | solution.py:258
  79.4 10.1 %all-to-all-done.1.arrived = bf16[8,128,768]{2,1,0:T(8,128)(2,1)} async-done(((bf16[8,128,768]{2,1,0:T(8,128)(2,1)}), bf16[8,128,768]{2,1,0:T(8,128)(2,1)}, u32[]{:S(2)}, u32[]{:S(2)}) %all-to-all-start.1) | async-done | bytes 1572896 | tf_op jit(solution)/shard_map/all_to_all | solution.py:338
  89.5 1.3 copy-done.4
  90.7 10.0 %shard_map.139 = (bf16[1024,640]{1,0:T(8,128)(2,1)}, f32[3,4096]{1,0:T(4,128)S(1)}, bf16[192,1024]{1,0:T(8,128)(2,1)}, bf16[1024,640]{1,0:T(8,128)(2,1)}) custom-call(bf16[512,1152]{1,0:T(8,128)(2,1)S(1)} %copy-done.2, bf16[512,1152]{1,0:T(8,128)(2,1)S(1)} %copy-done.4, bf16[1024,1024]{1,0:T(8,128)(2,1)} %get-tuple-element.19.normed, ...), custom_call_target="tpu_custom_call" | custom-call | flops 8589934592 | bytes 8388608 | tf_op jit(solution)/shard_map/pallas_call | solution.py:281
  100.8 0.8 fusion
  101.6 0.4 dynamic_update_slice.3
  102.0 0.6 reshape.196.table
  102.7 4.5 %all-to-all-start.2 = ((bf16[8,24,1024]{2,1,0:T(8,128)(2,1)}), bf16[8,24,1024]{2,1,0:T(8,128)(2,1)S(1)}, u32[]{:S(2)}, u32[]{:S(2)}) async-start(bf16[8,24,1024]{2,1,0:T(8,128)(2,1)} %bitcast.15), calls=%async_computation.2 | async-start | bytes 786432 | tf_op jit(solution)/shard_map/all_to_all | solution.py:338
  107.2 7.6 %shard_map.140 = bf16[64,1024]{1,0:T(8,128)(2,1)} custom-call(bf16[512,1152]{1,0:T(8,128)(2,1)} %copy-done.1, bf16[512,1152]{1,0:T(8,128)(2,1)} %copy-done.3, bf16[512,1152]{1,0:T(8,128)(2,1)} %copy-done.1, bf16[1024,640]{1,0:T(8,128)(2,1)} %get-tuple-element.20.dproj, bf16[1024,1024]{1,0:T(8,128)(2,1)} %get-tuple-element.21.xhat, ...), custom_call_target="tpu_custom_call" | custom-call | flops 4294967296 | bytes 8388608 | tf_op jit(solution)/shard_map/pallas_call | solution.py:313
  114.7 0.1 all-to-all-done.2
  114.9 5.8 %all-to-all-start.3 = ((bf16[32,16,128]{2,1,0:T(8,128)(2,1)}), bf16[32,16,128]{2,1,0:T(8,128)(2,1)S(1)}, u32[]{:S(2)}, u32[]{:S(2)}) async-start(bf16[32,16,128]{2,1,0:T(8,128)(2,1)} %bitcast.65), calls=%async_computation.3 | async-start | bytes 262144 | tf_op jit(solution)/shard_map/all_to_all | solution.py:338
  120.7 0.3 reshape.201
  121.0 0.1 copy.27
  121.1 0.2 reshape.202
  121.3 7.8 %all-to-all-done.3 = bf16[32,16,128]{2,1,0:T(8,128)(2,1)S(1)} async-done(((bf16[32,16,128]{2,1,0:T(8,128)(2,1)}), bf16[32,16,128]{2,1,0:T(8,128)(2,1)S(1)}, u32[]{:S(2)}, u32[]{:S(2)}) %all-to-all-start.3) | async-done | bytes 131104 | tf_op jit(solution)/shard_map/all_to_all | solution.py:338
  129.2 0.7 pad_maximum_fusion.1
  130.0 6.6 %all-to-all-start.4 = ((bf16[16,64,128]{2,1,0:T(8,128)(2,1)}), bf16[16,64,128]{2,1,0:T(8,128)(2,1)S(1)}, u32[]{:S(2)}, u32[]{:S(2)}) async-start(bf16[16,64,128]{2,1,0:T(8,128)(2,1)} %pad_maximum_fusion.1), calls=%async_computation.4 | async-start | bytes 524288 | tf_op jit(solution)/shard_map/all_to_all | solution.py:338
  136.7 12.6 %all-to-all-done.4 = bf16[16,64,128]{2,1,0:T(8,128)(2,1)S(1)} async-done(((bf16[16,64,128]{2,1,0:T(8,128)(2,1)}), bf16[16,64,128]{2,1,0:T(8,128)(2,1)S(1)}, u32[]{:S(2)}, u32[]{:S(2)}) %all-to-all-start.4) | async-done | bytes 262176 | tf_op jit(solution)/shard_map/all_to_all | solution.py:338
  149.3 0.1 bitcast_select_fusion
  149.5 18.1 %all_to_all.30.total = bf16[32,28,128]{2,1,0:T(8,128)(2,1)S(1)} all-to-all(bf16[32,28,128]{2,1,0:T(8,128)(2,1)S(1)} %pad_maximum_fusion.2), channel_id=1, replica_groups=mesh['yl'=4,'x'=4,'core'=2,'col'=8,'dp'=2] {'yl','x','core'}, dimensions={0} | all-to-all | bytes 458752 | tf_op jit(solution)/shard_map/all_to_all | solution.py:338
  167.6 0.7 shard_map.141
  (55 shorter events, 1.0 us)
Async XLA Ops:
  0.6 70.0 %copy-start = (f32[12,225]{1,0:T(8,128)S(1)}, f32[12,225]{1,0:T(8,128)}, u32[]{:S(2)}) copy-start(f32[12,225]{1,0:T(8,128)} %param.17) | copy-start | bytes 32404
  0.6 3.4 %copy-start.5 = (bf16[1,8,32,1024]{3,2,1,0:T(8,128)(2,1)S(1)}, bf16[1,8,32,1024]{3,2,1,0:T(8,128)(2,1)}, u32[]{:S(2)}) copy-start(bf16[1,8,32,1024]{3,2,1,0:T(8,128)(2,1)} %param.11) | copy-start | bytes 1572868
  0.7 16.8 %slice-start = ((bf16[32,144]{1,0:T(8,128)(2,1)}), bf16[32,16]{1,0:T(8,128)(2,1)S(1)}, s32[]{:S(2)}) async-start(bf16[32,144]{1,0:T(8,128)(2,1)} %param.15), calls=%async_computation.6 | async-start | bytes 16384 | tf_op jit(solution)/shard_map/slice | solution.py:441
  0.7 14.9 %copy-start.9 = (s32[1,2]{1,0:T(1,128)S(1)}, s32[1,2]{1,0:T(1,128)}, u32[]{:S(2)}) copy-start(s32[1,2]{1,0:T(1,128)} %param.19) | copy-start | bytes 28
  0.7 16.8 %copy-start.8 = (bf16[24,64]{1,0:T(8,128)(2,1)S(1)}, bf16[24,64]{1,0:T(8,128)(2,1)}, u32[]{:S(2)}) copy-start(bf16[24,64]{1,0:T(8,128)(2,1)} %param.16) | copy-start | bytes 9220
  4.0 17.9 %slice-start.1 = ((bf16[32,144]{1,0:T(8,128)(2,1)}), bf16[32,128]{1,0:T(8,128)(2,1)S(1)}, s32[]{:S(2)}) async-start(bf16[32,144]{1,0:T(8,128)(2,1)} %param.15), calls=%async_computation.7 | async-start | bytes 16384 | tf_op jit(solution)/shard_map/slice | solution.py:444
  4.0 14.2 %collective-permute-start = (bf16[8,8,1152]{2,1,0:T(8,128)(2,1)S(1)}, bf16[8,8,1152]{2,1,0:T(8,128)(2,1)S(1)}, u32[]{:S(2)}, u32[]{:S(2)}) collective-permute-start(bf16[8,8,1152]{2,1,0:T(8,128)(2,1)S(1)} %pad_maximum_fusion.3), channel_id=1, source_target_pairs={{0,14},{2,0},{4,2},{6,4},{8,6},{10,8},{12,10},{14,12},{1,15},{3,1}... | collective-permute-start | bytes 442376 | tf_op jit(solution)/shard_map/ppermute | solution.py:348
  18.7 17.3 %collective-permute-start.1 = (bf16[7,32,1152]{2,1,0:T(8,128)(2,1)S(1)}, bf16[7,32,1152]{2,1,0:T(8,128)(2,1)S(1)}, u32[]{:S(2)}, u32[]{:S(2)}) collective-permute-start(bf16[7,32,1152]{2,1,0:T(8,128)(2,1)S(1)} %slice.52), channel_id=1, source_target_pairs={{0,496},{16,0},{32,16},{48,32},{64,48},{80,64},{96,80},{112,96},{1... | collective-permute-start | bytes 1548296 | tf_op jit(solution)/shard_map/ppermute | solution.py:348
  23.0 32.9 %all-to-all-start = ((bf16[64,48,128]{2,1,0:T(8,128)(2,1)}), bf16[64,48,128]{2,1,0:T(8,128)(2,1)S(1)}, u32[]{:S(2)}, u32[]{:S(2)}) async-start(bf16[64,48,128]{2,1,0:T(8,128)(2,1)} %broadcast_in_dim.72), calls=%async_computation | async-start | bytes 1572864 | tf_op jit(solution)/shard_map/all_to_all | solution.py:338
  36.3 15.3 %collective-permute-start.2 = (bf16[256,1152]{1,0:T(8,128)(2,1)S(1)}, bf16[256,1152]{1,0:T(8,128)(2,1)S(1)}, u32[]{:S(2)}, u32[]{:S(2)}) collective-permute-start(bf16[256,1152]{1,0:T(8,128)(2,1)S(1)} %bitcast.57), channel_id=1, source_target_pairs={{0,32},{32,0},{64,96},{96,64},{1,33},{33,1},{65,97},{97,65},{2,34}... | collective-permute-start | bytes 1769480 | tf_op jit(solution)/shard_map/ppermute | solution.py:353
  51.7 8.7 %copy-start.1 = (bf16[512,1152]{1,0:T(8,128)(2,1)}, bf16[512,1152]{1,0:T(8,128)(2,1)S(1)}, u32[]{:S(2)}) copy-start(bf16[512,1152]{1,0:T(8,128)(2,1)S(1)} %pad_maximum_fusion.two.own) | copy-start | bytes 3538948
  51.7 22.1 %collective-permute-start.3 = (bf16[512,1152]{1,0:T(8,128)(2,1)S(1)}, bf16[512,1152]{1,0:T(8,128)(2,1)S(1)}, u32[]{:S(2)}, u32[]{:S(2)}) collective-permute-start(bf16[512,1152]{1,0:T(8,128)(2,1)S(1)} %pad_maximum_fusion.two.own), channel_id=1, source_target_pairs={{0,16},{16,0},{1,17},{17,1},{2,18},{18,2},{3,19},{19,3},{4,20},{20... | collective-permute-start | bytes 3538952 | tf_op jit(solution)/shard_map/ppermute | solution.py:353
  60.3 10.2 %copy-start.7 = (s32[64,64]{1,0:T(8,128)S(1)}, s32[64,64]{1,0:T(8,128)}, u32[]{:S(2)}) copy-start(s32[64,64]{1,0:T(8,128)} %param.18) | copy-start | bytes 49156
  60.3 29.1 %all-to-all-start.1 = ((bf16[8,128,768]{2,1,0:T(8,128)(2,1)}), bf16[8,128,768]{2,1,0:T(8,128)(2,1)}, u32[]{:S(2)}, u32[]{:S(2)}) async-start(bf16[8,128,768]{2,1,0:T(8,128)(2,1)} %shard_map.138), calls=%async_computation.1 | async-start | bytes 3145728 | tf_op jit(solution)/shard_map/all_to_all | solution.py:338
  68.7 4.2 %copy-start.6 = (bf16[48,1024]{1,0:T(8,128)(2,1)S(1)}, bf16[48,1024]{1,0:T(8,128)(2,1)}, u32[]{:S(2)}) copy-start(bf16[48,1024]{1,0:T(8,128)(2,1)} %param.12) | copy-start | bytes 294916
  73.7 1.0 copy-start.3
  74.8 14.7 %copy-start.2 = (bf16[512,1152]{1,0:T(8,128)(2,1)S(1)}, bf16[512,1152]{1,0:T(8,128)(2,1)}, u32[]{:S(2)}) copy-start(bf16[512,1152]{1,0:T(8,128)(2,1)} %copy-done.1) | copy-start | bytes 3538948
  89.5 1.3 copy-start.4
  102.7 12.2 %all-to-all-start.2 = ((bf16[8,24,1024]{2,1,0:T(8,128)(2,1)}), bf16[8,24,1024]{2,1,0:T(8,128)(2,1)S(1)}, u32[]{:S(2)}, u32[]{:S(2)}) async-start(bf16[8,24,1024]{2,1,0:T(8,128)(2,1)} %bitcast.15), calls=%async_computation.2 | async-start | bytes 786432 | tf_op jit(solution)/shard_map/all_to_all | solution.py:338
  114.9 14.3 %all-to-all-start.3 = ((bf16[32,16,128]{2,1,0:T(8,128)(2,1)}), bf16[32,16,128]{2,1,0:T(8,128)(2,1)S(1)}, u32[]{:S(2)}, u32[]{:S(2)}) async-start(bf16[32,16,128]{2,1,0:T(8,128)(2,1)} %bitcast.65), calls=%async_computation.3 | async-start | bytes 262144 | tf_op jit(solution)/shard_map/all_to_all | solution.py:338
  130.0 19.3 %all-to-all-start.4 = ((bf16[16,64,128]{2,1,0:T(8,128)(2,1)}), bf16[16,64,128]{2,1,0:T(8,128)(2,1)S(1)}, u32[]{:S(2)}, u32[]{:S(2)}) async-start(bf16[16,64,128]{2,1,0:T(8,128)(2,1)} %pad_maximum_fusion.1), calls=%async_computation.4 | async-start | bytes 524288 | tf_op jit(solution)/shard_map/all_to_all | solution.py:338
